TPU v7x, 256 devices: a whole 4x4x8 slice. The times are simulated.
256 devices in a mesh: gx: 8 (over x, z_lo), gy: 8 (over z_hi, core), gz: 4 (over y).
Axes of the slice: x: 4, y: 4, z: 8 (z_hi: 4, z_lo: 2; z = z_hi * 2 + z_lo), core: 2. Of those that a mesh axis runs over, the one named last changes fastest.
Arguments:
- partials: float32 [32, 128, 128, 512], P('gx', None, 'gy', 'gz'), may hold values from -40 to 40
- code_bits: int32 [32, 128], replicated, may hold values from 0 to 1
- group_map: int32 [32], replicated, may hold values from 0 to 31, each once
- velocity: float32 [128, 128, 512], P('gx', 'gy', 'gz'), may hold values from 1.5 to 4.5
Outputs:
- gradient: float32 [128, 128, 512], P('gx', 'gy', 'gz')
- new_model: float32 [128, 128, 512], P('gx', 'gy', 'gz')
Inputs may be any that keep to these rules, and one draw needn't show every extreme that they name: `group_map`: every group of 0 to 31 stands in exactly one slot.
All inputs are finite; a program needn't handle non-finite values.
Results may differ from a plain program's by a relative error of at most 0.0001.
Values sent between devices are 32-bit elements; how exact they have to be, the bound alone decides.
No kernel may reach another device: no remote copies, remote signals or barrier semaphores. Data moves between devices by JAX's collectives and lax.ppermute only.
A program may use at most 64 MiB of HBM per device.

v0:
```python
import functools

import jax
import jax.numpy as jnp
from jax import lax
from jax.sharding import Mesh
from jax.sharding import PartitionSpec as P

ITERS = 3
GX = ("gx_0", "gx_1")
GY = ("gy_0", "gy_1")
GX_GY_GZ = ("gx_0", "gx_1", "gy_0", "gy_1", "gz")


step_length = 0.5
tv_weight = 0.2
dual_step = 0.28
primal_step = 0.28


def from_behind(block, axis, distance):
    devices = range(lax.axis_size(axis))
    route = [(i - distance, i) for i in devices if i - distance in devices]
    return lax.ppermute(block, axis, route)


def over_axes(shard, axes):
    return functools.reduce(lax.psum, axes, shard)


def edge_mask(position, count, length, shape):
    global_index = position * length + jnp.arange(length, dtype=jnp.int32)
    keep = (global_index < count * length - 1).astype(jnp.float32)
    return keep.reshape(shape)


def neighbours_after(extra):
    next_x = jnp.concatenate([extra[1:], from_behind(extra[:1], GX, -1)], 0)
    next_y = jnp.concatenate([extra[:, 1:], from_behind(extra[:, :1], GY, -1)], 1)
    next_z = jnp.concatenate([extra[:, :, 1:], from_behind(extra[:, :, :1], "gz", -1)], 2)
    return (next_x, next_y, next_z)


def neighbours_before(dual_field):
    before_x = jnp.concatenate([from_behind(dual_field[0, -1:], GX, 1), dual_field[0, :-1]], 0)
    before_y = jnp.concatenate(
        [from_behind(dual_field[1, :, -1:], GY, 1), dual_field[1, :, :-1]], 1
    )
    before_z = jnp.concatenate(
        [from_behind(dual_field[2, :, :, -1:], "gz", 1), dual_field[2, :, :, :-1]], 2
    )
    return (before_x, before_y, before_z)


def shards(partials, code_bits, group_map, velocity):
    groups = group_map.shape[0]
    block_x, block_y, block_z = velocity.shape
    onehot = (group_map[:, None] == jnp.arange(groups, dtype=jnp.int32)[None, :]).astype(
        jnp.float32
    )
    slot_bits = jnp.dot(onehot, code_bits.astype(jnp.float32), precision=lax.Precision.HIGHEST)
    sign_table = 2.0 * slot_bits - 1.0
    local_signs = lax.dynamic_slice_in_dim(sign_table, lax.axis_index(GX) * block_x, block_x, 1)
    gradient = jnp.einsum(
        "gx,gxyz->xyz",
        local_signs,
        lax.all_to_all(partials, GX, split_axis=1, concat_axis=0, tiled=True),
        precision=lax.Precision.HIGHEST,
    )
    square_sum = over_axes(jnp.sum(gradient * gradient), GX_GY_GZ)
    cell_count = (
        block_x * block_y * block_z * lax.axis_size(GX) * lax.axis_size(GY) * lax.axis_size("gz")
    )
    step_scale = step_length / jnp.sqrt(square_sum / cell_count + 1.0)
    target = velocity - step_scale * gradient
    mask_x = edge_mask(lax.axis_index(GX), lax.axis_size(GX), block_x, (block_x, 1, 1))
    mask_y = edge_mask(lax.axis_index(GY), lax.axis_size(GY), block_y, (1, block_y, 1))
    mask_z = edge_mask(lax.axis_index("gz"), lax.axis_size("gz"), block_z, (1, 1, block_z))
    current = target
    extra = target
    dual_field = jnp.zeros((3,) + target.shape, jnp.float32)
    for iteration in range(ITERS):
        next_x, next_y, next_z = neighbours_after(extra)
        differences = jnp.stack(
            [(next_x - extra) * mask_x, (next_y - extra) * mask_y, (next_z - extra) * mask_z]
        )
        dual_field = dual_field + dual_step * differences
        magnitude = jnp.sqrt(jnp.sum(dual_field * dual_field, axis=0))
        dual_field = dual_field / jnp.maximum(1.0, magnitude / tv_weight)[None]
        before_x, before_y, before_z = neighbours_before(dual_field)
        spread = dual_field[0] - before_x + (dual_field[1] - before_y) + (dual_field[2] - before_z)
        updated = (current + primal_step * spread + primal_step * target) / (1.0 + primal_step)
        extra = 2.0 * updated - current
        current = updated
    return (gradient, current)


def solution(mesh):
    torus = Mesh(
        mesh.devices.reshape(4, 2, 4, 2, mesh.shape["gz"]), ("gx_0", "gx_1", "gy_0", "gy_1", "gz")
    )
    placed = (P(GX, None, GY, "gz"), P(), P(), P(GX, GY, "gz"))
    return jax.shard_map(
        shards,
        mesh=torus,
        in_specs=placed,
        out_specs=(P(GX, GY, "gz"), P(GX, GY, "gz")),
        check_vma=False,
    )
```

profile of v0, /device:TPU:1, one launch (start us, length us, event | category | flops | bytes accessed | tf_op | source)
XLA Modules:
  0.0 183.8 jit_solution(953719524343635851)
XLA Ops:
  0.6 4.8 %copy.34 = f32[4,128,16,128]{3,2,0,1:T(8,128)} copy(f32[4,128,16,128]{3,2,1,0:T(8,128)} %param.4) | data formatting | bytes 8388608 | tf_op args[0]
  5.4 6.3 %all-to-all-start = ((f32[4,128,16,128]{3,2,0,1:T(8,128)}), f32[4,128,16,128]{3,2,0,1:T(8,128)}, u32[]{:S(2)}, u32[]{:S(2)}) async-start(f32[4,128,16,128]{3,2,0,1:T(8,128)} %copy.34), calls=%async_computation | async-start | bytes 8388608 | tf_op jit(solution)/shard_map/all_to_all | solution.py:67
  12.1 47.9 %all-to-all-done = f32[4,128,16,128]{3,2,0,1:T(8,128)} async-done(((f32[4,128,16,128]{3,2,0,1:T(8,128)}), f32[4,128,16,128]{3,2,0,1:T(8,128)}, u32[]{:S(2)}, u32[]{:S(2)}) %all-to-all-start) | async-done | bytes 4194336 | tf_op jit(solution)/shard_map/all_to_all | solution.py:67
  59.9 2.8 %copy.36 = f32[8,4,16,16,128]{4,3,2,1,0:T(8,128)S(1)} copy(f32[8,4,16,16,128]{4,3,1,2,0:T(8,128)} %bitcast.4) | data formatting | bytes 8388608 | tf_op jit(solution)/shard_map/all_to_all | solution.py:67
  62.7 4.3 %fusion = f32[16,1,16,128]{3,1,2,0:T(1,128)S(1)} fusion(f32[32,16,1,1]{0,2,3,1:T(1,128)S(1)} %bitcast.169, f32[32,16,16,128]{3,2,1,0:T(8,128)S(1)} %bitcast.164), kind=kOutput, calls=%fused_computation | convolution fusion | flops 12582912 | bytes 4327424 | tf_op jit(solution)/shard_map/gx,gxyz->xyz/dot_general | solution.py:64
  67.7 7.8 %psum.35 = f32[]{:T(128)} all-reduce(f32[]{:T(128)} %fusion.48), channel_id=1, replica_groups=mesh['gx_0'=4,'gx_1'=2,'gy_0'=4,'gy_1'=2,'gz'=4] {'gx_0'}, use_global_device_ids=true, to_apply=%region_1.0 | all-reduce | flops 1 | bytes 8 | tf_op jit(solution)/shard_map/psum | solution.py:28
  75.5 5.0 %psum.36 = f32[]{:T(128)} all-reduce(f32[]{:T(128)} %psum.35), channel_id=1, replica_groups=mesh['gx_0'=4,'gx_1'=2,'gy_0'=4,'gy_1'=2,'gz'=4] {'gx_1'}, use_global_device_ids=true, to_apply=%region_2.0 | all-reduce | flops 1 | bytes 8 | tf_op jit(solution)/shard_map/psum | solution.py:28
  80.5 12.6 %psum.37 = f32[]{:T(128)} all-reduce(f32[]{:T(128)} %psum.36), channel_id=1, replica_groups=mesh['gx_0'=4,'gx_1'=2,'gy_0'=4,'gy_1'=2,'gz'=4] {'gy_0'}, use_global_device_ids=true, to_apply=%region_3.0 | all-reduce | flops 1 | bytes 8 | tf_op jit(solution)/shard_map/psum | solution.py:28
  93.1 9.7 %psum.38 = f32[]{:T(128)} all-reduce(f32[]{:T(128)} %psum.37), channel_id=1, replica_groups=mesh['gx_0'=4,'gx_1'=2,'gy_0'=4,'gy_1'=2,'gz'=4] {'gy_1'}, use_global_device_ids=true, to_apply=%region_4.0 | all-reduce | flops 1 | bytes 8 | tf_op jit(solution)/shard_map/psum | solution.py:28
  102.8 9.3 %psum.39 = f32[]{:T(128)} all-reduce(f32[]{:T(128)} %psum.38), channel_id=1, replica_groups=mesh['gx_0'=4,'gx_1'=2,'gy_0'=4,'gy_1'=2,'gz'=4] {'gz'}, use_global_device_ids=true, to_apply=%region_5.0 | all-reduce | flops 1 | bytes 8 | tf_op jit(solution)/shard_map/psum | solution.py:28
  112.9 1.3 collective-permute-start.2
  114.2 1.3 collective-permute-start
  115.5 4.3 %collective-permute-start.1 = (f32[16,1,128]{2,0,1:T(8,128)S(1)}, f32[16,1,128]{2,0,1:T(8,128)S(1)}, u32[]{:S(2)}, u32[]{:S(2)}) collective-permute-start(f32[16,1,128]{2,0,1:T(8,128)S(1)} %slice.183), channel_id=1, source_target_pairs={{4,0},{8,4},{12,8},{16,12},{20,16},{24,20},{28,24},{5,1},{9,5},{13... | collective-permute-start | bytes 24584 | tf_op jit(solution)/shard_map/ppermute | solution.py:24
  120.0 1.4 collective-permute-done.1
  122.2 4.0 %collective-permute-start.5 = (f32[16,16,1]{2,0,1:T(8,128)S(1)}, f32[16,16,1]{2,0,1:T(8,128)S(1)}, u32[]{:S(2)}, u32[]{:S(2)}) collective-permute-start(f32[16,16,1]{2,0,1:T(8,128)S(1)} %copy.40), channel_id=1, source_target_pairs={{0,1},{1,2},{2,3},{4,5},{5,6},{6,7},{8,9},{9,10},{10,11},{12,13},{... | collective-permute-start | bytes 3080 | tf_op jit(solution)/shard_map/ppermute | solution.py:24
  126.2 4.1 %collective-permute-start.3 = (f32[1,16,128]{2,0,1:T(1,128)S(1)}, f32[1,16,128]{2,0,1:T(1,128)S(1)}, u32[]{:S(2)}, u32[]{:S(2)}) collective-permute-start(f32[1,16,128]{2,0,1:T(1,128)S(1)} %slice_bitcast_fusion.23), channel_id=1, source_target_pairs={{0,32},{32,64},{64,96},{96,128},{128,160},{160,192},{192,224},{1,3... | collective-permute-start | bytes 24584 | tf_op jit(solution)/shard_map/ppermute | solution.py:24
  130.4 2.5 %collective-permute-start.4 = (f32[16,1,128]{2,0,1:T(8,128)S(1)}, f32[16,1,128]{2,0,1:T(8,128)S(1)}, u32[]{:S(2)}, u32[]{:S(2)}) collective-permute-start(f32[16,1,128]{2,0,1:T(8,128)S(1)} %slice_bitcast_fusion.22), channel_id=1, source_target_pairs={{0,4},{4,8},{8,12},{12,16},{16,20},{20,24},{24,28},{1,5},{5,9},{9,... | collective-permute-start | bytes 24584 | tf_op jit(solution)/shard_map/ppermute | solution.py:24
  133.8 1.3 collective-permute-start.6
  135.1 1.9 %collective-permute-start.7 = (f32[16,1,128]{2,0,1:T(8,128)S(1)}, f32[16,1,128]{2,0,1:T(8,128)S(1)}, u32[]{:S(2)}, u32[]{:S(2)}) collective-permute-start(f32[16,1,128]{2,0,1:T(8,128)S(1)} %slice.198), channel_id=1, source_target_pairs={{4,0},{8,4},{12,8},{16,12},{20,16},{24,20},{28,24},{5,1},{9,5},{13... | collective-permute-start | bytes 24584 | tf_op jit(solution)/shard_map/ppermute | solution.py:24
  137.0 1.3 collective-permute-start.8
  138.4 5.6 %collective-permute-done.8 = f32[16,16,1]{2,0,1:T(8,128)S(1)} collective-permute-done((f32[16,16,1]{2,0,1:T(8,128)S(1)}, f32[16,16,1]{2,0,1:T(8,128)S(1)}, u32[]{:S(2)}, u32[]{:S(2)}) %collective-permute-start.8) | collective-permute-done | bytes 1056 | tf_op jit(solution)/shard_map/ppermute | solution.py:24
  144.9 2.0 %collective-permute-start.11 = (f32[16,16,1]{2,0,1:T(8,128)S(1)}, f32[16,16,1]{2,0,1:T(8,128)S(1)}, u32[]{:S(2)}, u32[]{:S(2)}) collective-permute-start(f32[16,16,1]{2,0,1:T(8,128)S(1)} %copy.43), channel_id=1, source_target_pairs={{0,1},{1,2},{2,3},{4,5},{5,6},{6,7},{8,9},{9,10},{10,11},{12,13},{... | collective-permute-start | bytes 3080 | tf_op jit(solution)/shard_map/ppermute | solution.py:24
  146.9 5.9 %collective-permute-start.10 = (f32[16,1,128]{2,0,1:T(8,128)S(1)}, f32[16,1,128]{2,0,1:T(8,128)S(1)}, u32[]{:S(2)}, u32[]{:S(2)}) collective-permute-start(f32[16,1,128]{2,0,1:T(8,128)S(1)} %slice_bitcast_fusion.20), channel_id=1, source_target_pairs={{0,4},{4,8},{8,12},{12,16},{16,20},{20,24},{24,28},{1,5},{5,9},{9,... | collective-permute-start | bytes 24584 | tf_op jit(solution)/shard_map/ppermute | solution.py:24
  152.8 4.3 %collective-permute-start.9 = (f32[1,16,128]{2,0,1:T(1,128)S(1)}, f32[1,16,128]{2,0,1:T(1,128)S(1)}, u32[]{:S(2)}, u32[]{:S(2)}) collective-permute-start(f32[1,16,128]{2,0,1:T(1,128)S(1)} %slice_bitcast_fusion.21), channel_id=1, source_target_pairs={{0,32},{32,64},{64,96},{96,128},{128,160},{160,192},{192,224},{1,3... | collective-permute-start | bytes 24584 | tf_op jit(solution)/shard_map/ppermute | solution.py:24
  157.1 0.7 collective-permute-done.9
  158.0 1.3 collective-permute-start.12
  159.3 1.9 %collective-permute-start.13 = (f32[16,1,128]{2,0,1:T(8,128)S(1)}, f32[16,1,128]{2,0,1:T(8,128)S(1)}, u32[]{:S(2)}, u32[]{:S(2)}) collective-permute-start(f32[16,1,128]{2,0,1:T(8,128)S(1)} %slice.213), channel_id=1, source_target_pairs={{4,0},{8,4},{12,8},{16,12},{20,16},{24,20},{28,24},{5,1},{9,5},{13... | collective-permute-start | bytes 24584 | tf_op jit(solution)/shard_map/ppermute | solution.py:24
  161.2 1.3 collective-permute-start.14
  162.7 4.3 %collective-permute-done.14 = f32[16,16,1]{2,0,1:T(8,128)S(1)} collective-permute-done((f32[16,16,1]{2,0,1:T(8,128)S(1)}, f32[16,16,1]{2,0,1:T(8,128)S(1)}, u32[]{:S(2)}, u32[]{:S(2)}) %collective-permute-start.14) | collective-permute-done | bytes 1056 | tf_op jit(solution)/shard_map/ppermute | solution.py:24
  167.9 2.4 %collective-permute-start.17 = (f32[16,16,1]{2,0,1:T(8,128)S(1)}, f32[16,16,1]{2,0,1:T(8,128)S(1)}, u32[]{:S(2)}, u32[]{:S(2)}) collective-permute-start(f32[16,16,1]{2,0,1:T(8,128)S(1)} %copy.46), channel_id=1, source_target_pairs={{0,1},{1,2},{2,3},{4,5},{5,6},{6,7},{8,9},{9,10},{10,11},{12,13},{... | collective-permute-start | bytes 3080 | tf_op jit(solution)/shard_map/ppermute | solution.py:24
  170.4 4.5 %collective-permute-start.15 = (f32[1,16,128]{2,0,1:T(1,128)S(1)}, f32[1,16,128]{2,0,1:T(1,128)S(1)}, u32[]{:S(2)}, u32[]{:S(2)}) collective-permute-start(f32[1,16,128]{2,0,1:T(1,128)S(1)} %slice_bitcast_fusion.19), channel_id=1, source_target_pairs={{0,32},{32,64},{64,96},{96,128},{128,160},{160,192},{192,224},{1,3... | collective-permute-start | bytes 24584 | tf_op jit(solution)/shard_map/ppermute | solution.py:24
  174.9 7.2 %collective-permute-start.16 = (f32[16,1,128]{2,0,1:T(8,128)S(1)}, f32[16,1,128]{2,0,1:T(8,128)S(1)}, u32[]{:S(2)}, u32[]{:S(2)}) collective-permute-start(f32[16,1,128]{2,0,1:T(8,128)S(1)} %slice_bitcast_fusion.18), channel_id=1, source_target_pairs={{0,4},{4,8},{8,12},{12,16},{16,20},{20,24},{24,28},{1,5},{5,9},{9,... | collective-permute-start | bytes 24584 | tf_op jit(solution)/shard_map/ppermute | solution.py:24
  (83 shorter events, 6.5 us)
Async XLA Ops:
  5.4 6.3 %copy-start.2 = (s32[32,128]{1,0:T(8,128)S(1)}, s32[32,128]{1,0:T(8,128)}, u32[]{:S(2)}) copy-start(s32[32,128]{1,0:T(8,128)} %param.5) | copy-start | bytes 49156
  5.4 6.3 %copy-start.3 = (s32[32]{0:T(128)S(1)}, s32[32]{0:T(128)}, u32[]{:S(2)}) copy-start(s32[32]{0:T(128)} %param.6) | copy-start | bytes 388
  5.4 54.5 %all-to-all-start = ((f32[4,128,16,128]{3,2,0,1:T(8,128)}), f32[4,128,16,128]{3,2,0,1:T(8,128)}, u32[]{:S(2)}, u32[]{:S(2)}) async-start(f32[4,128,16,128]{3,2,0,1:T(8,128)} %copy.34), calls=%async_computation | async-start | bytes 8388608 | tf_op jit(solution)/shard_map/all_to_all | solution.py:67
  62.7 50.1 %copy-start.1 = (f32[16,16,128]{2,1,0:T(8,128)S(1)}, f32[16,16,128]{2,1,0:T(8,128)}, u32[]{:S(2)}) copy-start(f32[16,16,128]{2,1,0:T(8,128)} %param.7) | copy-start | bytes 393220
  67.1 77.1 %copy-start = (f32[16,1,16,128]{3,1,2,0:T(1,128)}, f32[16,1,16,128]{3,1,2,0:T(1,128)S(1)}, u32[]{:S(2)}) copy-start(f32[16,1,16,128]{3,1,2,0:T(1,128)S(1)} %fusion) | copy-start | bytes 393220
  112.9 7.0 %collective-permute-start.2 = (f32[16,16,1]{2,0,1:T(8,128)S(1)}, f32[16,16,1]{2,0,1:T(8,128)S(1)}, u32[]{:S(2)}, u32[]{:S(2)}) collective-permute-start(f32[16,16,1]{2,0,1:T(8,128)S(1)} %bitcast.165), channel_id=1, source_target_pairs={{1,0},{2,1},{3,2},{5,4},{6,5},{7,6},{9,8},{10,9},{11,10},{13,12},{... | collective-permute-start | bytes 3080 | tf_op jit(solution)/shard_map/ppermute | solution.py:24
  114.2 5.7 %collective-permute-start = (f32[1,16,128]{2,0,1:T(1,128)S(1)}, f32[1,16,128]{2,0,1:T(1,128)S(1)}, u32[]{:S(2)}, u32[]{:S(2)}) collective-permute-start(f32[1,16,128]{2,0,1:T(1,128)S(1)} %slice.181), channel_id=1, source_target_pairs={{32,0},{64,32},{96,64},{128,96},{160,128},{192,160},{224,192},{33,... | collective-permute-start | bytes 24584 | tf_op jit(solution)/shard_map/ppermute | solution.py:24
  115.5 5.9 %collective-permute-start.1 = (f32[16,1,128]{2,0,1:T(8,128)S(1)}, f32[16,1,128]{2,0,1:T(8,128)S(1)}, u32[]{:S(2)}, u32[]{:S(2)}) collective-permute-start(f32[16,1,128]{2,0,1:T(8,128)S(1)} %slice.183), channel_id=1, source_target_pairs={{4,0},{8,4},{12,8},{16,12},{20,16},{24,20},{28,24},{5,1},{9,5},{13... | collective-permute-start | bytes 24584 | tf_op jit(solution)/shard_map/ppermute | solution.py:24
  122.2 10.7 %collective-permute-start.5 = (f32[16,16,1]{2,0,1:T(8,128)S(1)}, f32[16,16,1]{2,0,1:T(8,128)S(1)}, u32[]{:S(2)}, u32[]{:S(2)}) collective-permute-start(f32[16,16,1]{2,0,1:T(8,128)S(1)} %copy.40), channel_id=1, source_target_pairs={{0,1},{1,2},{2,3},{4,5},{5,6},{6,7},{8,9},{9,10},{10,11},{12,13},{... | collective-permute-start | bytes 3080 | tf_op jit(solution)/shard_map/ppermute | solution.py:24
  126.2 6.7 %collective-permute-start.3 = (f32[1,16,128]{2,0,1:T(1,128)S(1)}, f32[1,16,128]{2,0,1:T(1,128)S(1)}, u32[]{:S(2)}, u32[]{:S(2)}) collective-permute-start(f32[1,16,128]{2,0,1:T(1,128)S(1)} %slice_bitcast_fusion.23), channel_id=1, source_target_pairs={{0,32},{32,64},{64,96},{96,128},{128,160},{160,192},{192,224},{1,3... | collective-permute-start | bytes 24584 | tf_op jit(solution)/shard_map/ppermute | solution.py:24
  130.4 3.3 %collective-permute-start.4 = (f32[16,1,128]{2,0,1:T(8,128)S(1)}, f32[16,1,128]{2,0,1:T(8,128)S(1)}, u32[]{:S(2)}, u32[]{:S(2)}) collective-permute-start(f32[16,1,128]{2,0,1:T(8,128)S(1)} %slice_bitcast_fusion.22), channel_id=1, source_target_pairs={{0,4},{4,8},{8,12},{12,16},{16,20},{20,24},{24,28},{1,5},{5,9},{9,... | collective-permute-start | bytes 24584 | tf_op jit(solution)/shard_map/ppermute | solution.py:24
  133.8 10.2 %collective-permute-start.6 = (f32[1,16,128]{2,0,1:T(1,128)S(1)}, f32[1,16,128]{2,0,1:T(1,128)S(1)}, u32[]{:S(2)}, u32[]{:S(2)}) collective-permute-start(f32[1,16,128]{2,0,1:T(1,128)S(1)} %slice.196), channel_id=1, source_target_pairs={{32,0},{64,32},{96,64},{128,96},{160,128},{192,160},{224,192},{33,... | collective-permute-start | bytes 24584 | tf_op jit(solution)/shard_map/ppermute | solution.py:24
  135.1 8.9 %collective-permute-start.7 = (f32[16,1,128]{2,0,1:T(8,128)S(1)}, f32[16,1,128]{2,0,1:T(8,128)S(1)}, u32[]{:S(2)}, u32[]{:S(2)}) collective-permute-start(f32[16,1,128]{2,0,1:T(8,128)S(1)} %slice.198), channel_id=1, source_target_pairs={{4,0},{8,4},{12,8},{16,12},{20,16},{24,20},{28,24},{5,1},{9,5},{13... | collective-permute-start | bytes 24584 | tf_op jit(solution)/shard_map/ppermute | solution.py:24
  137.0 7.0 %collective-permute-start.8 = (f32[16,16,1]{2,0,1:T(8,128)S(1)}, f32[16,16,1]{2,0,1:T(8,128)S(1)}, u32[]{:S(2)}, u32[]{:S(2)}) collective-permute-start(f32[16,16,1]{2,0,1:T(8,128)S(1)} %bitcast.166), channel_id=1, source_target_pairs={{1,0},{2,1},{3,2},{5,4},{6,5},{7,6},{9,8},{10,9},{11,10},{13,12},{... | collective-permute-start | bytes 3080 | tf_op jit(solution)/shard_map/ppermute | solution.py:24
  144.9 12.2 %collective-permute-start.11 = (f32[16,16,1]{2,0,1:T(8,128)S(1)}, f32[16,16,1]{2,0,1:T(8,128)S(1)}, u32[]{:S(2)}, u32[]{:S(2)}) collective-permute-start(f32[16,16,1]{2,0,1:T(8,128)S(1)} %copy.43), channel_id=1, source_target_pairs={{0,1},{1,2},{2,3},{4,5},{5,6},{6,7},{8,9},{9,10},{10,11},{12,13},{... | collective-permute-start | bytes 3080 | tf_op jit(solution)/shard_map/ppermute | solution.py:24
  146.9 10.2 %collective-permute-start.10 = (f32[16,1,128]{2,0,1:T(8,128)S(1)}, f32[16,1,128]{2,0,1:T(8,128)S(1)}, u32[]{:S(2)}, u32[]{:S(2)}) collective-permute-start(f32[16,1,128]{2,0,1:T(8,128)S(1)} %slice_bitcast_fusion.20), channel_id=1, source_target_pairs={{0,4},{4,8},{8,12},{12,16},{16,20},{20,24},{24,28},{1,5},{5,9},{9,... | collective-permute-start | bytes 24584 | tf_op jit(solution)/shard_map/ppermute | solution.py:24
  152.8 5.0 %collective-permute-start.9 = (f32[1,16,128]{2,0,1:T(1,128)S(1)}, f32[1,16,128]{2,0,1:T(1,128)S(1)}, u32[]{:S(2)}, u32[]{:S(2)}) collective-permute-start(f32[1,16,128]{2,0,1:T(1,128)S(1)} %slice_bitcast_fusion.21), channel_id=1, source_target_pairs={{0,32},{32,64},{64,96},{96,128},{128,160},{160,192},{192,224},{1,3... | collective-permute-start | bytes 24584 | tf_op jit(solution)/shard_map/ppermute | solution.py:24
  158.0 8.9 %collective-permute-start.12 = (f32[1,16,128]{2,0,1:T(1,128)S(1)}, f32[1,16,128]{2,0,1:T(1,128)S(1)}, u32[]{:S(2)}, u32[]{:S(2)}) collective-permute-start(f32[1,16,128]{2,0,1:T(1,128)S(1)} %slice.211), channel_id=1, source_target_pairs={{32,0},{64,32},{96,64},{128,96},{160,128},{192,160},{224,192},{33,... | collective-permute-start | bytes 24584 | tf_op jit(solution)/shard_map/ppermute | solution.py:24
  159.3 7.6 %collective-permute-start.13 = (f32[16,1,128]{2,0,1:T(8,128)S(1)}, f32[16,1,128]{2,0,1:T(8,128)S(1)}, u32[]{:S(2)}, u32[]{:S(2)}) collective-permute-start(f32[16,1,128]{2,0,1:T(8,128)S(1)} %slice.213), channel_id=1, source_target_pairs={{4,0},{8,4},{12,8},{16,12},{20,16},{24,20},{28,24},{5,1},{9,5},{13... | collective-permute-start | bytes 24584 | tf_op jit(solution)/shard_map/ppermute | solution.py:24
  161.2 5.7 %collective-permute-start.14 = (f32[16,16,1]{2,0,1:T(8,128)S(1)}, f32[16,16,1]{2,0,1:T(8,128)S(1)}, u32[]{:S(2)}, u32[]{:S(2)}) collective-permute-start(f32[16,16,1]{2,0,1:T(8,128)S(1)} %bitcast.167), channel_id=1, source_target_pairs={{1,0},{2,1},{3,2},{5,4},{6,5},{7,6},{9,8},{10,9},{11,10},{13,12},{... | collective-permute-start | bytes 3080 | tf_op jit(solution)/shard_map/ppermute | solution.py:24
  167.9 14.3 %collective-permute-start.17 = (f32[16,16,1]{2,0,1:T(8,128)S(1)}, f32[16,16,1]{2,0,1:T(8,128)S(1)}, u32[]{:S(2)}, u32[]{:S(2)}) collective-permute-start(f32[16,16,1]{2,0,1:T(8,128)S(1)} %copy.46), channel_id=1, source_target_pairs={{0,1},{1,2},{2,3},{4,5},{5,6},{6,7},{8,9},{9,10},{10,11},{12,13},{... | collective-permute-start | bytes 3080 | tf_op jit(solution)/shard_map/ppermute | solution.py:24
  170.4 11.8 %collective-permute-start.15 = (f32[1,16,128]{2,0,1:T(1,128)S(1)}, f32[1,16,128]{2,0,1:T(1,128)S(1)}, u32[]{:S(2)}, u32[]{:S(2)}) collective-permute-start(f32[1,16,128]{2,0,1:T(1,128)S(1)} %slice_bitcast_fusion.19), channel_id=1, source_target_pairs={{0,32},{32,64},{64,96},{96,128},{128,160},{160,192},{192,224},{1,3... | collective-permute-start | bytes 24584 | tf_op jit(solution)/shard_map/ppermute | solution.py:24
  174.9 8.0 %collective-permute-start.16 = (f32[16,1,128]{2,0,1:T(8,128)S(1)}, f32[16,1,128]{2,0,1:T(8,128)S(1)}, u32[]{:S(2)}, u32[]{:S(2)}) collective-permute-start(f32[16,1,128]{2,0,1:T(8,128)S(1)} %slice_bitcast_fusion.18), channel_id=1, source_target_pairs={{0,4},{4,8},{8,12},{12,16},{16,20},{20,24},{24,28},{1,5},{5,9},{9,... | collective-permute-start | bytes 24584 | tf_op jit(solution)/shard_map/ppermute | solution.py:24
where the time goes:
time: 186 us; the launch traced here: 184 us
  waiting for transfers between devices  61.4 us (33%)
  starting transfers between devices  59.2 us (32%)
  blocking collectives  44.4 us (24%)
  local copies, waits for them, and re-layouts  10.1 us (5%)
  matrix products  4.61 us (2%)
  other arithmetic  2.17 us (1%)
  between operations  1.98 us (1%)
    ppermute x18, starting transfers between devices, from_behind(): return lax.ppermute(block, axis, route)  52.8 us
    all_to_all x1, waiting for transfers between devices, shards(): lax.all_to_all(partials, GX, split_axis=1, concat_axis=0, tiled=True)  47.9 us
    psum x5, blocking collectives, over_axes(): return functools.reduce(lax.psum, axes, shard)  44.4 us
    ppermute x18, waiting for transfers between devices, from_behind(): return lax.ppermute(block, axis, route)  13.5 us
    all_to_all x1, starting transfers between devices, shards(): lax.all_to_all(partials, GX, split_axis=1, concat_axis=0, tiled=True)  6.32 us
    unnamed x10, local copies, waits for them, and re-layouts  5.52 us
    dot_general x1, matrix products, shards(): jnp.einsum('gx,gxyz->xyz', local_signs, lax.all_to_all(partials, GX, spli...  4.35 us
  transfers between devices with their start and end apart: 19, of which 7 were waited for; matrix products, arithmetic and copies ran while one was open for 0% of the time, Pallas kernels for 0%

commit v1 on v0

v1 whole, which is shorter than its diff:
```python
import jax
import jax.numpy as jnp
from jax import lax
from jax.experimental import pallas as pl
from jax.experimental.pallas import tpu as pltpu
from jax.sharding import Mesh
from jax.sharding import PartitionSpec as P

ITERS = 3
HALO = ITERS
GX = ("gx_0", "gx_1")
GY = ("gy_0", "gy_1")
XY = GX + GY
ALL = XY + ("gz",)

step_length = 0.5
tv_weight = 0.2
dual_step = 0.28
primal_step = 0.28

VMEM = pl.BlockSpec(memory_space=pltpu.VMEM)
SMEM = pl.BlockSpec(memory_space=pltpu.SMEM)
HBM = pl.BlockSpec(memory_space=pltpu.HBM)
PARAMS = pltpu.CompilerParams(vmem_limit_bytes=16 * 1024 * 1024)
F32 = jnp.float32


def shift(block, axis, distance):
    size = lax.axis_size(axis)
    return lax.ppermute(block, axis, [(i, (i + distance) % size) for i in range(size)])


def struct(*shape):
    return jax.ShapeDtypeStruct(shape, F32)


def presum(partials, code_bits, group_map, base, chunks):
    slots, nx, by, bz = partials.shape
    rows = nx // chunks

    def kernel(base_ref, map_ref, bits_ref, part_ref, out_ref, buf, sems):
        def copy(c):
            part = pl.ds(c * rows, rows)
            return pltpu.make_async_copy(part_ref.at[:, part], buf.at[:, part], sems.at[c])

        for c in range(chunks):
            copy(c).start()
        groups = [map_ref[base_ref[0] + s] for s in range(slots)]
        for c in range(chunks):
            copy(c).wait()

            def row(i, carry):
                x = c * rows + i
                total = None
                for s in range(slots):
                    sign = (2 * bits_ref[groups[s], x] - 1).astype(F32)
                    term = sign * buf[s, x]
                    total = term if total is None else total + term
                out_ref[x] = total
                return carry

            lax.fori_loop(0, rows, row, 0, unroll=4)

    return pl.pallas_call(
        kernel,
        name="presum",
        compiler_params=PARAMS,
        out_shape=struct(nx, by, bz),
        in_specs=[SMEM, SMEM, SMEM, HBM],
        out_specs=VMEM,
        scratch_shapes=[pltpu.VMEM(partials.shape, F32), pltpu.SemaphoreType.DMA((chunks,))],
    )(base, group_map, code_bits, pltpu.with_memory_space_constraint(partials, pltpu.HBM))


def reduce_pack(parts, velocity, members):
    bx, by, bz = velocity.shape

    def kernel(part_ref, v_ref, g_ref, first_ref, last_ref, square_ref):
        squares = jnp.zeros((by, bz), F32)
        for i in range(bx):
            total = part_ref[i]
            for m in range(1, members):
                total = total + part_ref[m * bx + i]
            g_ref[i] = total
            squares = squares + total * total
            if i < HALO:
                first_ref[i] = total
                first_ref[HALO + i] = v_ref[i]
            if i >= bx - HALO:
                last_ref[i - bx + HALO] = total
                last_ref[i - bx + 2 * HALO] = v_ref[i]
        square_ref[...] = jnp.broadcast_to(jnp.sum(squares, axis=0, keepdims=True), (8, bz))

    edge = struct(2 * HALO, by, bz)
    return pl.pallas_call(
        kernel,
        name="reduce_pack",
        compiler_params=PARAMS,
        out_shape=(struct(bx, by, bz), edge, edge, struct(8, bz)),
        in_specs=[VMEM, VMEM],
        out_specs=(VMEM,) * 4,
    )(parts, velocity)


def plane_of(main_ref, before_ref, after_ref, field, p, bx):
    if p < HALO:
        return before_ref[field * HALO + p]
    if p < HALO + bx:
        return main_ref[p - HALO]
    return after_ref[field * HALO + p - HALO - bx]


def sublane(shape):
    return lax.broadcasted_iota(jnp.int32, shape, len(shape) - 2)


def lane(shape):
    return lax.broadcasted_iota(jnp.int32, shape, len(shape) - 1)


def pack_y(gradient, velocity, before_x, after_x):
    bx, by, bz = velocity.shape
    pairs = (bx + 2 * HALO) // 2

    def kernel(g_ref, v_ref, before_ref, after_ref, first_ref, last_ref):
        low = sublane((8, bz)) < 4
        for field, main in enumerate((g_ref, v_ref)):
            for q in range(pairs):
                even = plane_of(main, before_ref, after_ref, field, 2 * q, bx)
                odd = plane_of(main, before_ref, after_ref, field, 2 * q + 1, bx)
                first_ref[field * pairs + q] = jnp.where(low, even[:8], pltpu.roll(odd[:8], 4, 0))
                last_ref[field * pairs + q] = jnp.where(
                    low, pltpu.roll(even[by - 8 :], 4, 0), odd[by - 8 :]
                )

    edge = struct(2 * pairs, 8, bz)
    return pl.pallas_call(
        kernel,
        name="pack_y",
        compiler_params=PARAMS,
        out_shape=(edge, edge),
        in_specs=[VMEM] * 4,
        out_specs=(VMEM,) * 2,
    )(gradient, velocity, before_x, after_x)


def rows_of(before_ref, after_ref, field, p, pairs):
    after = after_ref[field * pairs + p // 2]
    before = before_ref[field * pairs + p // 2]
    low = sublane(after.shape) < 4
    if p % 2 == 0:
        return jnp.where(low, after, pltpu.roll(before, 4, 0))
    return jnp.where(low, pltpu.roll(after, 4, 0), before)


def pack_z(gradient, velocity, before_x, after_x, before_y, after_y, squares):
    bx, by, bz = velocity.shape
    planes = bx + 2 * HALO
    pairs = planes // 2
    groups = bz // 4
    tall = by + 8

    def kernel(g_ref, v_ref, bx_ref, ax_ref, by_ref, ay_ref, sq_ref, first_ref, last_ref, sum_ref):
        group = lane((tall, bz)) // 4
        for field, main in enumerate((g_ref, v_ref)):
            first = jnp.zeros((tall, bz), F32)
            last = jnp.zeros((tall, bz), F32)
            for p in range(planes):
                own = plane_of(main, bx_ref, ax_ref, field, p, bx)
                extra = rows_of(by_ref, ay_ref, field, p, pairs)
                plane = jnp.concatenate([own, extra], 0)
                turned = pltpu.roll(plane, 4 * p, 1) if p else plane
                first = jnp.where(group == p, turned, first)
                last = jnp.where(group == (p - 1) % groups, turned, last)
            first_ref[pl.ds(field * tall, tall)] = first
            last_ref[pl.ds(field * tall, tall)] = last
        total = jnp.broadcast_to(jnp.sum(sq_ref[...], axis=0), (8, bz))
        first_ref[pl.ds(2 * tall, 8)] = total
        last_ref[pl.ds(2 * tall, 8)] = total
        sum_ref[...] = total

    edge = struct(2 * tall + 8, bz)
    return pl.pallas_call(
        kernel,
        name="pack_z",
        compiler_params=PARAMS,
        out_shape=(edge, edge, struct(8, bz)),
        in_specs=[VMEM] * 7,
        out_specs=(VMEM,) * 3,
    )(gradient, velocity, before_x, after_x, before_y, after_y, squares)


def proximal(device, gradient, velocity, halos, sums, sizes):
    bx, by, bz = velocity.shape
    planes = bx + 2 * HALO
    pairs = planes // 2
    tall = by + 8
    wide = 2 * bz
    size_x, size_y, size_z = sizes
    cells = size_x * bx * size_y * by * size_z * bz

    def kernel(
        dev_ref,
        g_ref,
        v_ref,
        bx_ref,
        ax_ref,
        by_ref,
        ay_ref,
        bz_ref,
        az_ref,
        own_ref,
        far_ref,
        gradient_ref,
        model_ref,
        target,
        current,
        extra,
        dual_x,
        dual_y,
        dual_z,
        model,
        sems,
    ):
        gradient_copy = pltpu.make_async_copy(g_ref, gradient_ref, sems.at[0])
        gradient_copy.start()
        dev = dev_ref[0]
        pos_z = dev % size_z
        pos_y = (dev // size_z) % size_y
        pos_x = dev // (size_z * size_y)

        total = own_ref[0:1] + far_ref[0:1]
        total = total + bz_ref[2 * tall : 2 * tall + 1] + az_ref[2 * tall : 2 * tall + 1]
        total = jnp.sum(total, axis=1, keepdims=True)
        scale = step_length * lax.rsqrt(total / cells + 1.0)
        scale = jnp.broadcast_to(scale, (1, bz))

        side_lane = lane((tall, bz)) < bz // 2
        before_z = bz_ref[pl.ds(tall, tall)] - scale * bz_ref[pl.ds(0, tall)]
        after_z = az_ref[pl.ds(tall, tall)] - scale * az_ref[pl.ds(0, tall)]
        for p in range(planes):
            own = plane_of(v_ref, bx_ref, ax_ref, 1, p, bx) - scale * plane_of(
                g_ref, bx_ref, ax_ref, 0, p, bx
            )
            rows = rows_of(by_ref, ay_ref, 1, p, pairs) - scale * rows_of(
                by_ref, ay_ref, 0, p, pairs
            )
            back = (bz - 4 * p) % bz
            after = pltpu.roll(after_z, back, 1) if back else after_z
            before = pltpu.roll(before_z, back, 1) if back else before_z
            target[p, pl.ds(0, by), pl.ds(0, bz)] = own
            target[p, pl.ds(by, 8), pl.ds(0, bz)] = rows
            target[p, :, pl.ds(bz, bz)] = jnp.where(side_lane, after, before)

        def factor(index, limit):
            return jnp.where((index >= 0) & (index < limit - 1), dual_step, 0.0).astype(F32)

        row = sublane((tall, 1))
        row = jnp.where(row < by + 4, row, row - tall) + pos_y * by
        factor_y = factor(row, size_y * by)
        col = lane((1, wide))
        col = jnp.where(col < bz + bz // 2, col, col - wide) + pos_z * bz
        factor_z = factor(col, size_z * bz)
        shrink = 1.0 / (1.0 + primal_step)
        gain = primal_step / (1.0 + primal_step)

        for iteration in range(ITERS):
            first = iteration == 0
            final = iteration == ITERS - 1
            here_ref = target if first else extra
            ahead = here_ref[iteration]
            before_x = None
            for p in range(iteration, planes - 1 - iteration):
                here = ahead
                ahead = here_ref[p + 1]
                index = pos_x * bx + (p - HALO)
                factor_x = factor(index, size_x * bx)
                dx = factor_x * (ahead - here)
                dy = factor_y * (pltpu.roll(here, tall - 1, 0) - here)
                dz = factor_z * (pltpu.roll(here, wide - 1, 1) - here)
                if not first:
                    dx = dual_x[p] + dx
                    dy = dual_y[p] + dy
                    dz = dual_z[p] + dz
                norm = dx * dx + dy * dy + dz * dz
                ratio = jnp.minimum(1.0, tv_weight * lax.rsqrt(norm))
                dx = dx * ratio
                dy = dy * ratio
                dz = dz * ratio
                if not final:
                    dual_x[p] = dx
                    dual_y[p] = dy
                    dual_z[p] = dz
                if p > iteration:
                    if final:
                        spread = dx[:by, :bz] - before_x
                        spread += dy[:by, :bz] - pltpu.roll(dy[:, :bz], 1, 0)[:by]
                        spread += dz[:by, :bz] - pltpu.roll(dz[:by], 1, 1)[:, :bz]
                        goal = target[p, pl.ds(0, by), pl.ds(0, bz)]
                        old = current[p, pl.ds(0, by), pl.ds(0, bz)]
                        model[p - HALO] = shrink * old + gain * (spread + goal)
                    else:
                        spread = dx - before_x
                        spread += dy - pltpu.roll(dy, 1, 0)
                        spread += dz - pltpu.roll(dz, 1, 1)
                        if first:
                            new = here + gain * spread
                            old = here
                        else:
                            old = current[p]
                            new = shrink * old + gain * (spread + target[p])
                        current[p] = new
                        extra[p] = 2.0 * new - old
                before_x = dx[:by, :bz] if final else dx
        model_copy = pltpu.make_async_copy(model, model_ref, sems.at[1])
        model_copy.start()
        gradient_copy.wait()
        model_copy.wait()

    field = pltpu.VMEM((planes, tall, wide), F32)
    return pl.pallas_call(
        kernel,
        name="proximal",
        compiler_params=PARAMS,
        out_shape=(struct(bx, by, bz),) * 2,
        in_specs=[SMEM] + [VMEM] * 10,
        out_specs=(HBM,) * 2,
        scratch_shapes=[field] * 6 + [pltpu.VMEM((bx, by, bz), F32), pltpu.SemaphoreType.DMA((2,))],
    )(device, gradient, velocity, *halos, *sums)


def shards(partials, code_bits, group_map, velocity):
    bx, by, bz = velocity.shape
    size_x, size_y, size_z = (lax.axis_size(axis) for axis in (GX, GY, "gz"))
    base = (lax.axis_index(GX) * partials.shape[0]).astype(jnp.int32).reshape(1)
    device = lax.axis_index(ALL).astype(jnp.int32).reshape(1)

    local = presum(partials, code_bits, group_map, base, 8)
    parts = lax.all_to_all(local, GX, split_axis=0, concat_axis=0, tiled=True)
    gradient, first_x, last_x, squares = reduce_pack(parts, velocity, size_x)

    after_x = shift(first_x, GX, -1)
    before_x = shift(last_x, GX, 1)
    table = jnp.broadcast_to(squares[:1][None], (size_x * size_y, 1, bz))
    table = lax.all_to_all(table, XY, split_axis=0, concat_axis=0, tiled=True)

    first_y, last_y = pack_y(gradient, velocity, before_x, after_x)
    after_y = shift(first_y, GY, -1)
    before_y = shift(last_y, GY, 1)

    first_z, last_z, own = pack_z(
        gradient, velocity, before_x, after_x, before_y, after_y, table
    )
    after_z = shift(first_z, "gz", -1)
    before_z = shift(last_z, "gz", 1)
    far = shift(own, "gz", 2)

    return proximal(
        device,
        gradient,
        velocity,
        (before_x, after_x, before_y, after_y, before_z, after_z),
        (own, far),
        (size_x, size_y, size_z),
    )


def solution(mesh):
    torus = Mesh(
        mesh.devices.reshape(4, 2, 4, 2, mesh.shape["gz"]), ("gx_0", "gx_1", "gy_0", "gy_1", "gz")
    )
    placed = (P(GX, None, GY, "gz"), P(), P(), P(GX, GY, "gz"))
    return jax.shard_map(
        shards,
        mesh=torus,
        in_specs=placed,
        out_specs=(P(GX, GY, "gz"), P(GX, GY, "gz")),
        check_vma=False,
    )
```

time: 186 us -> 70.3 us (0.38); the launches traced: 184 us -> 70.1 us
  waiting for transfers between devices: 61.4 us -> 3.89 us
  starting transfers between devices: 59.2 us -> 14 us
  local copies, waits for them, and re-layouts: 10.1 us -> 1.43 us
  Pallas kernels: 0 us -> 8.12 us
  matrix products: 4.61 us -> 0 us
  blocking collectives: 44.4 us -> 41.9 us
  other arithmetic: 2.17 us -> 0 us
    all_to_all x1 -> x0, waiting for transfers between devices: 47.9 us -> none  [shards(): lax.all_to_all(partials, GX, split_axis=1, concat_axis=0, tiled=True)]
    psum x5 -> x0, blocking collectives: 44.4 us -> none  [over_axes(): return functools.reduce(lax.psum, axes, shard)]
    all_to_all x0 -> x2, blocking collectives: none -> 41.9 us  [the longest x1 21 us: shards(): table = lax.all_to_all(table, XY, split_axis=0, concat_axis=0, tiled=True)]
    ppermute x18 -> x7, starting transfers between devices: 52.8 us -> 14 us  [shift(): lax.ppermute(block, axis, [(i, (i + distance) % size) for i in range(size)])]
    ppermute x18 -> x7, waiting for transfers between devices: 13.5 us -> 3.89 us  [shift(): lax.ppermute(block, axis, [(i, (i + distance) % size) for i in range(size)])]
    pallas_call x0 -> x5, Pallas kernels: none -> 8.12 us  [the longest x1 4.66 us: proximal(): pl.pallas_call(kernel, name='proximal', compiler_params=PARAMS, out_shape...]
    all_to_all x1 -> x0, starting transfers between devices: 6.32 us -> none  [shards(): lax.all_to_all(partials, GX, split_axis=1, concat_axis=0, tiled=True)]
    dot_general x2 -> x0, matrix products: 4.61 us -> none  [the longest x1 4.35 us: shards(): jnp.einsum('gx,gxyz->xyz', local_signs, lax.all_to_all(partials, GX, spli...]
  transfers between devices with their start and end apart: 19 -> 7, of which waited for: 7 -> 2; matrix products, arithmetic and copies ran while one was open for 0% -> 0% of each run, Pallas kernels for 0% -> 0%
where the time goes in v1:
time: 70.3 us; the launch traced here: 70.1 us
  blocking collectives  41.9 us (60%)
  starting transfers between devices  14 us (20%)
  Pallas kernels  8.12 us (12%)
  waiting for transfers between devices  3.89 us (6%)
  local copies, waits for them, and re-layouts  1.43 us (2%)
    all_to_all x1, blocking collectives, shards(): table = lax.all_to_all(table, XY, split_axis=0, concat_axis=0, tiled=True)  21 us
    all_to_all x1, blocking collectives, shards(): parts = lax.all_to_all(local, GX, split_axis=0, concat_axis=0, tiled=True)  21 us
    ppermute x7, starting transfers between devices, shift(): lax.ppermute(block, axis, [(i, (i + distance) % size) for i in range(size)])  14 us
    pallas_call x1, Pallas kernels, proximal(): pl.pallas_call(kernel, name='proximal', compiler_params=PARAMS, out_shape...  4.66 us
    ppermute x7, waiting for transfers between devices, shift(): lax.ppermute(block, axis, [(i, (i + distance) % size) for i in range(size)])  3.89 us
    pallas_call x1, Pallas kernels, presum(): pl.pallas_call(kernel, name='presum', compiler_params=PARAMS, out_shape=s...  3.17 us
  transfers between devices with their start and end apart: 7, of which 2 were waited for; matrix products, arithmetic and copies ran while one was open for 0% of the time, Pallas kernels for 0%

profile of v1, /device:TPU:1, one launch (start us, length us, event | category | flops | bytes accessed | tf_op | source)
XLA Modules:
  0.0 70.1 jit_solution(16689980978631410075)
XLA Ops:
  0.6 0.0 copy-start
  0.7 0.0 copy-start.1
  0.7 0.7 %copy-done.1 = s32[32,128]{1,0:T(8,128)S(1)} copy-done((s32[32,128]{1,0:T(8,128)S(1)}, s32[32,128]{1,0:T(8,128)}, u32[]{:S(2)}) %copy-start.1) | copy-done | bytes 16408
  1.4 0.0 copy-start.2
  1.4 0.7 copy-done.2
  2.1 3.2 %presum.1 = f32[128,16,128]{2,1,0:T(8,128)S(1)} custom-call(s32[1]{0:T(128)} %bitcast.1.base_ref, s32[32]{0:T(128)S(1)} %copy-done.2, s32[32,128]{1,0:T(8,128)S(1)} %copy-done.1, f32[4,128,16,128]{3,2,1,0:T(8,128)} %part_ref.1), custom_call_target="tpu_custom_call" | custom-call | tf_op jit(solution)/shard_map/presum/pallas_call | solution.py:64
  5.2 21.0 %all_to_all.10.part_ref = f32[128,16,128]{2,1,0:T(8,128)S(1)} all-to-all(f32[128,16,128]{2,1,0:T(8,128)S(1)} %presum.1), channel_id=1, replica_groups=mesh['gx_0'=4,'gx_1'=2,'gy_0'=4,'gy_1'=2,'gz'=4] {'gx_0','gx_1'}, dimensions={0} | all-to-all | bytes 2097152 | tf_op jit(solution)/shard_map/all_to_all | solution.py:339
  26.2 0.0 copy-done
  26.2 0.1 reduce_pack.1
  26.3 0.5 collective-permute-start
  26.8 3.1 %collective-permute-start.1 = (f32[6,16,128]{2,1,0:T(8,128)S(1)}, f32[6,16,128]{2,1,0:T(8,128)S(1)}, u32[]{:S(2)}, u32[]{:S(2)}) collective-permute-start(f32[6,16,128]{2,1,0:T(8,128)S(1)} %get-tuple-element.13), channel_id=1, source_target_pairs={{0,224},{32,0},{64,32},{96,64},{128,96},{160,128},{192,160},{224,1... | collective-permute-start | bytes 147464 | tf_op jit(solution)/shard_map/ppermute | solution.py:30
  29.9 1.5 %collective-permute-done.before_ref.bx_ref = f32[6,16,128]{2,1,0:T(8,128)S(1)} collective-permute-done((f32[6,16,128]{2,1,0:T(8,128)S(1)}, f32[6,16,128]{2,1,0:T(8,128)S(1)}, u32[]{:S(2)}, u32[]{:S(2)}) %collective-permute-start) | collective-permute-done | bytes 49184 | tf_op jit(solution)/shard_map/ppermute | solution.py:30
  31.4 0.0 collective-permute-done.1.after_ref.ax_ref
  31.4 5.9 %collective-permute-start.2 = (f32[22,8,128]{2,1,0:T(8,128)S(1)}, f32[22,8,128]{2,1,0:T(8,128)S(1)}, u32[]{:S(2)}, u32[]{:S(2)}) collective-permute-start(f32[22,8,128]{2,1,0:T(8,128)S(1)} %get-tuple-element.14), channel_id=1, source_target_pairs={{0,4},{4,8},{8,12},{12,16},{16,20},{20,24},{24,28},{28,0},{1,5},{5... | collective-permute-start | bytes 270344 | tf_op jit(solution)/shard_map/ppermute | solution.py:30
  37.3 0.0 collective-permute-start.3
  37.4 21.0 %all_to_all.11.sq_ref = f32[64,1,128]{2,1,0:T(1,128)S(1)} all-to-all(f32[64,1,128]{2,1,0:T(1,128)S(1)} %broadcast_in_dim.9), channel_id=1, replica_groups=mesh['gx_0'=4,'gx_1'=2,'gy_0'=4,'gy_1'=2,'gz'=4] {'gx_0','gx_1','gy_0','..., dimensions={0} | all-to-all | bytes 65536 | tf_op jit(solution)/shard_map/all_to_all | solution.py:345
  58.3 0.0 collective-permute-done.2.by_ref
  58.3 0.0 collective-permute-done.3.ay_ref
  58.3 0.2 pack_z.1
  58.6 1.4 %collective-permute-start.4 = (f32[56,128]{1,0:T(8,128)S(1)}, f32[56,128]{1,0:T(8,128)S(1)}, u32[]{:S(2)}, u32[]{:S(2)}) collective-permute-start(f32[56,128]{1,0:T(8,128)S(1)} %get-tuple-element.17), channel_id=1, source_target_pairs={{0,1},{1,2},{2,3},{3,0},{4,5},{5,6},{6,7},{7,4},{8,9},{9,10},{10,1... | collective-permute-start | bytes 86024 | tf_op jit(solution)/shard_map/ppermute | solution.py:30
  59.9 1.5 %collective-permute-start.5 = (f32[56,128]{1,0:T(8,128)S(1)}, f32[56,128]{1,0:T(8,128)S(1)}, u32[]{:S(2)}, u32[]{:S(2)}) collective-permute-start(f32[56,128]{1,0:T(8,128)S(1)} %get-tuple-element.18), channel_id=1, source_target_pairs={{0,3},{1,0},{2,1},{3,2},{4,7},{5,4},{6,5},{7,6},{8,11},{9,8},{10,9... | collective-permute-start | bytes 86024 | tf_op jit(solution)/shard_map/ppermute | solution.py:30
  61.5 1.6 %collective-permute-start.6 = (f32[8,128]{1,0:T(8,128)S(1)}, f32[8,128]{1,0:T(8,128)S(1)}, u32[]{:S(2)}, u32[]{:S(2)}) collective-permute-start(f32[8,128]{1,0:T(8,128)S(1)} %get-tuple-element.19.own_ref), channel_id=1, source_target_pairs={{0,2},{1,3},{2,0},{3,1},{4,6},{5,7},{6,4},{7,5},{8,10},{9,11},{10,... | collective-permute-start | bytes 12296 | tf_op jit(solution)/shard_map/ppermute | solution.py:30
  63.0 2.4 %collective-permute-done.6.far_ref = f32[8,128]{1,0:T(8,128)S(1)} collective-permute-done((f32[8,128]{1,0:T(8,128)S(1)}, f32[8,128]{1,0:T(8,128)S(1)}, u32[]{:S(2)}, u32[]{:S(2)}) %collective-permute-start.6) | collective-permute-done | bytes 4128 | tf_op jit(solution)/shard_map/ppermute | solution.py:30
  65.4 0.0 collective-permute-done.4.bz_ref
  65.4 0.0 collective-permute-done.5.az_ref
  65.4 4.7 %proximal.1 = (f32[16,16,128]{2,1,0:T(8,128)}, f32[16,16,128]{2,1,0:T(8,128)}) custom-call(s32[1]{0:T(128)} %bitcast.dev_ref, f32[16,16,128]{2,1,0:T(8,128)S(1)} %get-tuple-element.11.g_ref, f32[16,16,128]{2,1,0:T(8,128)S(1)} %copy-done, f32[6,16,128]{2,1,0:T(8,128)S(1)} %collective-permute-done.before_ref.bx_ref, ...), custom_call_target="tpu_custom_call" | custom-call | tf_op jit(solution)/shard_map/proximal/pallas_call | solution.py:321
  (3 shorter events, 0.0 us)
Async XLA Ops:
  0.6 25.6 %copy-start = (f32[16,16,128]{2,1,0:T(8,128)S(1)}, f32[16,16,128]{2,1,0:T(8,128)}, u32[]{:S(2)}) copy-start(f32[16,16,128]{2,1,0:T(8,128)} %v_ref.7) | copy-start | bytes 393220
  0.7 0.8 %copy-start.1 = (s32[32,128]{1,0:T(8,128)S(1)}, s32[32,128]{1,0:T(8,128)}, u32[]{:S(2)}) copy-start(s32[32,128]{1,0:T(8,128)} %bits_ref.1) | copy-start | bytes 49156
  1.4 0.7 copy-start.2
  26.3 5.1 %collective-permute-start = (f32[6,16,128]{2,1,0:T(8,128)S(1)}, f32[6,16,128]{2,1,0:T(8,128)S(1)}, u32[]{:S(2)}, u32[]{:S(2)}) collective-permute-start(f32[6,16,128]{2,1,0:T(8,128)S(1)} %get-tuple-element.12), channel_id=1, source_target_pairs={{0,32},{32,64},{64,96},{96,128},{128,160},{160,192},{192,224},{224... | collective-permute-start | bytes 147464 | tf_op jit(solution)/shard_map/ppermute | solution.py:30
  26.8 4.6 %collective-permute-start.1 = (f32[6,16,128]{2,1,0:T(8,128)S(1)}, f32[6,16,128]{2,1,0:T(8,128)S(1)}, u32[]{:S(2)}, u32[]{:S(2)}) collective-permute-start(f32[6,16,128]{2,1,0:T(8,128)S(1)} %get-tuple-element.13), channel_id=1, source_target_pairs={{0,224},{32,0},{64,32},{96,64},{128,96},{160,128},{192,160},{224,1... | collective-permute-start | bytes 147464 | tf_op jit(solution)/shard_map/ppermute | solution.py:30
  31.4 26.9 %collective-permute-start.2 = (f32[22,8,128]{2,1,0:T(8,128)S(1)}, f32[22,8,128]{2,1,0:T(8,128)S(1)}, u32[]{:S(2)}, u32[]{:S(2)}) collective-permute-start(f32[22,8,128]{2,1,0:T(8,128)S(1)} %get-tuple-element.14), channel_id=1, source_target_pairs={{0,4},{4,8},{8,12},{12,16},{16,20},{20,24},{24,28},{28,0},{1,5},{5... | collective-permute-start | bytes 270344 | tf_op jit(solution)/shard_map/ppermute | solution.py:30
  37.3 21.0 %collective-permute-start.3 = (f32[22,8,128]{2,1,0:T(8,128)S(1)}, f32[22,8,128]{2,1,0:T(8,128)S(1)}, u32[]{:S(2)}, u32[]{:S(2)}) collective-permute-start(f32[22,8,128]{2,1,0:T(8,128)S(1)} %get-tuple-element.15), channel_id=1, source_target_pairs={{0,28},{4,0},{8,4},{12,8},{16,12},{20,16},{24,20},{28,24},{1,29},{... | collective-permute-start | bytes 270344 | tf_op jit(solution)/shard_map/ppermute | solution.py:30
  58.6 6.9 %collective-permute-start.4 = (f32[56,128]{1,0:T(8,128)S(1)}, f32[56,128]{1,0:T(8,128)S(1)}, u32[]{:S(2)}, u32[]{:S(2)}) collective-permute-start(f32[56,128]{1,0:T(8,128)S(1)} %get-tuple-element.17), channel_id=1, source_target_pairs={{0,1},{1,2},{2,3},{3,0},{4,5},{5,6},{6,7},{7,4},{8,9},{9,10},{10,1... | collective-permute-start | bytes 86024 | tf_op jit(solution)/shard_map/ppermute | solution.py:30
  59.9 5.5 %collective-permute-start.5 = (f32[56,128]{1,0:T(8,128)S(1)}, f32[56,128]{1,0:T(8,128)S(1)}, u32[]{:S(2)}, u32[]{:S(2)}) collective-permute-start(f32[56,128]{1,0:T(8,128)S(1)} %get-tuple-element.18), channel_id=1, source_target_pairs={{0,3},{1,0},{2,1},{3,2},{4,7},{5,4},{6,5},{7,6},{8,11},{9,8},{10,9... | collective-permute-start | bytes 86024 | tf_op jit(solution)/shard_map/ppermute | solution.py:30
  61.5 4.0 %collective-permute-start.6 = (f32[8,128]{1,0:T(8,128)S(1)}, f32[8,128]{1,0:T(8,128)S(1)}, u32[]{:S(2)}, u32[]{:S(2)}) collective-permute-start(f32[8,128]{1,0:T(8,128)S(1)} %get-tuple-element.19.own_ref), channel_id=1, source_target_pairs={{0,2},{1,3},{2,0},{3,1},{4,6},{5,7},{6,4},{7,5},{8,10},{9,11},{10,... | collective-permute-start | bytes 12296 | tf_op jit(solution)/shard_map/ppermute | solution.py:30

commit v2 on v1

--- a/solution.py
+++ b/solution.py
@@ -34,17 +34,28 @@
     return jax.ShapeDtypeStruct(shape, F32)
 
 
+def in_hbm(array):
+    return pltpu.with_memory_space_constraint(array, pltpu.HBM)
+
+
 def presum(partials, code_bits, group_map, base, chunks):
     slots, nx, by, bz = partials.shape
     rows = nx // chunks
 
-    def kernel(base_ref, map_ref, bits_ref, part_ref, out_ref, buf, sems):
+    def kernel(base_ref, map_hbm, bits_hbm, part_ref, out_ref, buf, map_ref, bits_ref, sems):
+        map_copy = pltpu.make_async_copy(map_hbm, map_ref, sems.at[chunks])
+        bits_copy = pltpu.make_async_copy(bits_hbm, bits_ref, sems.at[chunks + 1])
+        map_copy.start()
+        bits_copy.start()
+
         def copy(c):
             part = pl.ds(c * rows, rows)
             return pltpu.make_async_copy(part_ref.at[:, part], buf.at[:, part], sems.at[c])
 
         for c in range(chunks):
             copy(c).start()
+        map_copy.wait()
+        bits_copy.wait()
         groups = [map_ref[base_ref[0] + s] for s in range(slots)]
         for c in range(chunks):
             copy(c).wait()
@@ -66,10 +77,15 @@
         name="presum",
         compiler_params=PARAMS,
         out_shape=struct(nx, by, bz),
-        in_specs=[SMEM, SMEM, SMEM, HBM],
+        in_specs=[SMEM, HBM, HBM, HBM],
         out_specs=VMEM,
-        scratch_shapes=[pltpu.VMEM(partials.shape, F32), pltpu.SemaphoreType.DMA((chunks,))],
-    )(base, group_map, code_bits, pltpu.with_memory_space_constraint(partials, pltpu.HBM))
+        scratch_shapes=[
+            pltpu.VMEM(partials.shape, F32),
+            pltpu.SMEM(group_map.shape, jnp.int32),
+            pltpu.SMEM(code_bits.shape, jnp.int32),
+            pltpu.SemaphoreType.DMA((chunks + 2,)),
+        ],
+    )(base, in_hbm(group_map), in_hbm(code_bits), in_hbm(partials))
 
 
 def reduce_pack(parts, velocity, members):
@@ -330,7 +346,7 @@
 
 
 def shards(partials, code_bits, group_map, velocity):
-    bx, by, bz = velocity.shape
+    _, _, bz = velocity.shape
     size_x, size_y, size_z = (lax.axis_size(axis) for axis in (GX, GY, "gz"))
     base = (lax.axis_index(GX) * partials.shape[0]).astype(jnp.int32).reshape(1)
     device = lax.axis_index(ALL).astype(jnp.int32).reshape(1)
@@ -348,13 +364,10 @@
     after_y = shift(first_y, GY, -1)
     before_y = shift(last_y, GY, 1)
 
-    first_z, last_z, own = pack_z(
-        gradient, velocity, before_x, after_x, before_y, after_y, table
-    )
+    first_z, last_z, own = pack_z(gradient, velocity, before_x, after_x, before_y, after_y, table)
     after_z = shift(first_z, "gz", -1)
     before_z = shift(last_z, "gz", 1)
     far = shift(own, "gz", 2)
-
     return proximal(
         device,
         gradient,

time: 70.3 us -> 68.1 us (0.969)
  local copies, waits for them, and re-layouts: 1.43 us -> 0.03 us
  Pallas kernels: 8.12 us -> 7.37 us
    unnamed x6 -> x2, local copies, waits for them, and re-layouts: 1.4 us -> 0.01 us
    pallas_call x1, Pallas kernels: 3.17 us -> 2.42 us  [presum(): pl.pallas_call(kernel, name='presum', compiler_params=PARAMS, out_shape=s...]
where the time goes in v2:
time: 68.1 us; the launch traced here: 67.9 us
  blocking collectives  41.9 us (62%)
  starting transfers between devices  14 us (21%)
  Pallas kernels  7.37 us (11%)
  waiting for transfers between devices  3.89 us (6%)
    all_to_all x1, blocking collectives, shards(): table = lax.all_to_all(table, XY, split_axis=0, concat_axis=0, tiled=True)  21 us
    all_to_all x1, blocking collectives, shards(): parts = lax.all_to_all(local, GX, split_axis=0, concat_axis=0, tiled=True)  21 us
    ppermute x7, starting transfers between devices, shift(): lax.ppermute(block, axis, [(i, (i + distance) % size) for i in range(size)])  14 us
    pallas_call x1, Pallas kernels, proximal(): pl.pallas_call(kernel, name='proximal', compiler_params=PARAMS, out_shape...  4.66 us
    ppermute x7, waiting for transfers between devices, shift(): lax.ppermute(block, axis, [(i, (i + distance) % size) for i in range(size)])  3.89 us
    pallas_call x1, Pallas kernels, presum(): pl.pallas_call(kernel, name='presum', compiler_params=PARAMS, out_shape=s...  2.42 us
  transfers between devices with their start and end apart: 7, of which 2 were waited for; matrix products, arithmetic and copies ran while one was open for 0% of the time, Pallas kernels for 0%

profile of v2, /device:TPU:1, one launch (start us, length us, event | category | flops | bytes accessed | tf_op | source)
XLA Modules:
  0.0 67.9 jit_solution(4275550522672820159)
XLA Ops:
  0.6 0.0 copy-start
  0.7 2.4 %presum.1 = f32[128,16,128]{2,1,0:T(8,128)S(1)} custom-call(s32[1]{0:T(128)} %bitcast.1.base_ref, s32[32]{0:T(128)} %map_hbm.1, s32[32,128]{1,0:T(8,128)} %bits_hbm.1, f32[4,128,16,128]{3,2,1,0:T(8,128)} %part_ref.1), custom_call_target="tpu_custom_call" | custom-call | tf_op jit(solution)/shard_map/presum/pallas_call | solution.py:75
  3.1 21.0 %all_to_all.10.part_ref = f32[128,16,128]{2,1,0:T(8,128)S(1)} all-to-all(f32[128,16,128]{2,1,0:T(8,128)S(1)} %presum.1), channel_id=1, replica_groups=mesh['gx_0'=4,'gx_1'=2,'gy_0'=4,'gy_1'=2,'gz'=4] {'gx_0','gx_1'}, dimensions={0} | all-to-all | bytes 2097152 | tf_op jit(solution)/shard_map/all_to_all | solution.py:355
  24.0 0.0 copy-done
  24.1 0.1 reduce_pack.1
  24.1 0.5 collective-permute-start
  24.6 3.1 %collective-permute-start.1 = (f32[6,16,128]{2,1,0:T(8,128)S(1)}, f32[6,16,128]{2,1,0:T(8,128)S(1)}, u32[]{:S(2)}, u32[]{:S(2)}) collective-permute-start(f32[6,16,128]{2,1,0:T(8,128)S(1)} %get-tuple-element.13), channel_id=1, source_target_pairs={{0,224},{32,0},{64,32},{96,64},{128,96},{160,128},{192,160},{224,1... | collective-permute-start | bytes 147464 | tf_op jit(solution)/shard_map/ppermute | solution.py:30
  27.8 1.5 %collective-permute-done.before_ref.bx_ref = f32[6,16,128]{2,1,0:T(8,128)S(1)} collective-permute-done((f32[6,16,128]{2,1,0:T(8,128)S(1)}, f32[6,16,128]{2,1,0:T(8,128)S(1)}, u32[]{:S(2)}, u32[]{:S(2)}) %collective-permute-start) | collective-permute-done | bytes 49184 | tf_op jit(solution)/shard_map/ppermute | solution.py:30
  29.2 0.0 collective-permute-done.1.after_ref.ax_ref
  29.3 5.9 %collective-permute-start.2 = (f32[22,8,128]{2,1,0:T(8,128)S(1)}, f32[22,8,128]{2,1,0:T(8,128)S(1)}, u32[]{:S(2)}, u32[]{:S(2)}) collective-permute-start(f32[22,8,128]{2,1,0:T(8,128)S(1)} %get-tuple-element.14), channel_id=1, source_target_pairs={{0,4},{4,8},{8,12},{12,16},{16,20},{20,24},{24,28},{28,0},{1,5},{5... | collective-permute-start | bytes 270344 | tf_op jit(solution)/shard_map/ppermute | solution.py:30
  35.2 0.0 collective-permute-start.3
  35.2 21.0 %all_to_all.11.sq_ref = f32[64,1,128]{2,1,0:T(1,128)S(1)} all-to-all(f32[64,1,128]{2,1,0:T(1,128)S(1)} %broadcast_in_dim.9), channel_id=1, replica_groups=mesh['gx_0'=4,'gx_1'=2,'gy_0'=4,'gy_1'=2,'gz'=4] {'gx_0','gx_1','gy_0','..., dimensions={0} | all-to-all | bytes 65536 | tf_op jit(solution)/shard_map/all_to_all | solution.py:361
  56.2 0.0 collective-permute-done.2.by_ref
  56.2 0.0 collective-permute-done.3.ay_ref
  56.2 0.2 pack_z.1
  56.4 1.4 %collective-permute-start.4 = (f32[56,128]{1,0:T(8,128)S(1)}, f32[56,128]{1,0:T(8,128)S(1)}, u32[]{:S(2)}, u32[]{:S(2)}) collective-permute-start(f32[56,128]{1,0:T(8,128)S(1)} %get-tuple-element.17), channel_id=1, source_target_pairs={{0,1},{1,2},{2,3},{3,0},{4,5},{5,6},{6,7},{7,4},{8,9},{9,10},{10,1... | collective-permute-start | bytes 86024 | tf_op jit(solution)/shard_map/ppermute | solution.py:30
  57.8 1.5 %collective-permute-start.5 = (f32[56,128]{1,0:T(8,128)S(1)}, f32[56,128]{1,0:T(8,128)S(1)}, u32[]{:S(2)}, u32[]{:S(2)}) collective-permute-start(f32[56,128]{1,0:T(8,128)S(1)} %get-tuple-element.18), channel_id=1, source_target_pairs={{0,3},{1,0},{2,1},{3,2},{4,7},{5,4},{6,5},{7,6},{8,11},{9,8},{10,9... | collective-permute-start | bytes 86024 | tf_op jit(solution)/shard_map/ppermute | solution.py:30
  59.3 1.6 %collective-permute-start.6 = (f32[8,128]{1,0:T(8,128)S(1)}, f32[8,128]{1,0:T(8,128)S(1)}, u32[]{:S(2)}, u32[]{:S(2)}) collective-permute-start(f32[8,128]{1,0:T(8,128)S(1)} %get-tuple-element.19.own_ref), channel_id=1, source_target_pairs={{0,2},{1,3},{2,0},{3,1},{4,6},{5,7},{6,4},{7,5},{8,10},{9,11},{10,... | collective-permute-start | bytes 12296 | tf_op jit(solution)/shard_map/ppermute | solution.py:30
  60.9 2.4 %collective-permute-done.6.far_ref = f32[8,128]{1,0:T(8,128)S(1)} collective-permute-done((f32[8,128]{1,0:T(8,128)S(1)}, f32[8,128]{1,0:T(8,128)S(1)}, u32[]{:S(2)}, u32[]{:S(2)}) %collective-permute-start.6) | collective-permute-done | bytes 4128 | tf_op jit(solution)/shard_map/ppermute | solution.py:30
  63.3 0.0 collective-permute-done.4.bz_ref
  63.3 0.0 collective-permute-done.5.az_ref
  63.3 4.7 %proximal.1 = (f32[16,16,128]{2,1,0:T(8,128)}, f32[16,16,128]{2,1,0:T(8,128)}) custom-call(s32[1]{0:T(128)} %bitcast.dev_ref, f32[16,16,128]{2,1,0:T(8,128)S(1)} %get-tuple-element.11.g_ref, f32[16,16,128]{2,1,0:T(8,128)S(1)} %copy-done, f32[6,16,128]{2,1,0:T(8,128)S(1)} %collective-permute-done.before_ref.bx_ref, ...), custom_call_target="tpu_custom_call" | custom-call | tf_op jit(solution)/shard_map/proximal/pallas_call | solution.py:337
  (3 shorter events, 0.0 us)
Async XLA Ops:
  0.6 23.4 %copy-start = (f32[16,16,128]{2,1,0:T(8,128)S(1)}, f32[16,16,128]{2,1,0:T(8,128)}, u32[]{:S(2)}) copy-start(f32[16,16,128]{2,1,0:T(8,128)} %v_ref.7) | copy-start | bytes 393220
  24.1 5.1 %collective-permute-start = (f32[6,16,128]{2,1,0:T(8,128)S(1)}, f32[6,16,128]{2,1,0:T(8,128)S(1)}, u32[]{:S(2)}, u32[]{:S(2)}) collective-permute-start(f32[6,16,128]{2,1,0:T(8,128)S(1)} %get-tuple-element.12), channel_id=1, source_target_pairs={{0,32},{32,64},{64,96},{96,128},{128,160},{160,192},{192,224},{224... | collective-permute-start | bytes 147464 | tf_op jit(solution)/shard_map/ppermute | solution.py:30
  24.6 4.6 %collective-permute-start.1 = (f32[6,16,128]{2,1,0:T(8,128)S(1)}, f32[6,16,128]{2,1,0:T(8,128)S(1)}, u32[]{:S(2)}, u32[]{:S(2)}) collective-permute-start(f32[6,16,128]{2,1,0:T(8,128)S(1)} %get-tuple-element.13), channel_id=1, source_target_pairs={{0,224},{32,0},{64,32},{96,64},{128,96},{160,128},{192,160},{224,1... | collective-permute-start | bytes 147464 | tf_op jit(solution)/shard_map/ppermute | solution.py:30
  29.3 26.9 %collective-permute-start.2 = (f32[22,8,128]{2,1,0:T(8,128)S(1)}, f32[22,8,128]{2,1,0:T(8,128)S(1)}, u32[]{:S(2)}, u32[]{:S(2)}) collective-permute-start(f32[22,8,128]{2,1,0:T(8,128)S(1)} %get-tuple-element.14), channel_id=1, source_target_pairs={{0,4},{4,8},{8,12},{12,16},{16,20},{20,24},{24,28},{28,0},{1,5},{5... | collective-permute-start | bytes 270344 | tf_op jit(solution)/shard_map/ppermute | solution.py:30
  35.2 21.0 %collective-permute-start.3 = (f32[22,8,128]{2,1,0:T(8,128)S(1)}, f32[22,8,128]{2,1,0:T(8,128)S(1)}, u32[]{:S(2)}, u32[]{:S(2)}) collective-permute-start(f32[22,8,128]{2,1,0:T(8,128)S(1)} %get-tuple-element.15), channel_id=1, source_target_pairs={{0,28},{4,0},{8,4},{12,8},{16,12},{20,16},{24,20},{28,24},{1,29},{... | collective-permute-start | bytes 270344 | tf_op jit(solution)/shard_map/ppermute | solution.py:30
  56.4 6.9 %collective-permute-start.4 = (f32[56,128]{1,0:T(8,128)S(1)}, f32[56,128]{1,0:T(8,128)S(1)}, u32[]{:S(2)}, u32[]{:S(2)}) collective-permute-start(f32[56,128]{1,0:T(8,128)S(1)} %get-tuple-element.17), channel_id=1, source_target_pairs={{0,1},{1,2},{2,3},{3,0},{4,5},{5,6},{6,7},{7,4},{8,9},{9,10},{10,1... | collective-permute-start | bytes 86024 | tf_op jit(solution)/shard_map/ppermute | solution.py:30
  57.8 5.5 %collective-permute-start.5 = (f32[56,128]{1,0:T(8,128)S(1)}, f32[56,128]{1,0:T(8,128)S(1)}, u32[]{:S(2)}, u32[]{:S(2)}) collective-permute-start(f32[56,128]{1,0:T(8,128)S(1)} %get-tuple-element.18), channel_id=1, source_target_pairs={{0,3},{1,0},{2,1},{3,2},{4,7},{5,4},{6,5},{7,6},{8,11},{9,8},{10,9... | collective-permute-start | bytes 86024 | tf_op jit(solution)/shard_map/ppermute | solution.py:30
  59.3 4.0 %collective-permute-start.6 = (f32[8,128]{1,0:T(8,128)S(1)}, f32[8,128]{1,0:T(8,128)S(1)}, u32[]{:S(2)}, u32[]{:S(2)}) collective-permute-start(f32[8,128]{1,0:T(8,128)S(1)} %get-tuple-element.19.own_ref), channel_id=1, source_target_pairs={{0,2},{1,3},{2,0},{3,1},{4,6},{5,7},{6,4},{7,5},{8,10},{9,11},{10,... | collective-permute-start | bytes 12296 | tf_op jit(solution)/shard_map/ppermute | solution.py:30

commit v3 on v2

--- a/solution.py
+++ b/solution.py
@@ -10,8 +10,7 @@
 HALO = ITERS
 GX = ("gx_0", "gx_1")
 GY = ("gy_0", "gy_1")
-XY = GX + GY
-ALL = XY + ("gz",)
+ALL = GX + GY + ("gz",)
 
 step_length = 0.5
 tv_weight = 0.2
@@ -169,14 +168,14 @@
     return jnp.where(low, pltpu.roll(after, 4, 0), before)
 
 
-def pack_z(gradient, velocity, before_x, after_x, before_y, after_y, squares):
+def pack_z(gradient, velocity, before_x, after_x, before_y, after_y):
     bx, by, bz = velocity.shape
     planes = bx + 2 * HALO
     pairs = planes // 2
     groups = bz // 4
     tall = by + 8
 
-    def kernel(g_ref, v_ref, bx_ref, ax_ref, by_ref, ay_ref, sq_ref, first_ref, last_ref, sum_ref):
+    def kernel(g_ref, v_ref, bx_ref, ax_ref, by_ref, ay_ref, first_ref, last_ref):
         group = lane((tall, bz)) // 4
         for field, main in enumerate((g_ref, v_ref)):
             first = jnp.zeros((tall, bz), F32)
@@ -190,23 +189,19 @@
                 last = jnp.where(group == (p - 1) % groups, turned, last)
             first_ref[pl.ds(field * tall, tall)] = first
             last_ref[pl.ds(field * tall, tall)] = last
-        total = jnp.broadcast_to(jnp.sum(sq_ref[...], axis=0), (8, bz))
-        first_ref[pl.ds(2 * tall, 8)] = total
-        last_ref[pl.ds(2 * tall, 8)] = total
-        sum_ref[...] = total
-
-    edge = struct(2 * tall + 8, bz)
+
+    edge = struct(2 * tall, bz)
     return pl.pallas_call(
         kernel,
         name="pack_z",
         compiler_params=PARAMS,
-        out_shape=(edge, edge, struct(8, bz)),
-        in_specs=[VMEM] * 7,
-        out_specs=(VMEM,) * 3,
-    )(gradient, velocity, before_x, after_x, before_y, after_y, squares)
-
-
-def proximal(device, gradient, velocity, halos, sums, sizes):
+        out_shape=(edge, edge),
+        in_specs=[VMEM] * 6,
+        out_specs=(VMEM,) * 2,
+    )(gradient, velocity, before_x, after_x, before_y, after_y)
+
+
+def proximal(device, gradient, velocity, halos, squares, sizes):
     bx, by, bz = velocity.shape
     planes = bx + 2 * HALO
     pairs = planes // 2
@@ -225,8 +220,7 @@
         ay_ref,
         bz_ref,
         az_ref,
-        own_ref,
-        far_ref,
+        sq_ref,
         gradient_ref,
         model_ref,
         target,
@@ -245,9 +239,7 @@
         pos_y = (dev // size_z) % size_y
         pos_x = dev // (size_z * size_y)
 
-        total = own_ref[0:1] + far_ref[0:1]
-        total = total + bz_ref[2 * tall : 2 * tall + 1] + az_ref[2 * tall : 2 * tall + 1]
-        total = jnp.sum(total, axis=1, keepdims=True)
+        total = jnp.sum(jnp.sum(sq_ref[...], axis=0), axis=1, keepdims=True)
         scale = step_length * lax.rsqrt(total / cells + 1.0)
         scale = jnp.broadcast_to(scale, (1, bz))
 
@@ -339,10 +331,10 @@
         name="proximal",
         compiler_params=PARAMS,
         out_shape=(struct(bx, by, bz),) * 2,
-        in_specs=[SMEM] + [VMEM] * 10,
+        in_specs=[SMEM] + [VMEM] * 9,
         out_specs=(HBM,) * 2,
         scratch_shapes=[field] * 6 + [pltpu.VMEM((bx, by, bz), F32), pltpu.SemaphoreType.DMA((2,))],
-    )(device, gradient, velocity, *halos, *sums)
+    )(device, gradient, velocity, *halos, squares)
 
 
 def shards(partials, code_bits, group_map, velocity):
@@ -357,23 +349,23 @@
 
     after_x = shift(first_x, GX, -1)
     before_x = shift(last_x, GX, 1)
-    table = jnp.broadcast_to(squares[:1][None], (size_x * size_y, 1, bz))
-    table = lax.all_to_all(table, XY, split_axis=0, concat_axis=0, tiled=True)
+    table = jnp.broadcast_to(squares[:1][None], (size_x * size_y * size_z, 1, bz))
+    table = lax.all_to_all(table, ALL, split_axis=0, concat_axis=0, tiled=True)
 
     first_y, last_y = pack_y(gradient, velocity, before_x, after_x)
     after_y = shift(first_y, GY, -1)
     before_y = shift(last_y, GY, 1)
 
-    first_z, last_z, own = pack_z(gradient, velocity, before_x, after_x, before_y, after_y, table)
+    first_z, last_z = pack_z(gradient, velocity, before_x, after_x, before_y, after_y)
     after_z = shift(first_z, "gz", -1)
     before_z = shift(last_z, "gz", 1)
-    far = shift(own, "gz", 2)
+
     return proximal(
         device,
         gradient,
         velocity,
         (before_x, after_x, before_y, after_y, before_z, after_z),
-        (own, far),
+        table,
         (size_x, size_y, size_z),
     )
 

time: 68.1 us -> 61.8 us (0.907)
  blocking collectives: 41.9 us -> 21 us
  starting transfers between devices: 14 us -> 23.5 us
  waiting for transfers between devices: 3.89 us -> 10.1 us
  Pallas kernels: 7.37 us -> 5.28 us
  local copies, waits for them, and re-layouts: 0.03 us -> 0.73 us
    all_to_all x1 -> x0, blocking collectives: 21 us -> none  [shards(): table = lax.all_to_all(table, XY, split_axis=0, concat_axis=0, tiled=True)]
    all_to_all x0 -> x1, starting transfers between devices: none -> 13.2 us  [shards(): table = lax.all_to_all(table, ALL, split_axis=0, concat_axis=0, tiled=True)]
    ppermute x7 -> x6, waiting for transfers between devices: 3.89 us -> 10.1 us  [shift(): lax.ppermute(block, axis, [(i, (i + distance) % size) for i in range(size)])]
    ppermute x7 -> x6, starting transfers between devices: 14 us -> 10.3 us  [shift(): lax.ppermute(block, axis, [(i, (i + distance) % size) for i in range(size)])]
    pallas_call x1, Pallas kernels: 4.66 us -> 2.57 us  [proximal(): pl.pallas_call(kernel, name='proximal', compiler_params=PARAMS, out_shape...]
    broadcast_in_dim x2, local copies, waits for them, and re-layouts: 0.02 us -> 0.73 us  [shards(): jnp.broadcast_to(squares[:1][None], (size_x * size_y * size_z, 1, bz))]
  transfers between devices with their start and end apart: 7 -> 7, of which waited for: 2 -> 4; matrix products, arithmetic and copies ran while one was open for 0% -> 0% of each run, Pallas kernels for 0% -> 0%
where the time goes in v3:
time: 61.8 us; the launch traced here: 61.2 us
  starting transfers between devices  23.5 us (38%)
  blocking collectives  21 us (34%)
  waiting for transfers between devices  10.1 us (16%)
  Pallas kernels  5.28 us (9%)
  local copies, waits for them, and re-layouts  0.73 us (1%)
  between operations  0.69 us (1%)
    all_to_all x1, blocking collectives, shards(): parts = lax.all_to_all(local, GX, split_axis=0, concat_axis=0, tiled=True)  21 us
    all_to_all x1, starting transfers between devices, shards(): table = lax.all_to_all(table, ALL, split_axis=0, concat_axis=0, tiled=True)  13.2 us
    ppermute x6, starting transfers between devices, shift(): lax.ppermute(block, axis, [(i, (i + distance) % size) for i in range(size)])  10.3 us
    ppermute x6, waiting for transfers between devices, shift(): lax.ppermute(block, axis, [(i, (i + distance) % size) for i in range(size)])  10.1 us
    pallas_call x1, Pallas kernels, proximal(): pl.pallas_call(kernel, name='proximal', compiler_params=PARAMS, out_shape...  2.57 us
    pallas_call x1, Pallas kernels, presum(): pl.pallas_call(kernel, name='presum', compiler_params=PARAMS, out_shape=s...  2.42 us
  transfers between devices with their start and end apart: 7, of which 4 were waited for; matrix products, arithmetic and copies ran while one was open for 0% of the time, Pallas kernels for 0%

profile of v3, /device:TPU:1, one launch (start us, length us, event | category | flops | bytes accessed | tf_op | source)
XLA Modules:
  0.0 61.2 jit_solution(4507547640888758604)
XLA Ops:
  0.6 0.0 copy-start
  0.7 2.4 %presum.1 = f32[128,16,128]{2,1,0:T(8,128)S(1)} custom-call(s32[1]{0:T(128)} %bitcast.1.base_ref, s32[32]{0:T(128)} %map_hbm.1, s32[32,128]{1,0:T(8,128)} %bits_hbm.1, f32[4,128,16,128]{3,2,1,0:T(8,128)} %part_ref.1), custom_call_target="tpu_custom_call" | custom-call | tf_op jit(solution)/shard_map/presum/pallas_call | solution.py:74
  3.1 21.0 %all_to_all.10.part_ref = f32[128,16,128]{2,1,0:T(8,128)S(1)} all-to-all(f32[128,16,128]{2,1,0:T(8,128)S(1)} %presum.1), channel_id=1, replica_groups=mesh['gx_0'=4,'gx_1'=2,'gy_0'=4,'gy_1'=2,'gz'=4] {'gx_0','gx_1'}, dimensions={0} | all-to-all | bytes 2097152 | tf_op jit(solution)/shard_map/all_to_all | solution.py:347
  24.0 0.0 copy-done
  24.1 0.1 reduce_pack.1
  24.1 0.7 %broadcast_in_dim.9 = f32[256,1,128]{2,1,0:T(1,128)} broadcast(f32[128]{0:T(128)S(1)} %slice_bitcast_fusion), dimensions={2} | broadcast | bytes 131584 | tf_op jit(solution)/shard_map/broadcast_in_dim | solution.py:352
  24.8 13.2 %all-to-all-start.1 = ((f32[256,1,128]{2,1,0:T(1,128)}), f32[256,1,128]{2,1,0:T(1,128)S(1)}, u32[]{:S(2)}, u32[]{:S(2)}) async-start(f32[256,1,128]{2,1,0:T(1,128)} %broadcast_in_dim.9), calls=%async_computation.1 | async-start | bytes 262144 | tf_op jit(solution)/shard_map/all_to_all | solution.py:353
  38.0 1.6 %collective-permute-start = (f32[6,16,128]{2,1,0:T(8,128)S(1)}, f32[6,16,128]{2,1,0:T(8,128)S(1)}, u32[]{:S(2)}, u32[]{:S(2)}) collective-permute-start(f32[6,16,128]{2,1,0:T(8,128)S(1)} %get-tuple-element.11), channel_id=1, source_target_pairs={{0,32},{32,64},{64,96},{96,128},{128,160},{160,192},{192,224},{224... | collective-permute-start | bytes 147464 | tf_op jit(solution)/shard_map/ppermute | solution.py:29
  39.6 2.2 %collective-permute-start.1 = (f32[6,16,128]{2,1,0:T(8,128)S(1)}, f32[6,16,128]{2,1,0:T(8,128)S(1)}, u32[]{:S(2)}, u32[]{:S(2)}) collective-permute-start(f32[6,16,128]{2,1,0:T(8,128)S(1)} %get-tuple-element.12), channel_id=1, source_target_pairs={{0,224},{32,0},{64,32},{96,64},{128,96},{160,128},{192,160},{224,1... | collective-permute-start | bytes 147464 | tf_op jit(solution)/shard_map/ppermute | solution.py:29
  41.8 2.8 %collective-permute-done.before_ref.bx_ref = f32[6,16,128]{2,1,0:T(8,128)S(1)} collective-permute-done((f32[6,16,128]{2,1,0:T(8,128)S(1)}, f32[6,16,128]{2,1,0:T(8,128)S(1)}, u32[]{:S(2)}, u32[]{:S(2)}) %collective-permute-start) | collective-permute-done | bytes 49184 | tf_op jit(solution)/shard_map/ppermute | solution.py:29
  44.6 0.0 collective-permute-done.1.after_ref.ax_ref
  44.6 3.7 %collective-permute-start.2 = (f32[22,8,128]{2,1,0:T(8,128)S(1)}, f32[22,8,128]{2,1,0:T(8,128)S(1)}, u32[]{:S(2)}, u32[]{:S(2)}) collective-permute-start(f32[22,8,128]{2,1,0:T(8,128)S(1)} %get-tuple-element.13), channel_id=1, source_target_pairs={{0,4},{4,8},{8,12},{12,16},{16,20},{20,24},{24,28},{28,0},{1,5},{5... | collective-permute-start | bytes 270344 | tf_op jit(solution)/shard_map/ppermute | solution.py:29
  48.4 0.0 collective-permute-start.3
  48.4 1.6 %collective-permute-done.2.by_ref = f32[22,8,128]{2,1,0:T(8,128)S(1)} collective-permute-done((f32[22,8,128]{2,1,0:T(8,128)S(1)}, f32[22,8,128]{2,1,0:T(8,128)S(1)}, u32[]{:S(2)}, u32[]{:S(2)}) %collective-permute-start.2) | collective-permute-done | bytes 90144 | tf_op jit(solution)/shard_map/ppermute | solution.py:29
  49.9 4.3 %collective-permute-done.3.ay_ref = f32[22,8,128]{2,1,0:T(8,128)S(1)} collective-permute-done((f32[22,8,128]{2,1,0:T(8,128)S(1)}, f32[22,8,128]{2,1,0:T(8,128)S(1)}, u32[]{:S(2)}, u32[]{:S(2)}) %collective-permute-start.3) | collective-permute-done | bytes 90144 | tf_op jit(solution)/shard_map/ppermute | solution.py:29
  54.2 0.2 pack_z.1
  54.4 1.4 %collective-permute-start.4 = (f32[48,128]{1,0:T(8,128)S(1)}, f32[48,128]{1,0:T(8,128)S(1)}, u32[]{:S(2)}, u32[]{:S(2)}) collective-permute-start(f32[48,128]{1,0:T(8,128)S(1)} %get-tuple-element.15), channel_id=1, source_target_pairs={{0,1},{1,2},{2,3},{3,0},{4,5},{5,6},{6,7},{7,4},{8,9},{9,10},{10,1... | collective-permute-start | bytes 73736 | tf_op jit(solution)/shard_map/ppermute | solution.py:29
  55.8 1.3 %collective-permute-start.5 = (f32[48,128]{1,0:T(8,128)S(1)}, f32[48,128]{1,0:T(8,128)S(1)}, u32[]{:S(2)}, u32[]{:S(2)}) collective-permute-start(f32[48,128]{1,0:T(8,128)S(1)} %get-tuple-element.16), channel_id=1, source_target_pairs={{0,3},{1,0},{2,1},{3,2},{4,7},{5,4},{6,5},{7,6},{8,11},{9,8},{10,9... | collective-permute-start | bytes 73736 | tf_op jit(solution)/shard_map/ppermute | solution.py:29
  57.2 1.5 %collective-permute-done.4.bz_ref = f32[48,128]{1,0:T(8,128)S(1)} collective-permute-done((f32[48,128]{1,0:T(8,128)S(1)}, f32[48,128]{1,0:T(8,128)S(1)}, u32[]{:S(2)}, u32[]{:S(2)}) %collective-permute-start.4) | collective-permute-done | bytes 24608 | tf_op jit(solution)/shard_map/ppermute | solution.py:29
  58.6 0.0 collective-permute-done.5.az_ref
  58.6 0.0 all-to-all-done.1.sq_ref
  58.6 2.6 %proximal.1 = (f32[16,16,128]{2,1,0:T(8,128)}, f32[16,16,128]{2,1,0:T(8,128)}) custom-call(s32[1]{0:T(128)} %bitcast.dev_ref, f32[16,16,128]{2,1,0:T(8,128)S(1)} %get-tuple-element.10.g_ref, f32[16,16,128]{2,1,0:T(8,128)S(1)} %copy-done, f32[6,16,128]{2,1,0:T(8,128)S(1)} %collective-permute-done.before_ref.bx_ref, ...), custom_call_target="tpu_custom_call" | custom-call | tf_op jit(solution)/shard_map/proximal/pallas_call | solution.py:329
  (2 shorter events, 0.0 us)
Async XLA Ops:
  0.6 23.4 %copy-start = (f32[16,16,128]{2,1,0:T(8,128)S(1)}, f32[16,16,128]{2,1,0:T(8,128)}, u32[]{:S(2)}) copy-start(f32[16,16,128]{2,1,0:T(8,128)} %v_ref.7) | copy-start | bytes 393220
  24.8 33.8 %all-to-all-start.1 = ((f32[256,1,128]{2,1,0:T(1,128)}), f32[256,1,128]{2,1,0:T(1,128)S(1)}, u32[]{:S(2)}, u32[]{:S(2)}) async-start(f32[256,1,128]{2,1,0:T(1,128)} %broadcast_in_dim.9), calls=%async_computation.1 | async-start | bytes 262144 | tf_op jit(solution)/shard_map/all_to_all | solution.py:353
  38.0 6.6 %collective-permute-start = (f32[6,16,128]{2,1,0:T(8,128)S(1)}, f32[6,16,128]{2,1,0:T(8,128)S(1)}, u32[]{:S(2)}, u32[]{:S(2)}) collective-permute-start(f32[6,16,128]{2,1,0:T(8,128)S(1)} %get-tuple-element.11), channel_id=1, source_target_pairs={{0,32},{32,64},{64,96},{96,128},{128,160},{160,192},{192,224},{224... | collective-permute-start | bytes 147464 | tf_op jit(solution)/shard_map/ppermute | solution.py:29
  39.6 5.0 %collective-permute-start.1 = (f32[6,16,128]{2,1,0:T(8,128)S(1)}, f32[6,16,128]{2,1,0:T(8,128)S(1)}, u32[]{:S(2)}, u32[]{:S(2)}) collective-permute-start(f32[6,16,128]{2,1,0:T(8,128)S(1)} %get-tuple-element.12), channel_id=1, source_target_pairs={{0,224},{32,0},{64,32},{96,64},{128,96},{160,128},{192,160},{224,1... | collective-permute-start | bytes 147464 | tf_op jit(solution)/shard_map/ppermute | solution.py:29
  44.6 5.3 %collective-permute-start.2 = (f32[22,8,128]{2,1,0:T(8,128)S(1)}, f32[22,8,128]{2,1,0:T(8,128)S(1)}, u32[]{:S(2)}, u32[]{:S(2)}) collective-permute-start(f32[22,8,128]{2,1,0:T(8,128)S(1)} %get-tuple-element.13), channel_id=1, source_target_pairs={{0,4},{4,8},{8,12},{12,16},{16,20},{20,24},{24,28},{28,0},{1,5},{5... | collective-permute-start | bytes 270344 | tf_op jit(solution)/shard_map/ppermute | solution.py:29
  48.4 5.8 %collective-permute-start.3 = (f32[22,8,128]{2,1,0:T(8,128)S(1)}, f32[22,8,128]{2,1,0:T(8,128)S(1)}, u32[]{:S(2)}, u32[]{:S(2)}) collective-permute-start(f32[22,8,128]{2,1,0:T(8,128)S(1)} %get-tuple-element.14), channel_id=1, source_target_pairs={{0,28},{4,0},{8,4},{12,8},{16,12},{20,16},{24,20},{28,24},{1,29},{... | collective-permute-start | bytes 270344 | tf_op jit(solution)/shard_map/ppermute | solution.py:29
  54.4 4.2 %collective-permute-start.4 = (f32[48,128]{1,0:T(8,128)S(1)}, f32[48,128]{1,0:T(8,128)S(1)}, u32[]{:S(2)}, u32[]{:S(2)}) collective-permute-start(f32[48,128]{1,0:T(8,128)S(1)} %get-tuple-element.15), channel_id=1, source_target_pairs={{0,1},{1,2},{2,3},{3,0},{4,5},{5,6},{6,7},{7,4},{8,9},{9,10},{10,1... | collective-permute-start | bytes 73736 | tf_op jit(solution)/shard_map/ppermute | solution.py:29
  55.8 2.8 %collective-permute-start.5 = (f32[48,128]{1,0:T(8,128)S(1)}, f32[48,128]{1,0:T(8,128)S(1)}, u32[]{:S(2)}, u32[]{:S(2)}) collective-permute-start(f32[48,128]{1,0:T(8,128)S(1)} %get-tuple-element.16), channel_id=1, source_target_pairs={{0,3},{1,0},{2,1},{3,2},{4,7},{5,4},{6,5},{7,6},{8,11},{9,8},{10,9... | collective-permute-start | bytes 73736 | tf_op jit(solution)/shard_map/ppermute | solution.py:29

commit v4 on v3

--- a/solution.py
+++ b/solution.py
@@ -11,6 +11,7 @@
 GX = ("gx_0", "gx_1")
 GY = ("gy_0", "gy_1")
 ALL = GX + GY + ("gz",)
+REST = GX[:1] + GY + ("gz",)
 
 step_length = 0.5
 tv_weight = 0.2
@@ -99,14 +100,17 @@
             g_ref[i] = total
             squares = squares + total * total
             if i < HALO:
-                first_ref[i] = total
-                first_ref[HALO + i] = v_ref[i]
+                first_ref[pl.ds(i * by, by)] = total
+                first_ref[pl.ds((HALO + i) * by, by)] = v_ref[i]
             if i >= bx - HALO:
-                last_ref[i - bx + HALO] = total
-                last_ref[i - bx + 2 * HALO] = v_ref[i]
-        square_ref[...] = jnp.broadcast_to(jnp.sum(squares, axis=0, keepdims=True), (8, bz))
-
-    edge = struct(2 * HALO, by, bz)
+                last_ref[pl.ds((i - bx + HALO) * by, by)] = total
+                last_ref[pl.ds((i - bx + 2 * HALO) * by, by)] = v_ref[i]
+        row = jnp.broadcast_to(jnp.sum(squares, axis=0, keepdims=True), (8, bz))
+        square_ref[...] = row
+        first_ref[pl.ds(2 * HALO * by, 8)] = row
+        last_ref[pl.ds(2 * HALO * by, 8)] = row
+
+    edge = struct(2 * HALO * by + 8, bz)
     return pl.pallas_call(
         kernel,
         name="reduce_pack",
@@ -117,12 +121,13 @@
     )(parts, velocity)
 
 
-def plane_of(main_ref, before_ref, after_ref, field, p, bx):
+def plane_of(main_ref, before_ref, after_ref, field, p):
+    bx, by, _ = main_ref.shape
     if p < HALO:
-        return before_ref[field * HALO + p]
+        return before_ref[pl.ds((field * HALO + p) * by, by)]
     if p < HALO + bx:
         return main_ref[p - HALO]
-    return after_ref[field * HALO + p - HALO - bx]
+    return after_ref[pl.ds((field * HALO + p - HALO - bx) * by, by)]
 
 
 def sublane(shape):
@@ -133,16 +138,24 @@
     return lax.broadcasted_iota(jnp.int32, shape, len(shape) - 1)
 
 
-def pack_y(gradient, velocity, before_x, after_x):
+def pack_y(device, gradient, velocity, before_x, after_x, squares, sizes):
     bx, by, bz = velocity.shape
     pairs = (bx + 2 * HALO) // 2
-
-    def kernel(g_ref, v_ref, before_ref, after_ref, first_ref, last_ref):
+    size_x, size_y, size_z = sizes
+    receivers = size_x // 2 * size_y * size_z
+
+    def kernel(
+        dev_ref, g_ref, v_ref, before_ref, after_ref, sq_ref, first_ref, last_ref, table_ref
+    ):
+        even_x = (dev_ref[0] // (size_y * size_z)) % 2 == 0
+        where = pl.ds(2 * HALO * by, 8)
+        row = sq_ref[...] + jnp.where(even_x, after_ref[where], before_ref[where])
+        table_ref[...] = jnp.broadcast_to(row[:1][None], table_ref.shape)
         low = sublane((8, bz)) < 4
         for field, main in enumerate((g_ref, v_ref)):
             for q in range(pairs):
-                even = plane_of(main, before_ref, after_ref, field, 2 * q, bx)
-                odd = plane_of(main, before_ref, after_ref, field, 2 * q + 1, bx)
+                even = plane_of(main, before_ref, after_ref, field, 2 * q)
+                odd = plane_of(main, before_ref, after_ref, field, 2 * q + 1)
                 first_ref[field * pairs + q] = jnp.where(low, even[:8], pltpu.roll(odd[:8], 4, 0))
                 last_ref[field * pairs + q] = jnp.where(
                     low, pltpu.roll(even[by - 8 :], 4, 0), odd[by - 8 :]
@@ -153,10 +166,10 @@
         kernel,
         name="pack_y",
         compiler_params=PARAMS,
-        out_shape=(edge, edge),
-        in_specs=[VMEM] * 4,
-        out_specs=(VMEM,) * 2,
-    )(gradient, velocity, before_x, after_x)
+        out_shape=(edge, edge, struct(receivers, 1, bz)),
+        in_specs=[SMEM] + [VMEM] * 5,
+        out_specs=(VMEM,) * 3,
+    )(device, gradient, velocity, before_x, after_x, squares)
 
 
 def rows_of(before_ref, after_ref, field, p, pairs):
@@ -181,7 +194,7 @@
             first = jnp.zeros((tall, bz), F32)
             last = jnp.zeros((tall, bz), F32)
             for p in range(planes):
-                own = plane_of(main, bx_ref, ax_ref, field, p, bx)
+                own = plane_of(main, bx_ref, ax_ref, field, p)
                 extra = rows_of(by_ref, ay_ref, field, p, pairs)
                 plane = jnp.concatenate([own, extra], 0)
                 turned = pltpu.roll(plane, 4 * p, 1) if p else plane
@@ -247,9 +260,7 @@
         before_z = bz_ref[pl.ds(tall, tall)] - scale * bz_ref[pl.ds(0, tall)]
         after_z = az_ref[pl.ds(tall, tall)] - scale * az_ref[pl.ds(0, tall)]
         for p in range(planes):
-            own = plane_of(v_ref, bx_ref, ax_ref, 1, p, bx) - scale * plane_of(
-                g_ref, bx_ref, ax_ref, 0, p, bx
-            )
+            own = plane_of(v_ref, bx_ref, ax_ref, 1, p) - scale * plane_of(g_ref, bx_ref, ax_ref, 0, p)
             rows = rows_of(by_ref, ay_ref, 1, p, pairs) - scale * rows_of(
                 by_ref, ay_ref, 0, p, pairs
             )
@@ -338,23 +349,20 @@
 
 
 def shards(partials, code_bits, group_map, velocity):
-    _, _, bz = velocity.shape
-    size_x, size_y, size_z = (lax.axis_size(axis) for axis in (GX, GY, "gz"))
+    sizes = tuple(lax.axis_size(axis) for axis in (GX, GY, "gz"))
     base = (lax.axis_index(GX) * partials.shape[0]).astype(jnp.int32).reshape(1)
     device = lax.axis_index(ALL).astype(jnp.int32).reshape(1)
 
     local = presum(partials, code_bits, group_map, base, 8)
     parts = lax.all_to_all(local, GX, split_axis=0, concat_axis=0, tiled=True)
-    gradient, first_x, last_x, squares = reduce_pack(parts, velocity, size_x)
+    gradient, first_x, last_x, squares = reduce_pack(parts, velocity, sizes[0])
 
     after_x = shift(first_x, GX, -1)
     before_x = shift(last_x, GX, 1)
-    table = jnp.broadcast_to(squares[:1][None], (size_x * size_y * size_z, 1, bz))
-    table = lax.all_to_all(table, ALL, split_axis=0, concat_axis=0, tiled=True)
-
-    first_y, last_y = pack_y(gradient, velocity, before_x, after_x)
+    first_y, last_y, table = pack_y(device, gradient, velocity, before_x, after_x, squares, sizes)
     after_y = shift(first_y, GY, -1)
     before_y = shift(last_y, GY, 1)
+    table = lax.all_to_all(table, REST, split_axis=0, concat_axis=0, tiled=True)
 
     first_z, last_z = pack_z(gradient, velocity, before_x, after_x, before_y, after_y)
     after_z = shift(first_z, "gz", -1)
@@ -366,7 +374,7 @@
         velocity,
         (before_x, after_x, before_y, after_y, before_z, after_z),
         table,
-        (size_x, size_y, size_z),
+        sizes,
     )
 
 

time: 61.8 us -> 62.8 us (1.016)
  the two profiles are of different devices: /device:TPU:1 before, /device:TPU:103 now
where the time goes in v4:
time: 62.8 us; the launch traced here: 62.7 us
  starting transfers between devices  25.3 us (40%)
  blocking collectives  17.9 us (29%)
  waiting for transfers between devices  12.4 us (20%)
  Pallas kernels  6.45 us (10%)
  between operations  0.68 us (1%)
    all_to_all x1, blocking collectives, shards(): parts = lax.all_to_all(local, GX, split_axis=0, concat_axis=0, tiled=True)  17.9 us
    all_to_all x1, starting transfers between devices, shards(): table = lax.all_to_all(table, REST, split_axis=0, concat_axis=0, tiled=True)  16.8 us
    ppermute x6, waiting for transfers between devices, shift(): lax.ppermute(block, axis, [(i, (i + distance) % size) for i in range(size)])  12.4 us
    ppermute x6, starting transfers between devices, shift(): lax.ppermute(block, axis, [(i, (i + distance) % size) for i in range(size)])  8.52 us
    pallas_call x1, Pallas kernels, proximal(): pl.pallas_call(kernel, name='proximal', compiler_params=PARAMS, out_shape...  3.08 us
    pallas_call x1, Pallas kernels, presum(): pl.pallas_call(kernel, name='presum', compiler_params=PARAMS, out_shape=s...  2.42 us
  transfers between devices with their start and end apart: 7, of which 5 were waited for; matrix products, arithmetic and copies ran while one was open for 0% of the time, Pallas kernels for 0%

profile of v4, /device:TPU:103, one launch (start us, length us, event | category | flops | bytes accessed | tf_op | source)
XLA Modules:
  0.0 62.7 jit_solution(2816395092911329841)
XLA Ops:
  0.6 0.0 copy-start
  0.7 2.4 %presum.1 = f32[128,16,128]{2,1,0:T(8,128)S(1)} custom-call(s32[1]{0:T(128)} %bitcast.1.base_ref, s32[32]{0:T(128)} %map_hbm.1, s32[32,128]{1,0:T(8,128)} %bits_hbm.1, f32[4,128,16,128]{3,2,1,0:T(8,128)} %part_ref.1), custom_call_target="tpu_custom_call" | custom-call | tf_op jit(solution)/shard_map/presum/pallas_call | solution.py:75
  3.1 17.9 %all_to_all.10.part_ref = f32[128,16,128]{2,1,0:T(8,128)S(1)} all-to-all(f32[128,16,128]{2,1,0:T(8,128)S(1)} %presum.1), channel_id=1, replica_groups=mesh['gx_0'=4,'gx_1'=2,'gy_0'=4,'gy_1'=2,'gz'=4] {'gx_0','gx_1'}, dimensions={0} | all-to-all | bytes 2097152 | tf_op jit(solution)/shard_map/all_to_all | solution.py:357
  21.0 0.0 copy-done
  21.0 0.1 reduce_pack.1
  21.0 2.1 %collective-permute-start = (f32[104,128]{1,0:T(8,128)S(1)}, f32[104,128]{1,0:T(8,128)S(1)}, u32[]{:S(2)}, u32[]{:S(2)}) collective-permute-start(f32[104,128]{1,0:T(8,128)S(1)} %get-tuple-element.12), channel_id=1, source_target_pairs={{0,32},{32,64},{64,96},{96,128},{128,160},{160,192},{192,224},{224... | collective-permute-start | bytes 159752 | tf_op jit(solution)/shard_map/ppermute | solution.py:30
  23.1 0.0 collective-permute-start.1
  23.1 1.2 %collective-permute-done.before_ref.bx_ref = f32[104,128]{1,0:T(8,128)S(1)} collective-permute-done((f32[104,128]{1,0:T(8,128)S(1)}, f32[104,128]{1,0:T(8,128)S(1)}, u32[]{:S(2)}, u32[]{:S(2)}) %collective-permute-start) | collective-permute-done | bytes 53280 | tf_op jit(solution)/shard_map/ppermute | solution.py:30
  24.3 3.9 %collective-permute-done.1.after_ref.ax_ref = f32[104,128]{1,0:T(8,128)S(1)} collective-permute-done((f32[104,128]{1,0:T(8,128)S(1)}, f32[104,128]{1,0:T(8,128)S(1)}, u32[]{:S(2)}, u32[]{:S(2)}) %collective-permute-start.1) | collective-permute-done | bytes 53280 | tf_op jit(solution)/shard_map/ppermute | solution.py:30
  28.2 0.7 %pack_y.1 = (f32[22,8,128]{2,1,0:T(8,128)S(1)}, f32[22,8,128]{2,1,0:T(8,128)S(1)}, f32[128,1,128]{2,1,0:T(1,128)}) custom-call(s32[1]{0:T(128)} %bitcast.dev_ref, f32[16,16,128]{2,1,0:T(8,128)S(1)} %get-tuple-element.11.g_ref, f32[16,16,128]{2,1,0:T(8,128)S(1)} %copy-done, f32[104,128]{1,0:T(8,128)S(1)} %collective-permute-done.before_ref.bx_ref, ...), custom_call_target="tpu_custom_call" | custom-call | tf_op jit(solution)/shard_map/pack_y/pallas_call | solution.py:165
  28.9 16.8 %all-to-all-start.1 = ((f32[128,1,128]{2,1,0:T(1,128)}), f32[128,1,128]{2,1,0:T(1,128)S(1)}, u32[]{:S(2)}, u32[]{:S(2)}) async-start(f32[128,1,128]{2,1,0:T(1,128)} %get-tuple-element.19), calls=%async_computation.1 | async-start | bytes 131072 | tf_op jit(solution)/shard_map/all_to_all | solution.py:365
  45.7 3.7 %collective-permute-start.2 = (f32[22,8,128]{2,1,0:T(8,128)S(1)}, f32[22,8,128]{2,1,0:T(8,128)S(1)}, u32[]{:S(2)}, u32[]{:S(2)}) collective-permute-start(f32[22,8,128]{2,1,0:T(8,128)S(1)} %get-tuple-element.15), channel_id=1, source_target_pairs={{0,4},{4,8},{8,12},{12,16},{16,20},{20,24},{24,28},{28,0},{1,5},{5... | collective-permute-start | bytes 270344 | tf_op jit(solution)/shard_map/ppermute | solution.py:30
  49.3 0.0 collective-permute-start.3
  49.3 1.6 %collective-permute-done.2.by_ref = f32[22,8,128]{2,1,0:T(8,128)S(1)} collective-permute-done((f32[22,8,128]{2,1,0:T(8,128)S(1)}, f32[22,8,128]{2,1,0:T(8,128)S(1)}, u32[]{:S(2)}, u32[]{:S(2)}) %collective-permute-start.2) | collective-permute-done | bytes 90144 | tf_op jit(solution)/shard_map/ppermute | solution.py:30
  50.9 4.5 %collective-permute-done.3.ay_ref = f32[22,8,128]{2,1,0:T(8,128)S(1)} collective-permute-done((f32[22,8,128]{2,1,0:T(8,128)S(1)}, f32[22,8,128]{2,1,0:T(8,128)S(1)}, u32[]{:S(2)}, u32[]{:S(2)}) %collective-permute-start.3) | collective-permute-done | bytes 90144 | tf_op jit(solution)/shard_map/ppermute | solution.py:30
  55.4 0.2 pack_z.1
  55.6 1.3 %collective-permute-start.4 = (f32[48,128]{1,0:T(8,128)S(1)}, f32[48,128]{1,0:T(8,128)S(1)}, u32[]{:S(2)}, u32[]{:S(2)}) collective-permute-start(f32[48,128]{1,0:T(8,128)S(1)} %get-tuple-element.17), channel_id=1, source_target_pairs={{0,1},{1,2},{2,3},{3,0},{4,5},{5,6},{6,7},{7,4},{8,9},{9,10},{10,1... | collective-permute-start | bytes 73736 | tf_op jit(solution)/shard_map/ppermute | solution.py:30
  56.9 1.5 %collective-permute-start.5 = (f32[48,128]{1,0:T(8,128)S(1)}, f32[48,128]{1,0:T(8,128)S(1)}, u32[]{:S(2)}, u32[]{:S(2)}) collective-permute-start(f32[48,128]{1,0:T(8,128)S(1)} %get-tuple-element.18), channel_id=1, source_target_pairs={{0,3},{1,0},{2,1},{3,2},{4,7},{5,4},{6,5},{7,6},{8,11},{9,8},{10,9... | collective-permute-start | bytes 73736 | tf_op jit(solution)/shard_map/ppermute | solution.py:30
  58.4 1.2 %collective-permute-done.4.bz_ref = f32[48,128]{1,0:T(8,128)S(1)} collective-permute-done((f32[48,128]{1,0:T(8,128)S(1)}, f32[48,128]{1,0:T(8,128)S(1)}, u32[]{:S(2)}, u32[]{:S(2)}) %collective-permute-start.4) | collective-permute-done | bytes 24608 | tf_op jit(solution)/shard_map/ppermute | solution.py:30
  59.6 0.0 collective-permute-done.5.az_ref
  59.6 0.0 all-to-all-done.1.sq_ref
  59.6 3.1 %proximal.1 = (f32[16,16,128]{2,1,0:T(8,128)}, f32[16,16,128]{2,1,0:T(8,128)}) custom-call(s32[1]{0:T(128)} %bitcast.dev_ref, f32[16,16,128]{2,1,0:T(8,128)S(1)} %get-tuple-element.11.g_ref, f32[16,16,128]{2,1,0:T(8,128)S(1)} %copy-done, f32[104,128]{1,0:T(8,128)S(1)} %collective-permute-done.before_ref.bx_ref, ...), custom_call_target="tpu_custom_call" | custom-call | tf_op jit(solution)/shard_map/proximal/pallas_call | solution.py:340
Async XLA Ops:
  0.6 20.3 %copy-start = (f32[16,16,128]{2,1,0:T(8,128)S(1)}, f32[16,16,128]{2,1,0:T(8,128)}, u32[]{:S(2)}) copy-start(f32[16,16,128]{2,1,0:T(8,128)} %v_ref.7) | copy-start | bytes 393220
  21.0 3.3 %collective-permute-start = (f32[104,128]{1,0:T(8,128)S(1)}, f32[104,128]{1,0:T(8,128)S(1)}, u32[]{:S(2)}, u32[]{:S(2)}) collective-permute-start(f32[104,128]{1,0:T(8,128)S(1)} %get-tuple-element.12), channel_id=1, source_target_pairs={{0,32},{32,64},{64,96},{96,128},{128,160},{160,192},{192,224},{224... | collective-permute-start | bytes 159752 | tf_op jit(solution)/shard_map/ppermute | solution.py:30
  23.1 5.1 %collective-permute-start.1 = (f32[104,128]{1,0:T(8,128)S(1)}, f32[104,128]{1,0:T(8,128)S(1)}, u32[]{:S(2)}, u32[]{:S(2)}) collective-permute-start(f32[104,128]{1,0:T(8,128)S(1)} %get-tuple-element.13), channel_id=1, source_target_pairs={{0,224},{32,0},{64,32},{96,64},{128,96},{160,128},{192,160},{224,1... | collective-permute-start | bytes 159752 | tf_op jit(solution)/shard_map/ppermute | solution.py:30
  28.9 30.7 %all-to-all-start.1 = ((f32[128,1,128]{2,1,0:T(1,128)}), f32[128,1,128]{2,1,0:T(1,128)S(1)}, u32[]{:S(2)}, u32[]{:S(2)}) async-start(f32[128,1,128]{2,1,0:T(1,128)} %get-tuple-element.19), calls=%async_computation.1 | async-start | bytes 131072 | tf_op jit(solution)/shard_map/all_to_all | solution.py:365
  45.7 5.2 %collective-permute-start.2 = (f32[22,8,128]{2,1,0:T(8,128)S(1)}, f32[22,8,128]{2,1,0:T(8,128)S(1)}, u32[]{:S(2)}, u32[]{:S(2)}) collective-permute-start(f32[22,8,128]{2,1,0:T(8,128)S(1)} %get-tuple-element.15), channel_id=1, source_target_pairs={{0,4},{4,8},{8,12},{12,16},{16,20},{20,24},{24,28},{28,0},{1,5},{5... | collective-permute-start | bytes 270344 | tf_op jit(solution)/shard_map/ppermute | solution.py:30
  49.3 6.1 %collective-permute-start.3 = (f32[22,8,128]{2,1,0:T(8,128)S(1)}, f32[22,8,128]{2,1,0:T(8,128)S(1)}, u32[]{:S(2)}, u32[]{:S(2)}) collective-permute-start(f32[22,8,128]{2,1,0:T(8,128)S(1)} %get-tuple-element.16), channel_id=1, source_target_pairs={{0,28},{4,0},{8,4},{12,8},{16,12},{20,16},{24,20},{28,24},{1,29},{... | collective-permute-start | bytes 270344 | tf_op jit(solution)/shard_map/ppermute | solution.py:30
  55.6 4.0 %collective-permute-start.4 = (f32[48,128]{1,0:T(8,128)S(1)}, f32[48,128]{1,0:T(8,128)S(1)}, u32[]{:S(2)}, u32[]{:S(2)}) collective-permute-start(f32[48,128]{1,0:T(8,128)S(1)} %get-tuple-element.17), channel_id=1, source_target_pairs={{0,1},{1,2},{2,3},{3,0},{4,5},{5,6},{6,7},{7,4},{8,9},{9,10},{10,1... | collective-permute-start | bytes 73736 | tf_op jit(solution)/shard_map/ppermute | solution.py:30
  56.9 2.7 %collective-permute-start.5 = (f32[48,128]{1,0:T(8,128)S(1)}, f32[48,128]{1,0:T(8,128)S(1)}, u32[]{:S(2)}, u32[]{:S(2)}) collective-permute-start(f32[48,128]{1,0:T(8,128)S(1)} %get-tuple-element.18), channel_id=1, source_target_pairs={{0,3},{1,0},{2,1},{3,2},{4,7},{5,4},{6,5},{7,6},{8,11},{9,8},{10,9... | collective-permute-start | bytes 73736 | tf_op jit(solution)/shard_map/ppermute | solution.py:30

commit v5 on v3

--- a/solution.py
+++ b/solution.py
@@ -11,6 +11,7 @@
 GX = ("gx_0", "gx_1")
 GY = ("gy_0", "gy_1")
 ALL = GX + GY + ("gz",)
+XZ = GX + ("gz",)
 
 step_length = 0.5
 tv_weight = 0.2
@@ -25,6 +26,11 @@
 
 
 def shift(block, axis, distance):
+    devices = range(lax.axis_size(axis))
+    return lax.ppermute(block, axis, [(i, i + distance) for i in devices if i + distance in devices])
+
+
+def turn(block, axis, distance):
     size = lax.axis_size(axis)
     return lax.ppermute(block, axis, [(i, (i + distance) % size) for i in range(size)])
 
@@ -201,7 +207,7 @@
     )(gradient, velocity, before_x, after_x, before_y, after_y)
 
 
-def proximal(device, gradient, velocity, halos, squares, sizes):
+def proximal(device, gradient, velocity, halos, sums, sizes):
     bx, by, bz = velocity.shape
     planes = bx + 2 * HALO
     pairs = planes // 2
@@ -220,18 +226,11 @@
         ay_ref,
         bz_ref,
         az_ref,
-        sq_ref,
-        gradient_ref,
-        model_ref,
-        target,
-        current,
-        extra,
-        dual_x,
-        dual_y,
-        dual_z,
-        model,
-        sems,
+        *refs,
     ):
+        sum_refs = refs[: len(sums)]
+        gradient_ref, model_ref, target, current, extra = refs[len(sums) : len(sums) + 5]
+        dual_x, dual_y, dual_z, model, sems = refs[len(sums) + 5 :]
         gradient_copy = pltpu.make_async_copy(g_ref, gradient_ref, sems.at[0])
         gradient_copy.start()
         dev = dev_ref[0]
@@ -239,7 +238,10 @@
         pos_y = (dev // size_z) % size_y
         pos_x = dev // (size_z * size_y)
 
-        total = jnp.sum(jnp.sum(sq_ref[...], axis=0), axis=1, keepdims=True)
+        total = sum_refs[0][0:1]
+        for ref in sum_refs[1:]:
+            total = total + ref[0:1]
+        total = jnp.sum(total, axis=1, keepdims=True)
         scale = step_length * lax.rsqrt(total / cells + 1.0)
         scale = jnp.broadcast_to(scale, (1, bz))
 
@@ -331,30 +333,34 @@
         name="proximal",
         compiler_params=PARAMS,
         out_shape=(struct(bx, by, bz),) * 2,
-        in_specs=[SMEM] + [VMEM] * 9,
+        in_specs=[SMEM] + [VMEM] * (8 + len(sums)),
         out_specs=(HBM,) * 2,
         scratch_shapes=[field] * 6 + [pltpu.VMEM((bx, by, bz), F32), pltpu.SemaphoreType.DMA((2,))],
-    )(device, gradient, velocity, *halos, squares)
+    )(device, gradient, velocity, *halos, *sums)
 
 
 def shards(partials, code_bits, group_map, velocity):
-    _, _, bz = velocity.shape
-    size_x, size_y, size_z = (lax.axis_size(axis) for axis in (GX, GY, "gz"))
+    sizes = tuple(lax.axis_size(axis) for axis in (GX, GY, "gz"))
     base = (lax.axis_index(GX) * partials.shape[0]).astype(jnp.int32).reshape(1)
     device = lax.axis_index(ALL).astype(jnp.int32).reshape(1)
 
     local = presum(partials, code_bits, group_map, base, 8)
     parts = lax.all_to_all(local, GX, split_axis=0, concat_axis=0, tiled=True)
-    gradient, first_x, last_x, squares = reduce_pack(parts, velocity, size_x)
+    gradient, first_x, last_x, squares = reduce_pack(parts, velocity, sizes[0])
 
     after_x = shift(first_x, GX, -1)
     before_x = shift(last_x, GX, 1)
-    table = jnp.broadcast_to(squares[:1][None], (size_x * size_y * size_z, 1, bz))
-    table = lax.all_to_all(table, ALL, split_axis=0, concat_axis=0, tiled=True)
+    table = jnp.broadcast_to(squares[:1][None], (sizes[0] * sizes[2], 1, squares.shape[1]))
+    table = lax.all_to_all(table, XZ, split_axis=0, concat_axis=0, tiled=True)
 
     first_y, last_y = pack_y(gradient, velocity, before_x, after_x)
     after_y = shift(first_y, GY, -1)
     before_y = shift(last_y, GY, 1)
+
+    column = jnp.broadcast_to(jnp.sum(table, axis=0), squares.shape)
+    for d in range(1, lax.axis_size(GY[1])):
+        column = column + turn(column, GY[1], d)
+    columns = [turn(column, GY[0], d) for d in range(1, lax.axis_size(GY[0]))]
 
     first_z, last_z = pack_z(gradient, velocity, before_x, after_x, before_y, after_y)
     after_z = shift(first_z, "gz", -1)
@@ -365,8 +371,8 @@
         gradient,
         velocity,
         (before_x, after_x, before_y, after_y, before_z, after_z),
-        table,
-        (size_x, size_y, size_z),
+        [column, *columns],
+        sizes,
     )
 
 

time: 61.8 us -> 78.9 us (1.28)
  blocking collectives: 21 us -> 35.2 us
  starting transfers between devices: 23.5 us -> 28 us
  waiting for transfers between devices: 10.1 us -> 6.17 us
  Pallas kernels: 5.28 us -> 7.37 us
    ppermute x6 -> x10, starting transfers between devices: 10.3 us -> 28 us  [the longest x6 17.1 us: shift(): lax.ppermute(block, axis, [(i, i + distance) for i in devices if i + dist...]
    all_to_all x0 -> x1, blocking collectives: none -> 14.3 us  [shards(): table = lax.all_to_all(table, XZ, split_axis=0, concat_axis=0, tiled=True)]
    all_to_all x1 -> x0, starting transfers between devices: 13.2 us -> none  [shards(): table = lax.all_to_all(table, ALL, split_axis=0, concat_axis=0, tiled=True)]
    ppermute x6 -> x10, waiting for transfers between devices: 10.1 us -> 6.17 us  [the longest x6 3.57 us: shift(): lax.ppermute(block, axis, [(i, i + distance) for i in devices if i + dist...]
    pallas_call x1, Pallas kernels: 2.57 us -> 4.66 us  [proximal(): pl.pallas_call(kernel, name='proximal', compiler_params=PARAMS, out_shape...]
  transfers between devices with their start and end apart: 7 -> 10, of which waited for: 4 -> 3; matrix products, arithmetic and copies ran while one was open for 0% -> 0% of each run, Pallas kernels for 0% -> 0%
where the time goes in v5:
time: 78.9 us; the launch traced here: 77.6 us
  blocking collectives  35.2 us (45%)
  starting transfers between devices  28 us (35%)
  Pallas kernels  7.37 us (9%)
  waiting for transfers between devices  6.17 us (8%)
    all_to_all x1, blocking collectives, shards(): parts = lax.all_to_all(local, GX, split_axis=0, concat_axis=0, tiled=True)  21 us
    ppermute x6, starting transfers between devices, shift(): lax.ppermute(block, axis, [(i, i + distance) for i in devices if i + dist...  17.1 us
    all_to_all x1, blocking collectives, shards(): table = lax.all_to_all(table, XZ, split_axis=0, concat_axis=0, tiled=True)  14.3 us
    ppermute x4, starting transfers between devices, turn(): lax.ppermute(block, axis, [(i, (i + distance) % size) for i in range(size)])  10.9 us
    pallas_call x1, Pallas kernels, proximal(): pl.pallas_call(kernel, name='proximal', compiler_params=PARAMS, out_shape...  4.66 us
    ppermute x6, waiting for transfers between devices, shift(): lax.ppermute(block, axis, [(i, i + distance) for i in devices if i + dist...  3.57 us
    ppermute x4, waiting for transfers between devices, turn(): lax.ppermute(block, axis, [(i, (i + distance) % size) for i in range(size)])  2.6 us
    pallas_call x1, Pallas kernels, presum(): pl.pallas_call(kernel, name='presum', compiler_params=PARAMS, out_shape=s...  2.42 us
  transfers between devices with their start and end apart: 10, of which 3 were waited for; matrix products, arithmetic and copies ran while one was open for 0% of the time, Pallas kernels for 0%

profile of v5, /device:TPU:1, one launch (start us, length us, event | category | flops | bytes accessed | tf_op | source)
XLA Modules:
  0.0 77.6 jit_solution(10229147384294259483)
XLA Ops:
  0.6 0.0 copy-start
  0.7 2.4 %presum.1 = f32[128,16,128]{2,1,0:T(8,128)S(1)} custom-call(s32[1]{0:T(128)} %bitcast.1.base_ref, s32[32]{0:T(128)} %map_hbm.1, s32[32,128]{1,0:T(8,128)} %bits_hbm.1, f32[4,128,16,128]{3,2,1,0:T(8,128)} %part_ref.1), custom_call_target="tpu_custom_call" | custom-call | tf_op jit(solution)/shard_map/presum/pallas_call | solution.py:80
  3.1 21.0 %all_to_all.10.part_ref = f32[128,16,128]{2,1,0:T(8,128)S(1)} all-to-all(f32[128,16,128]{2,1,0:T(8,128)S(1)} %presum.1), channel_id=1, replica_groups=mesh['gx_0'=4,'gx_1'=2,'gy_0'=4,'gy_1'=2,'gz'=4] {'gx_0','gx_1'}, dimensions={0} | all-to-all | bytes 2097152 | tf_op jit(solution)/shard_map/all_to_all | solution.py:348
  24.0 0.0 copy-done
  24.1 0.1 reduce_pack.1
  24.1 2.3 %collective-permute-start = (f32[6,16,128]{2,1,0:T(8,128)S(1)}, f32[6,16,128]{2,1,0:T(8,128)S(1)}, u32[]{:S(2)}, u32[]{:S(2)}) collective-permute-start(f32[6,16,128]{2,1,0:T(8,128)S(1)} %get-tuple-element.11), channel_id=1, source_target_pairs={{0,32},{32,64},{64,96},{96,128},{128,160},{160,192},{192,224},{1,3... | collective-permute-start | bytes 147464 | tf_op jit(solution)/shard_map/ppermute | solution.py:30
  26.5 1.3 %collective-permute-start.1 = (f32[6,16,128]{2,1,0:T(8,128)S(1)}, f32[6,16,128]{2,1,0:T(8,128)S(1)}, u32[]{:S(2)}, u32[]{:S(2)}) collective-permute-start(f32[6,16,128]{2,1,0:T(8,128)S(1)} %get-tuple-element.12), channel_id=1, source_target_pairs={{32,0},{64,32},{96,64},{128,96},{160,128},{192,160},{224,192},{33,... | collective-permute-start | bytes 147464 | tf_op jit(solution)/shard_map/ppermute | solution.py:30
  27.8 0.0 collective-permute-done.before_ref.bx_ref
  27.8 3.6 %collective-permute-done.1.after_ref.ax_ref = f32[6,16,128]{2,1,0:T(8,128)S(1)} collective-permute-done((f32[6,16,128]{2,1,0:T(8,128)S(1)}, f32[6,16,128]{2,1,0:T(8,128)S(1)}, u32[]{:S(2)}, u32[]{:S(2)}) %collective-permute-start.1) | collective-permute-done | bytes 49184 | tf_op jit(solution)/shard_map/ppermute | solution.py:30
  31.4 8.0 %collective-permute-start.2 = (f32[22,8,128]{2,1,0:T(8,128)S(1)}, f32[22,8,128]{2,1,0:T(8,128)S(1)}, u32[]{:S(2)}, u32[]{:S(2)}) collective-permute-start(f32[22,8,128]{2,1,0:T(8,128)S(1)} %get-tuple-element.13), channel_id=1, source_target_pairs={{0,4},{4,8},{8,12},{12,16},{16,20},{20,24},{24,28},{1,5},{5,9},{9,... | collective-permute-start | bytes 270344 | tf_op jit(solution)/shard_map/ppermute | solution.py:30
  39.4 1.9 %collective-permute-start.3 = (f32[22,8,128]{2,1,0:T(8,128)S(1)}, f32[22,8,128]{2,1,0:T(8,128)S(1)}, u32[]{:S(2)}, u32[]{:S(2)}) collective-permute-start(f32[22,8,128]{2,1,0:T(8,128)S(1)} %get-tuple-element.14), channel_id=1, source_target_pairs={{4,0},{8,4},{12,8},{16,12},{20,16},{24,20},{28,24},{5,1},{9,5},{13... | collective-permute-start | bytes 270344 | tf_op jit(solution)/shard_map/ppermute | solution.py:30
  41.3 14.3 %all_to_all.11 = f32[32,1,128]{2,1,0:T(1,128)S(1)} all-to-all(f32[32,1,128]{2,1,0:T(1,128)S(1)} %broadcast_in_dim.14), channel_id=1, replica_groups=mesh['gx_0'=4,'gx_1'=2,'gy_0'=4,'gy_1'=2,'gz'=4] {'gx_0','gx_1','gz'}, dimensions={0} | all-to-all | bytes 32768 | tf_op jit(solution)/shard_map/all_to_all | solution.py:354
  55.6 0.1 collective-permute-start.6
  55.7 0.0 collective-permute-done.2.by_ref
  55.7 0.0 collective-permute-done.3.ay_ref
  55.7 0.2 pack_z.1
  56.0 2.2 %collective-permute-start.4 = (f32[48,128]{1,0:T(8,128)S(1)}, f32[48,128]{1,0:T(8,128)S(1)}, u32[]{:S(2)}, u32[]{:S(2)}) collective-permute-start(f32[48,128]{1,0:T(8,128)S(1)} %get-tuple-element.15), channel_id=1, source_target_pairs={{0,1},{1,2},{2,3},{4,5},{5,6},{6,7},{8,9},{9,10},{10,11},{12,13},{... | collective-permute-start | bytes 73736 | tf_op jit(solution)/shard_map/ppermute | solution.py:30
  58.2 1.3 %collective-permute-start.5 = (f32[48,128]{1,0:T(8,128)S(1)}, f32[48,128]{1,0:T(8,128)S(1)}, u32[]{:S(2)}, u32[]{:S(2)}) collective-permute-start(f32[48,128]{1,0:T(8,128)S(1)} %get-tuple-element.16), channel_id=1, source_target_pairs={{1,0},{2,1},{3,2},{5,4},{6,5},{7,6},{9,8},{10,9},{11,10},{13,12},{... | collective-permute-start | bytes 73736 | tf_op jit(solution)/shard_map/ppermute | solution.py:30
  59.5 0.0 collective-permute-done.6
  59.5 6.4 %collective-permute-start.9 = (f32[8,128]{1,0:T(8,128)S(1)}, f32[8,128]{1,0:T(8,128)S(1)}, u32[]{:S(2)}, u32[]{:S(2)}) collective-permute-start(f32[8,128]{1,0:T(8,128)S(1)} %broadcast_add_fusion.refs_0_), channel_id=1, source_target_pairs={{0,24},{8,0},{16,8},{24,16},{1,25},{9,1},{17,9},{25,17},{2,26},{10... | collective-permute-start | bytes 12296 | tf_op jit(solution)/shard_map/ppermute | solution.py:35
  65.8 2.2 %collective-permute-start.8 = (f32[8,128]{1,0:T(8,128)S(1)}, f32[8,128]{1,0:T(8,128)S(1)}, u32[]{:S(2)}, u32[]{:S(2)}) collective-permute-start(f32[8,128]{1,0:T(8,128)S(1)} %broadcast_add_fusion.refs_0_), channel_id=1, source_target_pairs={{0,16},{8,24},{16,0},{24,8},{1,17},{9,25},{17,1},{25,9},{2,18},{10... | collective-permute-start | bytes 12296 | tf_op jit(solution)/shard_map/ppermute | solution.py:35
  68.1 2.3 %collective-permute-start.7 = (f32[8,128]{1,0:T(8,128)S(1)}, f32[8,128]{1,0:T(8,128)S(1)}, u32[]{:S(2)}, u32[]{:S(2)}) collective-permute-start(f32[8,128]{1,0:T(8,128)S(1)} %broadcast_add_fusion.refs_0_), channel_id=1, source_target_pairs={{0,8},{8,16},{16,24},{24,0},{1,9},{9,17},{17,25},{25,1},{2,10},{10... | collective-permute-start | bytes 12296 | tf_op jit(solution)/shard_map/ppermute | solution.py:35
  70.3 0.0 collective-permute-done.9.refs_3_
  70.3 1.9 %collective-permute-done.8.refs_2_ = f32[8,128]{1,0:T(8,128)S(1)} collective-permute-done((f32[8,128]{1,0:T(8,128)S(1)}, f32[8,128]{1,0:T(8,128)S(1)}, u32[]{:S(2)}, u32[]{:S(2)}) %collective-permute-start.8) | collective-permute-done | bytes 4128 | tf_op jit(solution)/shard_map/ppermute | solution.py:35
  72.2 0.7 collective-permute-done.7.refs_1_
  72.9 0.0 collective-permute-done.4.bz_ref
  72.9 0.0 collective-permute-done.5.az_ref
  72.9 4.7 %proximal.1 = (f32[16,16,128]{2,1,0:T(8,128)}, f32[16,16,128]{2,1,0:T(8,128)}) custom-call(s32[1]{0:T(128)} %bitcast.dev_ref, f32[16,16,128]{2,1,0:T(8,128)S(1)} %get-tuple-element.10.g_ref, f32[16,16,128]{2,1,0:T(8,128)S(1)} %copy-done, f32[6,16,128]{2,1,0:T(8,128)S(1)} %collective-permute-done.before_ref.bx_ref, ...), custom_call_target="tpu_custom_call" | custom-call | tf_op jit(solution)/shard_map/proximal/pallas_call | solution.py:331
  (6 shorter events, 0.1 us)
Async XLA Ops:
  0.6 23.4 %copy-start = (f32[16,16,128]{2,1,0:T(8,128)S(1)}, f32[16,16,128]{2,1,0:T(8,128)}, u32[]{:S(2)}) copy-start(f32[16,16,128]{2,1,0:T(8,128)} %v_ref.7) | copy-start | bytes 393220
  24.1 3.7 %collective-permute-start = (f32[6,16,128]{2,1,0:T(8,128)S(1)}, f32[6,16,128]{2,1,0:T(8,128)S(1)}, u32[]{:S(2)}, u32[]{:S(2)}) collective-permute-start(f32[6,16,128]{2,1,0:T(8,128)S(1)} %get-tuple-element.11), channel_id=1, source_target_pairs={{0,32},{32,64},{64,96},{96,128},{128,160},{160,192},{192,224},{1,3... | collective-permute-start | bytes 147464 | tf_op jit(solution)/shard_map/ppermute | solution.py:30
  26.5 4.9 %collective-permute-start.1 = (f32[6,16,128]{2,1,0:T(8,128)S(1)}, f32[6,16,128]{2,1,0:T(8,128)S(1)}, u32[]{:S(2)}, u32[]{:S(2)}) collective-permute-start(f32[6,16,128]{2,1,0:T(8,128)S(1)} %get-tuple-element.12), channel_id=1, source_target_pairs={{32,0},{64,32},{96,64},{128,96},{160,128},{192,160},{224,192},{33,... | collective-permute-start | bytes 147464 | tf_op jit(solution)/shard_map/ppermute | solution.py:30
  31.4 24.4 %collective-permute-start.2 = (f32[22,8,128]{2,1,0:T(8,128)S(1)}, f32[22,8,128]{2,1,0:T(8,128)S(1)}, u32[]{:S(2)}, u32[]{:S(2)}) collective-permute-start(f32[22,8,128]{2,1,0:T(8,128)S(1)} %get-tuple-element.13), channel_id=1, source_target_pairs={{0,4},{4,8},{8,12},{12,16},{16,20},{20,24},{24,28},{1,5},{5,9},{9,... | collective-permute-start | bytes 270344 | tf_op jit(solution)/shard_map/ppermute | solution.py:30
  39.4 16.4 %collective-permute-start.3 = (f32[22,8,128]{2,1,0:T(8,128)S(1)}, f32[22,8,128]{2,1,0:T(8,128)S(1)}, u32[]{:S(2)}, u32[]{:S(2)}) collective-permute-start(f32[22,8,128]{2,1,0:T(8,128)S(1)} %get-tuple-element.14), channel_id=1, source_target_pairs={{4,0},{8,4},{12,8},{16,12},{20,16},{24,20},{28,24},{5,1},{9,5},{13... | collective-permute-start | bytes 270344 | tf_op jit(solution)/shard_map/ppermute | solution.py:30
  55.6 3.8 %collective-permute-start.6 = (f32[8,128]{1,0:T(8,128)S(1)}, f32[8,128]{1,0:T(8,128)S(1)}, u32[]{:S(2)}, u32[]{:S(2)}) collective-permute-start(f32[8,128]{1,0:T(8,128)S(1)} %broadcast_in_dim.15), channel_id=1, source_target_pairs={{0,4},{4,0},{1,5},{5,1},{2,6},{6,2},{3,7},{7,3},{8,12},{12,8},{9,1... | collective-permute-start | bytes 12296 | tf_op jit(solution)/shard_map/ppermute | solution.py:35
  56.0 17.0 %collective-permute-start.4 = (f32[48,128]{1,0:T(8,128)S(1)}, f32[48,128]{1,0:T(8,128)S(1)}, u32[]{:S(2)}, u32[]{:S(2)}) collective-permute-start(f32[48,128]{1,0:T(8,128)S(1)} %get-tuple-element.15), channel_id=1, source_target_pairs={{0,1},{1,2},{2,3},{4,5},{5,6},{6,7},{8,9},{9,10},{10,11},{12,13},{... | collective-permute-start | bytes 73736 | tf_op jit(solution)/shard_map/ppermute | solution.py:30
  58.2 14.7 %collective-permute-start.5 = (f32[48,128]{1,0:T(8,128)S(1)}, f32[48,128]{1,0:T(8,128)S(1)}, u32[]{:S(2)}, u32[]{:S(2)}) collective-permute-start(f32[48,128]{1,0:T(8,128)S(1)} %get-tuple-element.16), channel_id=1, source_target_pairs={{1,0},{2,1},{3,2},{5,4},{6,5},{7,6},{9,8},{10,9},{11,10},{13,12},{... | collective-permute-start | bytes 73736 | tf_op jit(solution)/shard_map/ppermute | solution.py:30
  59.5 10.8 %collective-permute-start.9 = (f32[8,128]{1,0:T(8,128)S(1)}, f32[8,128]{1,0:T(8,128)S(1)}, u32[]{:S(2)}, u32[]{:S(2)}) collective-permute-start(f32[8,128]{1,0:T(8,128)S(1)} %broadcast_add_fusion.refs_0_), channel_id=1, source_target_pairs={{0,24},{8,0},{16,8},{24,16},{1,25},{9,1},{17,9},{25,17},{2,26},{10... | collective-permute-start | bytes 12296 | tf_op jit(solution)/shard_map/ppermute | solution.py:35
  65.8 6.4 %collective-permute-start.8 = (f32[8,128]{1,0:T(8,128)S(1)}, f32[8,128]{1,0:T(8,128)S(1)}, u32[]{:S(2)}, u32[]{:S(2)}) collective-permute-start(f32[8,128]{1,0:T(8,128)S(1)} %broadcast_add_fusion.refs_0_), channel_id=1, source_target_pairs={{0,16},{8,24},{16,0},{24,8},{1,17},{9,25},{17,1},{25,9},{2,18},{10... | collective-permute-start | bytes 12296 | tf_op jit(solution)/shard_map/ppermute | solution.py:35
  68.1 4.9 %collective-permute-start.7 = (f32[8,128]{1,0:T(8,128)S(1)}, f32[8,128]{1,0:T(8,128)S(1)}, u32[]{:S(2)}, u32[]{:S(2)}) collective-permute-start(f32[8,128]{1,0:T(8,128)S(1)} %broadcast_add_fusion.refs_0_), channel_id=1, source_target_pairs={{0,8},{8,16},{16,24},{24,0},{1,9},{9,17},{17,25},{25,1},{2,10},{10... | collective-permute-start | bytes 12296 | tf_op jit(solution)/shard_map/ppermute | solution.py:35

commit v6 on v5

--- a/solution.py
+++ b/solution.py
@@ -26,11 +26,6 @@
 
 
 def shift(block, axis, distance):
-    devices = range(lax.axis_size(axis))
-    return lax.ppermute(block, axis, [(i, i + distance) for i in devices if i + distance in devices])
-
-
-def turn(block, axis, distance):
     size = lax.axis_size(axis)
     return lax.ppermute(block, axis, [(i, (i + distance) % size) for i in range(size)])
 
@@ -359,8 +354,8 @@
 
     column = jnp.broadcast_to(jnp.sum(table, axis=0), squares.shape)
     for d in range(1, lax.axis_size(GY[1])):
-        column = column + turn(column, GY[1], d)
-    columns = [turn(column, GY[0], d) for d in range(1, lax.axis_size(GY[0]))]
+        column = column + shift(column, GY[1], d)
+    columns = [shift(column, GY[0], d) for d in range(1, lax.axis_size(GY[0]))]
 
     first_z, last_z = pack_z(gradient, velocity, before_x, after_x, before_y, after_y)
     after_z = shift(first_z, "gz", -1)

time: 78.9 us -> 71.3 us (0.904); the launches traced: 77.6 us -> 71.1 us
  starting transfers between devices: 28 us -> 23.2 us
  waiting for transfers between devices: 6.17 us -> 3.78 us
  blocking collectives: 35.2 us -> 36.1 us
    ppermute x10, starting transfers between devices: 28 us -> 23.2 us  [shift(): lax.ppermute(block, axis, [(i, (i + distance) % size) for i in range(size)])]
    ppermute x10, waiting for transfers between devices: 6.17 us -> 3.78 us  [shift(): lax.ppermute(block, axis, [(i, (i + distance) % size) for i in range(size)])]
    all_to_all x1, blocking collectives: 14.3 us -> 15.1 us  [shards(): table = lax.all_to_all(table, XZ, split_axis=0, concat_axis=0, tiled=True)]
where the time goes in v6:
time: 71.3 us; the launch traced here: 71.1 us
  blocking collectives  36.1 us (51%)
  starting transfers between devices  23.2 us (33%)
  Pallas kernels  7.37 us (10%)
  waiting for transfers between devices  3.78 us (5%)
    ppermute x10, starting transfers between devices, shift(): lax.ppermute(block, axis, [(i, (i + distance) % size) for i in range(size)])  23.2 us
    all_to_all x1, blocking collectives, shards(): parts = lax.all_to_all(local, GX, split_axis=0, concat_axis=0, tiled=True)  21 us
    all_to_all x1, blocking collectives, shards(): table = lax.all_to_all(table, XZ, split_axis=0, concat_axis=0, tiled=True)  15.1 us
    pallas_call x1, Pallas kernels, proximal(): pl.pallas_call(kernel, name='proximal', compiler_params=PARAMS, out_shape...  4.66 us
    ppermute x10, waiting for transfers between devices, shift(): lax.ppermute(block, axis, [(i, (i + distance) % size) for i in range(size)])  3.78 us
    pallas_call x1, Pallas kernels, presum(): pl.pallas_call(kernel, name='presum', compiler_params=PARAMS, out_shape=s...  2.42 us
  transfers between devices with their start and end apart: 10, of which 3 were waited for; matrix products, arithmetic and copies ran while one was open for 0% of the time, Pallas kernels for 0%

profile of v6, /device:TPU:1, one launch (start us, length us, event | category | flops | bytes accessed | tf_op | source)
XLA Modules:
  0.0 71.1 jit_solution(2265454479130741700)
XLA Ops:
  0.6 0.0 copy-start
  0.7 2.4 %presum.1 = f32[128,16,128]{2,1,0:T(8,128)S(1)} custom-call(s32[1]{0:T(128)} %bitcast.1.base_ref, s32[32]{0:T(128)} %map_hbm.1, s32[32,128]{1,0:T(8,128)} %bits_hbm.1, f32[4,128,16,128]{3,2,1,0:T(8,128)} %part_ref.1), custom_call_target="tpu_custom_call" | custom-call | tf_op jit(solution)/shard_map/presum/pallas_call | solution.py:75
  3.1 21.0 %all_to_all.10.part_ref = f32[128,16,128]{2,1,0:T(8,128)S(1)} all-to-all(f32[128,16,128]{2,1,0:T(8,128)S(1)} %presum.1), channel_id=1, replica_groups=mesh['gx_0'=4,'gx_1'=2,'gy_0'=4,'gy_1'=2,'gz'=4] {'gx_0','gx_1'}, dimensions={0} | all-to-all | bytes 2097152 | tf_op jit(solution)/shard_map/all_to_all | solution.py:343
  24.0 0.0 copy-done
  24.1 0.1 reduce_pack.1
  24.1 0.5 collective-permute-start
  24.6 3.1 %collective-permute-start.1 = (f32[6,16,128]{2,1,0:T(8,128)S(1)}, f32[6,16,128]{2,1,0:T(8,128)S(1)}, u32[]{:S(2)}, u32[]{:S(2)}) collective-permute-start(f32[6,16,128]{2,1,0:T(8,128)S(1)} %get-tuple-element.12), channel_id=1, source_target_pairs={{0,224},{32,0},{64,32},{96,64},{128,96},{160,128},{192,160},{224,1... | collective-permute-start | bytes 147464 | tf_op jit(solution)/shard_map/ppermute | solution.py:30
  27.8 1.5 %collective-permute-done.before_ref.bx_ref = f32[6,16,128]{2,1,0:T(8,128)S(1)} collective-permute-done((f32[6,16,128]{2,1,0:T(8,128)S(1)}, f32[6,16,128]{2,1,0:T(8,128)S(1)}, u32[]{:S(2)}, u32[]{:S(2)}) %collective-permute-start) | collective-permute-done | bytes 49184 | tf_op jit(solution)/shard_map/ppermute | solution.py:30
  29.2 0.0 collective-permute-done.1.after_ref.ax_ref
  29.3 5.9 %collective-permute-start.2 = (f32[22,8,128]{2,1,0:T(8,128)S(1)}, f32[22,8,128]{2,1,0:T(8,128)S(1)}, u32[]{:S(2)}, u32[]{:S(2)}) collective-permute-start(f32[22,8,128]{2,1,0:T(8,128)S(1)} %get-tuple-element.13), channel_id=1, source_target_pairs={{0,4},{4,8},{8,12},{12,16},{16,20},{20,24},{24,28},{28,0},{1,5},{5... | collective-permute-start | bytes 270344 | tf_op jit(solution)/shard_map/ppermute | solution.py:30
  35.2 0.0 collective-permute-start.3
  35.2 15.1 %all_to_all.11 = f32[32,1,128]{2,1,0:T(1,128)S(1)} all-to-all(f32[32,1,128]{2,1,0:T(1,128)S(1)} %broadcast_in_dim.14), channel_id=1, replica_groups=mesh['gx_0'=4,'gx_1'=2,'gy_0'=4,'gy_1'=2,'gz'=4] {'gx_0','gx_1','gz'}, dimensions={0} | all-to-all | bytes 32768 | tf_op jit(solution)/shard_map/all_to_all | solution.py:349
  50.3 2.5 %collective-permute-start.6 = (f32[8,128]{1,0:T(8,128)S(1)}, f32[8,128]{1,0:T(8,128)S(1)}, u32[]{:S(2)}, u32[]{:S(2)}) collective-permute-start(f32[8,128]{1,0:T(8,128)S(1)} %broadcast_in_dim.15), channel_id=1, source_target_pairs={{0,4},{4,0},{1,5},{5,1},{2,6},{6,2},{3,7},{7,3},{8,12},{12,8},{9,1... | collective-permute-start | bytes 12296 | tf_op jit(solution)/shard_map/ppermute | solution.py:30
  52.8 0.0 collective-permute-done.2.by_ref
  52.8 0.0 collective-permute-done.3.ay_ref
  52.8 0.2 pack_z.1
  53.0 0.4 collective-permute-start.4
  53.4 2.4 %collective-permute-start.5 = (f32[48,128]{1,0:T(8,128)S(1)}, f32[48,128]{1,0:T(8,128)S(1)}, u32[]{:S(2)}, u32[]{:S(2)}) collective-permute-start(f32[48,128]{1,0:T(8,128)S(1)} %get-tuple-element.16), channel_id=1, source_target_pairs={{0,3},{1,0},{2,1},{3,2},{4,7},{5,4},{6,5},{7,6},{8,11},{9,8},{10,9... | collective-permute-start | bytes 73736 | tf_op jit(solution)/shard_map/ppermute | solution.py:30
  55.8 0.0 collective-permute-done.6
  55.8 4.1 %collective-permute-start.9 = (f32[8,128]{1,0:T(8,128)S(1)}, f32[8,128]{1,0:T(8,128)S(1)}, u32[]{:S(2)}, u32[]{:S(2)}) collective-permute-start(f32[8,128]{1,0:T(8,128)S(1)} %broadcast_add_fusion.refs_0_), channel_id=1, source_target_pairs={{0,24},{8,0},{16,8},{24,16},{1,25},{9,1},{17,9},{25,17},{2,26},{10... | collective-permute-start | bytes 12296 | tf_op jit(solution)/shard_map/ppermute | solution.py:30
  59.9 2.0 %collective-permute-start.8 = (f32[8,128]{1,0:T(8,128)S(1)}, f32[8,128]{1,0:T(8,128)S(1)}, u32[]{:S(2)}, u32[]{:S(2)}) collective-permute-start(f32[8,128]{1,0:T(8,128)S(1)} %broadcast_add_fusion.refs_0_), channel_id=1, source_target_pairs={{0,16},{8,24},{16,0},{24,8},{1,17},{9,25},{17,1},{25,9},{2,18},{10... | collective-permute-start | bytes 12296 | tf_op jit(solution)/shard_map/ppermute | solution.py:30
  61.9 2.3 %collective-permute-start.7 = (f32[8,128]{1,0:T(8,128)S(1)}, f32[8,128]{1,0:T(8,128)S(1)}, u32[]{:S(2)}, u32[]{:S(2)}) collective-permute-start(f32[8,128]{1,0:T(8,128)S(1)} %broadcast_add_fusion.refs_0_), channel_id=1, source_target_pairs={{0,8},{8,16},{16,24},{24,0},{1,9},{9,17},{17,25},{25,1},{2,10},{10... | collective-permute-start | bytes 12296 | tf_op jit(solution)/shard_map/ppermute | solution.py:30
  64.2 0.0 collective-permute-done.9.refs_3_
  64.2 2.1 %collective-permute-done.8.refs_2_ = f32[8,128]{1,0:T(8,128)S(1)} collective-permute-done((f32[8,128]{1,0:T(8,128)S(1)}, f32[8,128]{1,0:T(8,128)S(1)}, u32[]{:S(2)}, u32[]{:S(2)}) %collective-permute-start.8) | collective-permute-done | bytes 4128 | tf_op jit(solution)/shard_map/ppermute | solution.py:30
  66.3 0.2 collective-permute-done.7.refs_1_
  66.5 0.0 collective-permute-done.4.bz_ref
  66.5 0.0 collective-permute-done.5.az_ref
  66.5 4.7 %proximal.1 = (f32[16,16,128]{2,1,0:T(8,128)}, f32[16,16,128]{2,1,0:T(8,128)}) custom-call(s32[1]{0:T(128)} %bitcast.dev_ref, f32[16,16,128]{2,1,0:T(8,128)S(1)} %get-tuple-element.10.g_ref, f32[16,16,128]{2,1,0:T(8,128)S(1)} %copy-done, f32[6,16,128]{2,1,0:T(8,128)S(1)} %collective-permute-done.before_ref.bx_ref, ...), custom_call_target="tpu_custom_call" | custom-call | tf_op jit(solution)/shard_map/proximal/pallas_call | solution.py:326
  (6 shorter events, 0.1 us)
Async XLA Ops:
  0.6 23.4 %copy-start = (f32[16,16,128]{2,1,0:T(8,128)S(1)}, f32[16,16,128]{2,1,0:T(8,128)}, u32[]{:S(2)}) copy-start(f32[16,16,128]{2,1,0:T(8,128)} %v_ref.7) | copy-start | bytes 393220
  24.1 5.1 %collective-permute-start = (f32[6,16,128]{2,1,0:T(8,128)S(1)}, f32[6,16,128]{2,1,0:T(8,128)S(1)}, u32[]{:S(2)}, u32[]{:S(2)}) collective-permute-start(f32[6,16,128]{2,1,0:T(8,128)S(1)} %get-tuple-element.11), channel_id=1, source_target_pairs={{0,32},{32,64},{64,96},{96,128},{128,160},{160,192},{192,224},{224... | collective-permute-start | bytes 147464 | tf_op jit(solution)/shard_map/ppermute | solution.py:30
  24.6 4.6 %collective-permute-start.1 = (f32[6,16,128]{2,1,0:T(8,128)S(1)}, f32[6,16,128]{2,1,0:T(8,128)S(1)}, u32[]{:S(2)}, u32[]{:S(2)}) collective-permute-start(f32[6,16,128]{2,1,0:T(8,128)S(1)} %get-tuple-element.12), channel_id=1, source_target_pairs={{0,224},{32,0},{64,32},{96,64},{128,96},{160,128},{192,160},{224,1... | collective-permute-start | bytes 147464 | tf_op jit(solution)/shard_map/ppermute | solution.py:30
  29.3 23.6 %collective-permute-start.2 = (f32[22,8,128]{2,1,0:T(8,128)S(1)}, f32[22,8,128]{2,1,0:T(8,128)S(1)}, u32[]{:S(2)}, u32[]{:S(2)}) collective-permute-start(f32[22,8,128]{2,1,0:T(8,128)S(1)} %get-tuple-element.13), channel_id=1, source_target_pairs={{0,4},{4,8},{8,12},{12,16},{16,20},{20,24},{24,28},{28,0},{1,5},{5... | collective-permute-start | bytes 270344 | tf_op jit(solution)/shard_map/ppermute | solution.py:30
  35.2 17.7 %collective-permute-start.3 = (f32[22,8,128]{2,1,0:T(8,128)S(1)}, f32[22,8,128]{2,1,0:T(8,128)S(1)}, u32[]{:S(2)}, u32[]{:S(2)}) collective-permute-start(f32[22,8,128]{2,1,0:T(8,128)S(1)} %get-tuple-element.14), channel_id=1, source_target_pairs={{0,28},{4,0},{8,4},{12,8},{16,12},{20,16},{24,20},{28,24},{1,29},{... | collective-permute-start | bytes 270344 | tf_op jit(solution)/shard_map/ppermute | solution.py:30
  50.3 5.5 %collective-permute-start.6 = (f32[8,128]{1,0:T(8,128)S(1)}, f32[8,128]{1,0:T(8,128)S(1)}, u32[]{:S(2)}, u32[]{:S(2)}) collective-permute-start(f32[8,128]{1,0:T(8,128)S(1)} %broadcast_in_dim.15), channel_id=1, source_target_pairs={{0,4},{4,0},{1,5},{5,1},{2,6},{6,2},{3,7},{7,3},{8,12},{12,8},{9,1... | collective-permute-start | bytes 12296 | tf_op jit(solution)/shard_map/ppermute | solution.py:30
  53.0 13.4 %collective-permute-start.4 = (f32[48,128]{1,0:T(8,128)S(1)}, f32[48,128]{1,0:T(8,128)S(1)}, u32[]{:S(2)}, u32[]{:S(2)}) collective-permute-start(f32[48,128]{1,0:T(8,128)S(1)} %get-tuple-element.15), channel_id=1, source_target_pairs={{0,1},{1,2},{2,3},{3,0},{4,5},{5,6},{6,7},{7,4},{8,9},{9,10},{10,1... | collective-permute-start | bytes 73736 | tf_op jit(solution)/shard_map/ppermute | solution.py:30
  53.4 13.1 %collective-permute-start.5 = (f32[48,128]{1,0:T(8,128)S(1)}, f32[48,128]{1,0:T(8,128)S(1)}, u32[]{:S(2)}, u32[]{:S(2)}) collective-permute-start(f32[48,128]{1,0:T(8,128)S(1)} %get-tuple-element.16), channel_id=1, source_target_pairs={{0,3},{1,0},{2,1},{3,2},{4,7},{5,4},{6,5},{7,6},{8,11},{9,8},{10,9... | collective-permute-start | bytes 73736 | tf_op jit(solution)/shard_map/ppermute | solution.py:30
  55.8 8.4 %collective-permute-start.9 = (f32[8,128]{1,0:T(8,128)S(1)}, f32[8,128]{1,0:T(8,128)S(1)}, u32[]{:S(2)}, u32[]{:S(2)}) collective-permute-start(f32[8,128]{1,0:T(8,128)S(1)} %broadcast_add_fusion.refs_0_), channel_id=1, source_target_pairs={{0,24},{8,0},{16,8},{24,16},{1,25},{9,1},{17,9},{25,17},{2,26},{10... | collective-permute-start | bytes 12296 | tf_op jit(solution)/shard_map/ppermute | solution.py:30
  59.9 6.4 %collective-permute-start.8 = (f32[8,128]{1,0:T(8,128)S(1)}, f32[8,128]{1,0:T(8,128)S(1)}, u32[]{:S(2)}, u32[]{:S(2)}) collective-permute-start(f32[8,128]{1,0:T(8,128)S(1)} %broadcast_add_fusion.refs_0_), channel_id=1, source_target_pairs={{0,16},{8,24},{16,0},{24,8},{1,17},{9,25},{17,1},{25,9},{2,18},{10... | collective-permute-start | bytes 12296 | tf_op jit(solution)/shard_map/ppermute | solution.py:30
  61.9 4.6 %collective-permute-start.7 = (f32[8,128]{1,0:T(8,128)S(1)}, f32[8,128]{1,0:T(8,128)S(1)}, u32[]{:S(2)}, u32[]{:S(2)}) collective-permute-start(f32[8,128]{1,0:T(8,128)S(1)} %broadcast_add_fusion.refs_0_), channel_id=1, source_target_pairs={{0,8},{8,16},{16,24},{24,0},{1,9},{9,17},{17,25},{25,1},{2,10},{10... | collective-permute-start | bytes 12296 | tf_op jit(solution)/shard_map/ppermute | solution.py:30

commit v7 on v3

--- a/solution.py
+++ b/solution.py
@@ -37,84 +37,119 @@
     return pltpu.with_memory_space_constraint(array, pltpu.HBM)
 
 
-def presum(partials, code_bits, group_map, base, chunks):
+def presum(partials, code_bits, group_map, base, blocks, segments):
     slots, nx, by, bz = partials.shape
-    rows = nx // chunks
+    length = nx // blocks
+    span = sum(count for _, count in segments)
+    pieces = len(segments)
 
     def kernel(base_ref, map_hbm, bits_hbm, part_ref, out_ref, buf, map_ref, bits_ref, sems):
-        map_copy = pltpu.make_async_copy(map_hbm, map_ref, sems.at[chunks])
-        bits_copy = pltpu.make_async_copy(bits_hbm, bits_ref, sems.at[chunks + 1])
+        map_copy = pltpu.make_async_copy(map_hbm, map_ref, sems.at[blocks * pieces])
+        bits_copy = pltpu.make_async_copy(bits_hbm, bits_ref, sems.at[blocks * pieces + 1])
         map_copy.start()
         bits_copy.start()
 
-        def copy(c):
-            part = pl.ds(c * rows, rows)
-            return pltpu.make_async_copy(part_ref.at[:, part], buf.at[:, part], sems.at[c])
-
-        for c in range(chunks):
-            copy(c).start()
+        def copy(d, k):
+            first, count = segments[k]
+            at = sum(c for _, c in segments[:k])
+            return pltpu.make_async_copy(
+                part_ref.at[:, pl.ds(d * length + first, count)],
+                buf.at[:, pl.ds(d * span + at, count)],
+                sems.at[d * pieces + k],
+            )
+
+        for d in range(blocks):
+            for k in range(pieces):
+                copy(d, k).start()
         map_copy.wait()
         bits_copy.wait()
         groups = [map_ref[base_ref[0] + s] for s in range(slots)]
-        for c in range(chunks):
-            copy(c).wait()
-
-            def row(i, carry):
-                x = c * rows + i
-                total = None
-                for s in range(slots):
-                    sign = (2 * bits_ref[groups[s], x] - 1).astype(F32)
-                    term = sign * buf[s, x]
-                    total = term if total is None else total + term
-                out_ref[x] = total
-                return carry
-
-            lax.fori_loop(0, rows, row, 0, unroll=4)
-
-    return pl.pallas_call(
-        kernel,
-        name="presum",
-        compiler_params=PARAMS,
-        out_shape=struct(nx, by, bz),
+
+        def block(d, carry):
+            row = d * span
+            for k, (first, count) in enumerate(segments):
+                copy(d, k).wait()
+                for i in range(count):
+                    total = None
+                    for s in range(slots):
+                        bit = bits_ref[groups[s], d * length + first + i]
+                        term = (2 * bit - 1).astype(F32) * buf[s, row]
+                        total = term if total is None else total + term
+                    out_ref[row] = total
+                    row = row + 1
+            return carry
+
+        lax.fori_loop(0, blocks, block, 0)
+
+    return pl.pallas_call(
+        kernel,
+        compiler_params=PARAMS,
+        out_shape=struct(blocks * span, by, bz),
         in_specs=[SMEM, HBM, HBM, HBM],
         out_specs=VMEM,
         scratch_shapes=[
-            pltpu.VMEM(partials.shape, F32),
+            pltpu.VMEM((slots, blocks * span, by, bz), F32),
             pltpu.SMEM(group_map.shape, jnp.int32),
             pltpu.SMEM(code_bits.shape, jnp.int32),
-            pltpu.SemaphoreType.DMA((chunks + 2,)),
+            pltpu.SemaphoreType.DMA((blocks * pieces + 2,)),
         ],
     )(base, in_hbm(group_map), in_hbm(code_bits), in_hbm(partials))
 
 
-def reduce_pack(parts, velocity, members):
+def member_sum(part_ref, i, span, members):
+    total = part_ref[i]
+    for m in range(1, members):
+        total = total + part_ref[m * span + i]
+    return total
+
+
+def reduce_edges(parts, velocity, members):
     bx, by, bz = velocity.shape
 
-    def kernel(part_ref, v_ref, g_ref, first_ref, last_ref, square_ref):
+    def kernel(part_ref, v_ref, first_ref, last_ref):
+        for i in range(HALO):
+            first_ref[i] = member_sum(part_ref, i, 2 * HALO, members)
+            first_ref[HALO + i] = v_ref[i]
+            last_ref[i] = member_sum(part_ref, HALO + i, 2 * HALO, members)
+            last_ref[HALO + i] = v_ref[bx - HALO + i]
+
+    edge = struct(2 * HALO, by, bz)
+    return pl.pallas_call(
+        kernel,
+        name="reduce_edges",
+        compiler_params=PARAMS,
+        out_shape=(edge, edge),
+        in_specs=[VMEM, VMEM],
+        out_specs=(VMEM,) * 2,
+    )(parts, velocity)
+
+
+def reduce_rest(parts, first_x, last_x, members):
+    _, by, bz = parts.shape
+    inner = parts.shape[0] // members
+    bx = inner + 2 * HALO
+
+    def kernel(part_ref, first_ref, last_ref, g_ref, square_ref):
         squares = jnp.zeros((by, bz), F32)
         for i in range(bx):
-            total = part_ref[i]
-            for m in range(1, members):
-                total = total + part_ref[m * bx + i]
+            if i < HALO:
+                total = first_ref[i]
+            elif i < bx - HALO:
+                total = member_sum(part_ref, i - HALO, inner, members)
+            else:
+                total = last_ref[i - bx + HALO]
             g_ref[i] = total
             squares = squares + total * total
-            if i < HALO:
-                first_ref[i] = total
-                first_ref[HALO + i] = v_ref[i]
-            if i >= bx - HALO:
-                last_ref[i - bx + HALO] = total
-                last_ref[i - bx + 2 * HALO] = v_ref[i]
         square_ref[...] = jnp.broadcast_to(jnp.sum(squares, axis=0, keepdims=True), (8, bz))
 
-    edge = struct(2 * HALO, by, bz)
-    return pl.pallas_call(
-        kernel,
-        name="reduce_pack",
-        compiler_params=PARAMS,
-        out_shape=(struct(bx, by, bz), edge, edge, struct(8, bz)),
-        in_specs=[VMEM, VMEM],
-        out_specs=(VMEM,) * 4,
-    )(parts, velocity)
+    return pl.pallas_call(
+        kernel,
+        name="reduce_rest",
+        compiler_params=PARAMS,
+        out_shape=(struct(bx, by, bz), struct(8, bz)),
+        in_specs=[VMEM] * 3,
+        out_specs=(VMEM,) * 2,
+    )(parts, first_x, last_x)
 
 
 def plane_of(main_ref, before_ref, after_ref, field, p, bx):
@@ -338,23 +373,28 @@
 
 
 def shards(partials, code_bits, group_map, velocity):
-    _, _, bz = velocity.shape
+    bx, _, bz = velocity.shape
     size_x, size_y, size_z = (lax.axis_size(axis) for axis in (GX, GY, "gz"))
     base = (lax.axis_index(GX) * partials.shape[0]).astype(jnp.int32).reshape(1)
     device = lax.axis_index(ALL).astype(jnp.int32).reshape(1)
 
-    local = presum(partials, code_bits, group_map, base, 8)
-    parts = lax.all_to_all(local, GX, split_axis=0, concat_axis=0, tiled=True)
-    gradient, first_x, last_x, squares = reduce_pack(parts, velocity, size_x)
-
+    bx = velocity.shape[0]
+    edge_layers = ((0, HALO), (bx - HALO, HALO))
+    inner_layers = ((HALO, bx - 2 * HALO),)
+    outer = presum(partials, code_bits, group_map, base, size_x, edge_layers)
+    outer = lax.all_to_all(outer, GX, split_axis=0, concat_axis=0, tiled=True)
+    inner = presum(partials, code_bits, group_map, base, size_x, inner_layers)
+    inner = lax.all_to_all(inner, GX, split_axis=0, concat_axis=0, tiled=True)
+    first_x, last_x = reduce_edges(outer, velocity, size_x)
     after_x = shift(first_x, GX, -1)
     before_x = shift(last_x, GX, 1)
-    table = jnp.broadcast_to(squares[:1][None], (size_x * size_y * size_z, 1, bz))
-    table = lax.all_to_all(table, ALL, split_axis=0, concat_axis=0, tiled=True)
-
+    gradient, squares = reduce_rest(inner, first_x, last_x, size_x)
     first_y, last_y = pack_y(gradient, velocity, before_x, after_x)
     after_y = shift(first_y, GY, -1)
     before_y = shift(last_y, GY, 1)
+
+    table = jnp.broadcast_to(squares[:1][None], (size_x * size_y * size_z, 1, bz))
+    table = lax.all_to_all(table, ALL, split_axis=0, concat_axis=0, tiled=True)
 
     first_z, last_z = pack_z(gradient, velocity, before_x, after_x, before_y, after_y)
     after_z = shift(first_z, "gz", -1)

time: 61.8 us -> 69.1 us (1.12)
  blocking collectives: 21 us -> 0 us
  waiting for transfers between devices: 10.1 us -> 24.9 us
  starting transfers between devices: 23.5 us -> 33.9 us
  Pallas kernels: 5.28 us -> 7.95 us
    all_to_all x1 -> x0, blocking collectives: 21 us -> none  [shards(): parts = lax.all_to_all(local, GX, split_axis=0, concat_axis=0, tiled=True)]
    all_to_all x0 -> x2, waiting for transfers between devices: none -> 14.8 us  [the longest x1 9.67 us: shards(): inner = lax.all_to_all(inner, GX, split_axis=0, concat_axis=0, tiled=True)]
    all_to_all x0 -> x2, starting transfers between devices: none -> 9.88 us  [the longest x1 6.34 us: shards(): outer = lax.all_to_all(outer, GX, split_axis=0, concat_axis=0, tiled=True)]
    pallas_call x2 -> x4, Pallas kernels: 2.49 us -> 5.16 us  [the longest x2 5.09 us: presum(): pl.pallas_call(kernel, compiler_params=PARAMS, out_shape=struct(blocks *...]
  transfers between devices with their start and end apart: 7 -> 9, of which waited for: 4 -> 6; matrix products, arithmetic and copies ran while one was open for 0% -> 0% of each run, Pallas kernels for 0% -> 4%
where the time goes in v7:
time: 69.1 us; the launch traced here: 68.2 us
  starting transfers between devices  33.9 us (49%)
  waiting for transfers between devices  24.9 us (36%)
  Pallas kernels  7.95 us (12%)
  local copies, waits for them, and re-layouts  0.74 us (1%)
  between operations  0.72 us (1%)
    all_to_all x1, starting transfers between devices, shards(): table = lax.all_to_all(table, ALL, split_axis=0, concat_axis=0, tiled=True)  13.7 us
    ppermute x6, starting transfers between devices, shift(): lax.ppermute(block, axis, [(i, (i + distance) % size) for i in range(size)])  10.3 us
    ppermute x6, waiting for transfers between devices, shift(): lax.ppermute(block, axis, [(i, (i + distance) % size) for i in range(size)])  10.1 us
    all_to_all x1, waiting for transfers between devices, shards(): inner = lax.all_to_all(inner, GX, split_axis=0, concat_axis=0, tiled=True)  9.67 us
    all_to_all x1, starting transfers between devices, shards(): outer = lax.all_to_all(outer, GX, split_axis=0, concat_axis=0, tiled=True)  6.34 us
    all_to_all x1, waiting for transfers between devices, shards(): outer = lax.all_to_all(outer, GX, split_axis=0, concat_axis=0, tiled=True)  5.14 us
    pallas_call x2, Pallas kernels, presum(): pl.pallas_call(kernel, compiler_params=PARAMS, out_shape=struct(blocks *...  5.09 us
    all_to_all x1, starting transfers between devices, shards(): inner = lax.all_to_all(inner, GX, split_axis=0, concat_axis=0, tiled=True)  3.54 us
  transfers between devices with their start and end apart: 9, of which 6 were waited for; matrix products, arithmetic and copies ran while one was open for 0% of the time, Pallas kernels for 4%

profile of v7, /device:TPU:1, one launch (start us, length us, event | category | flops | bytes accessed | tf_op | source)
XLA Modules:
  0.0 68.2 jit_solution(4849163789755783105)
XLA Ops:
  0.6 2.4 %shard_map.60 = f32[48,16,128]{2,1,0:T(8,128)} custom-call(s32[1]{0:T(128)} %bitcast.1.base_ref, s32[32]{0:T(128)} %map_hbm.3, s32[32,128]{1,0:T(8,128)} %bits_hbm.3, f32[4,128,16,128]{3,2,1,0:T(8,128)} %part_ref.3), custom_call_target="tpu_custom_call" | custom-call | tf_op jit(solution)/shard_map/pallas_call | solution.py:84
  3.1 0.0 copy-start
  3.1 6.3 %all-to-all-start.1 = ((f32[48,16,128]{2,1,0:T(8,128)}), f32[48,16,128]{2,1,0:T(8,128)S(1)}, u32[]{:S(2)}, u32[]{:S(2)}) async-start(f32[48,16,128]{2,1,0:T(8,128)} %shard_map.60), calls=%async_computation.1 | async-start | bytes 786432 | tf_op jit(solution)/shard_map/all_to_all | solution.py:385
  9.4 2.7 %shard_map.59 = f32[80,16,128]{2,1,0:T(8,128)} custom-call(s32[1]{0:T(128)} %bitcast.1.base_ref, s32[32]{0:T(128)} %map_hbm.3, s32[32,128]{1,0:T(8,128)} %bits_hbm.3, f32[4,128,16,128]{3,2,1,0:T(8,128)} %part_ref.3), custom_call_target="tpu_custom_call" | custom-call | tf_op jit(solution)/shard_map/pallas_call | solution.py:84
  12.1 5.1 %all-to-all-done.1.part_ref = f32[48,16,128]{2,1,0:T(8,128)S(1)} async-done(((f32[48,16,128]{2,1,0:T(8,128)}), f32[48,16,128]{2,1,0:T(8,128)S(1)}, u32[]{:S(2)}, u32[]{:S(2)}) %all-to-all-start.1) | async-done | bytes 393248 | tf_op jit(solution)/shard_map/all_to_all | solution.py:385
  17.2 3.5 %all-to-all-start = ((f32[80,16,128]{2,1,0:T(8,128)}), f32[80,16,128]{2,1,0:T(8,128)S(1)}, u32[]{:S(2)}, u32[]{:S(2)}) async-start(f32[80,16,128]{2,1,0:T(8,128)} %shard_map.59), calls=%async_computation | async-start | bytes 1310720 | tf_op jit(solution)/shard_map/all_to_all | solution.py:387
  20.8 0.0 copy-done
  20.8 9.7 %all-to-all-done.part_ref = f32[80,16,128]{2,1,0:T(8,128)S(1)} async-done(((f32[80,16,128]{2,1,0:T(8,128)}), f32[80,16,128]{2,1,0:T(8,128)S(1)}, u32[]{:S(2)}, u32[]{:S(2)}) %all-to-all-start) | async-done | bytes 655392 | tf_op jit(solution)/shard_map/all_to_all | solution.py:387
  30.5 0.7 %broadcast_in_dim.9 = f32[256,1,128]{2,1,0:T(1,128)} broadcast(f32[128]{0:T(128)S(1)} %slice_bitcast_fusion), dimensions={2} | broadcast | bytes 131584 | tf_op jit(solution)/shard_map/broadcast_in_dim | solution.py:396
  31.3 13.7 %all-to-all-start.2 = ((f32[256,1,128]{2,1,0:T(1,128)}), f32[256,1,128]{2,1,0:T(1,128)S(1)}, u32[]{:S(2)}, u32[]{:S(2)}) async-start(f32[256,1,128]{2,1,0:T(1,128)} %broadcast_in_dim.9), calls=%async_computation.2 | async-start | bytes 262144 | tf_op jit(solution)/shard_map/all_to_all | solution.py:397
  45.0 1.6 %collective-permute-start = (f32[6,16,128]{2,1,0:T(8,128)S(1)}, f32[6,16,128]{2,1,0:T(8,128)S(1)}, u32[]{:S(2)}, u32[]{:S(2)}) collective-permute-start(f32[6,16,128]{2,1,0:T(8,128)S(1)} %get-tuple-element.11.last_ref), channel_id=1, source_target_pairs={{0,32},{32,64},{64,96},{96,128},{128,160},{160,192},{192,224},{224... | collective-permute-start | bytes 147464 | tf_op jit(solution)/shard_map/ppermute | solution.py:29
  46.6 2.2 %collective-permute-start.1 = (f32[6,16,128]{2,1,0:T(8,128)S(1)}, f32[6,16,128]{2,1,0:T(8,128)S(1)}, u32[]{:S(2)}, u32[]{:S(2)}) collective-permute-start(f32[6,16,128]{2,1,0:T(8,128)S(1)} %get-tuple-element.10.first_ref), channel_id=1, source_target_pairs={{0,224},{32,0},{64,32},{96,64},{128,96},{160,128},{192,160},{224,1... | collective-permute-start | bytes 147464 | tf_op jit(solution)/shard_map/ppermute | solution.py:29
  48.8 2.8 %collective-permute-done.before_ref.bx_ref = f32[6,16,128]{2,1,0:T(8,128)S(1)} collective-permute-done((f32[6,16,128]{2,1,0:T(8,128)S(1)}, f32[6,16,128]{2,1,0:T(8,128)S(1)}, u32[]{:S(2)}, u32[]{:S(2)}) %collective-permute-start) | collective-permute-done | bytes 49184 | tf_op jit(solution)/shard_map/ppermute | solution.py:29
  51.6 0.0 collective-permute-done.1.after_ref.ax_ref
  51.6 3.7 %collective-permute-start.2 = (f32[22,8,128]{2,1,0:T(8,128)S(1)}, f32[22,8,128]{2,1,0:T(8,128)S(1)}, u32[]{:S(2)}, u32[]{:S(2)}) collective-permute-start(f32[22,8,128]{2,1,0:T(8,128)S(1)} %get-tuple-element.13), channel_id=1, source_target_pairs={{0,4},{4,8},{8,12},{12,16},{16,20},{20,24},{24,28},{28,0},{1,5},{5... | collective-permute-start | bytes 270344 | tf_op jit(solution)/shard_map/ppermute | solution.py:29
  55.4 0.0 collective-permute-start.3
  55.4 1.6 %collective-permute-done.2.by_ref = f32[22,8,128]{2,1,0:T(8,128)S(1)} collective-permute-done((f32[22,8,128]{2,1,0:T(8,128)S(1)}, f32[22,8,128]{2,1,0:T(8,128)S(1)}, u32[]{:S(2)}, u32[]{:S(2)}) %collective-permute-start.2) | collective-permute-done | bytes 90144 | tf_op jit(solution)/shard_map/ppermute | solution.py:29
  57.0 4.3 %collective-permute-done.3.ay_ref = f32[22,8,128]{2,1,0:T(8,128)S(1)} collective-permute-done((f32[22,8,128]{2,1,0:T(8,128)S(1)}, f32[22,8,128]{2,1,0:T(8,128)S(1)}, u32[]{:S(2)}, u32[]{:S(2)}) %collective-permute-start.3) | collective-permute-done | bytes 90144 | tf_op jit(solution)/shard_map/ppermute | solution.py:29
  61.2 0.2 pack_z.1
  61.4 1.4 %collective-permute-start.4 = (f32[48,128]{1,0:T(8,128)S(1)}, f32[48,128]{1,0:T(8,128)S(1)}, u32[]{:S(2)}, u32[]{:S(2)}) collective-permute-start(f32[48,128]{1,0:T(8,128)S(1)} %get-tuple-element.15), channel_id=1, source_target_pairs={{0,1},{1,2},{2,3},{3,0},{4,5},{5,6},{6,7},{7,4},{8,9},{9,10},{10,1... | collective-permute-start | bytes 73736 | tf_op jit(solution)/shard_map/ppermute | solution.py:29
  62.8 1.3 %collective-permute-start.5 = (f32[48,128]{1,0:T(8,128)S(1)}, f32[48,128]{1,0:T(8,128)S(1)}, u32[]{:S(2)}, u32[]{:S(2)}) collective-permute-start(f32[48,128]{1,0:T(8,128)S(1)} %get-tuple-element.16), channel_id=1, source_target_pairs={{0,3},{1,0},{2,1},{3,2},{4,7},{5,4},{6,5},{7,6},{8,11},{9,8},{10,9... | collective-permute-start | bytes 73736 | tf_op jit(solution)/shard_map/ppermute | solution.py:29
  64.2 1.5 %collective-permute-done.4.bz_ref = f32[48,128]{1,0:T(8,128)S(1)} collective-permute-done((f32[48,128]{1,0:T(8,128)S(1)}, f32[48,128]{1,0:T(8,128)S(1)}, u32[]{:S(2)}, u32[]{:S(2)}) %collective-permute-start.4) | collective-permute-done | bytes 24608 | tf_op jit(solution)/shard_map/ppermute | solution.py:29
  65.6 0.0 collective-permute-done.5.az_ref
  65.6 0.0 all-to-all-done.2.sq_ref
  65.6 2.6 %proximal.1 = (f32[16,16,128]{2,1,0:T(8,128)}, f32[16,16,128]{2,1,0:T(8,128)}) custom-call(s32[1]{0:T(128)} %bitcast.dev_ref, f32[16,16,128]{2,1,0:T(8,128)S(1)} %get-tuple-element.12.g_ref, f32[16,16,128]{2,1,0:T(8,128)S(1)} %copy-done, f32[6,16,128]{2,1,0:T(8,128)S(1)} %collective-permute-done.before_ref.bx_ref, ...), custom_call_target="tpu_custom_call" | custom-call | tf_op jit(solution)/shard_map/proximal/pallas_call | solution.py:364
  (4 shorter events, 0.1 us)
Async XLA Ops:
  3.1 17.7 %copy-start = (f32[16,16,128]{2,1,0:T(8,128)S(1)}, f32[16,16,128]{2,1,0:T(8,128)}, u32[]{:S(2)}) copy-start(f32[16,16,128]{2,1,0:T(8,128)} %v_ref.7) | copy-start | bytes 393220
  3.1 14.2 %all-to-all-start.1 = ((f32[48,16,128]{2,1,0:T(8,128)}), f32[48,16,128]{2,1,0:T(8,128)S(1)}, u32[]{:S(2)}, u32[]{:S(2)}) async-start(f32[48,16,128]{2,1,0:T(8,128)} %shard_map.60), calls=%async_computation.1 | async-start | bytes 786432 | tf_op jit(solution)/shard_map/all_to_all | solution.py:385
  17.2 13.3 %all-to-all-start = ((f32[80,16,128]{2,1,0:T(8,128)}), f32[80,16,128]{2,1,0:T(8,128)S(1)}, u32[]{:S(2)}, u32[]{:S(2)}) async-start(f32[80,16,128]{2,1,0:T(8,128)} %shard_map.59), calls=%async_computation | async-start | bytes 1310720 | tf_op jit(solution)/shard_map/all_to_all | solution.py:387
  31.3 34.4 %all-to-all-start.2 = ((f32[256,1,128]{2,1,0:T(1,128)}), f32[256,1,128]{2,1,0:T(1,128)S(1)}, u32[]{:S(2)}, u32[]{:S(2)}) async-start(f32[256,1,128]{2,1,0:T(1,128)} %broadcast_in_dim.9), calls=%async_computation.2 | async-start | bytes 262144 | tf_op jit(solution)/shard_map/all_to_all | solution.py:397
  45.0 6.6 %collective-permute-start = (f32[6,16,128]{2,1,0:T(8,128)S(1)}, f32[6,16,128]{2,1,0:T(8,128)S(1)}, u32[]{:S(2)}, u32[]{:S(2)}) collective-permute-start(f32[6,16,128]{2,1,0:T(8,128)S(1)} %get-tuple-element.11.last_ref), channel_id=1, source_target_pairs={{0,32},{32,64},{64,96},{96,128},{128,160},{160,192},{192,224},{224... | collective-permute-start | bytes 147464 | tf_op jit(solution)/shard_map/ppermute | solution.py:29
  46.6 5.0 %collective-permute-start.1 = (f32[6,16,128]{2,1,0:T(8,128)S(1)}, f32[6,16,128]{2,1,0:T(8,128)S(1)}, u32[]{:S(2)}, u32[]{:S(2)}) collective-permute-start(f32[6,16,128]{2,1,0:T(8,128)S(1)} %get-tuple-element.10.first_ref), channel_id=1, source_target_pairs={{0,224},{32,0},{64,32},{96,64},{128,96},{160,128},{192,160},{224,1... | collective-permute-start | bytes 147464 | tf_op jit(solution)/shard_map/ppermute | solution.py:29
  51.6 5.3 %collective-permute-start.2 = (f32[22,8,128]{2,1,0:T(8,128)S(1)}, f32[22,8,128]{2,1,0:T(8,128)S(1)}, u32[]{:S(2)}, u32[]{:S(2)}) collective-permute-start(f32[22,8,128]{2,1,0:T(8,128)S(1)} %get-tuple-element.13), channel_id=1, source_target_pairs={{0,4},{4,8},{8,12},{12,16},{16,20},{20,24},{24,28},{28,0},{1,5},{5... | collective-permute-start | bytes 270344 | tf_op jit(solution)/shard_map/ppermute | solution.py:29
  55.4 5.8 %collective-permute-start.3 = (f32[22,8,128]{2,1,0:T(8,128)S(1)}, f32[22,8,128]{2,1,0:T(8,128)S(1)}, u32[]{:S(2)}, u32[]{:S(2)}) collective-permute-start(f32[22,8,128]{2,1,0:T(8,128)S(1)} %get-tuple-element.14), channel_id=1, source_target_pairs={{0,28},{4,0},{8,4},{12,8},{16,12},{20,16},{24,20},{28,24},{1,29},{... | collective-permute-start | bytes 270344 | tf_op jit(solution)/shard_map/ppermute | solution.py:29
  61.4 4.2 %collective-permute-start.4 = (f32[48,128]{1,0:T(8,128)S(1)}, f32[48,128]{1,0:T(8,128)S(1)}, u32[]{:S(2)}, u32[]{:S(2)}) collective-permute-start(f32[48,128]{1,0:T(8,128)S(1)} %get-tuple-element.15), channel_id=1, source_target_pairs={{0,1},{1,2},{2,3},{3,0},{4,5},{5,6},{6,7},{7,4},{8,9},{9,10},{10,1... | collective-permute-start | bytes 73736 | tf_op jit(solution)/shard_map/ppermute | solution.py:29
  62.8 2.8 %collective-permute-start.5 = (f32[48,128]{1,0:T(8,128)S(1)}, f32[48,128]{1,0:T(8,128)S(1)}, u32[]{:S(2)}, u32[]{:S(2)}) collective-permute-start(f32[48,128]{1,0:T(8,128)S(1)} %get-tuple-element.16), channel_id=1, source_target_pairs={{0,3},{1,0},{2,1},{3,2},{4,7},{5,4},{6,5},{7,6},{8,11},{9,8},{10,9... | collective-permute-start | bytes 73736 | tf_op jit(solution)/shard_map/ppermute | solution.py:29

commit v8 on v3

--- a/solution.py
+++ b/solution.py
@@ -11,6 +11,7 @@
 GX = ("gx_0", "gx_1")
 GY = ("gy_0", "gy_1")
 ALL = GX + GY + ("gz",)
+XZ = GX + ("gz",)
 
 step_length = 0.5
 tv_weight = 0.2
@@ -24,9 +25,12 @@
 F32 = jnp.float32
 
 
-def shift(block, axis, distance):
+def swap(blocks, axis):
     size = lax.axis_size(axis)
-    return lax.ppermute(block, axis, [(i, (i + distance) % size) for i in range(size)])
+    pairs = [(i, i ^ 1) for i in range(size)]
+    others = [(i, ((i + 1) ^ 1) - 1) for i in range(size)]
+    others = [(i, j % size) for i, j in others]
+    return lax.ppermute(blocks[0], axis, pairs), lax.ppermute(blocks[1], axis, others)
 
 
 def struct(*shape):
@@ -37,11 +41,11 @@
     return pltpu.with_memory_space_constraint(array, pltpu.HBM)
 
 
-def presum(partials, code_bits, group_map, base, chunks):
+def presum(device, partials, code_bits, group_map, sizes, chunks):
     slots, nx, by, bz = partials.shape
     rows = nx // chunks
 
-    def kernel(base_ref, map_hbm, bits_hbm, part_ref, out_ref, buf, map_ref, bits_ref, sems):
+    def kernel(dev_ref, map_hbm, bits_hbm, part_ref, out_ref, buf, map_ref, bits_ref, sems):
         map_copy = pltpu.make_async_copy(map_hbm, map_ref, sems.at[chunks])
         bits_copy = pltpu.make_async_copy(bits_hbm, bits_ref, sems.at[chunks + 1])
         map_copy.start()
@@ -55,7 +59,8 @@
             copy(c).start()
         map_copy.wait()
         bits_copy.wait()
-        groups = [map_ref[base_ref[0] + s] for s in range(slots)]
+        base = position(dev_ref, sizes)[0] * slots
+        groups = [map_ref[base + s] for s in range(slots)]
         for c in range(chunks):
             copy(c).wait()
 
@@ -84,13 +89,25 @@
             pltpu.SMEM(code_bits.shape, jnp.int32),
             pltpu.SemaphoreType.DMA((chunks + 2,)),
         ],
-    )(base, in_hbm(group_map), in_hbm(code_bits), in_hbm(partials))
-
-
-def reduce_pack(parts, velocity, members):
+    )(device, in_hbm(group_map), in_hbm(code_bits), in_hbm(partials))
+
+
+def position(dev_ref, sizes):
+    _, size_y, size_z = sizes
+    dev = dev_ref[0]
+    return dev // (size_y * size_z), (dev // size_z) % size_y, dev % size_z
+
+
+def is_even(index):
+    return index % 2 == 0
+
+
+def reduce_pack(device, parts, velocity, sizes):
     bx, by, bz = velocity.shape
-
-    def kernel(part_ref, v_ref, g_ref, first_ref, last_ref, square_ref):
+    members = sizes[0]
+
+    def kernel(dev_ref, part_ref, v_ref, g_ref, near_ref, other_ref, square_ref):
+        even = is_even(position(dev_ref, sizes)[0])
         squares = jnp.zeros((by, bz), F32)
         for i in range(bx):
             total = part_ref[i]
@@ -98,12 +115,11 @@
                 total = total + part_ref[m * bx + i]
             g_ref[i] = total
             squares = squares + total * total
-            if i < HALO:
-                first_ref[i] = total
-                first_ref[HALO + i] = v_ref[i]
-            if i >= bx - HALO:
-                last_ref[i - bx + HALO] = total
-                last_ref[i - bx + 2 * HALO] = v_ref[i]
+        for i in range(HALO):
+            for k, ref in enumerate((g_ref, v_ref)):
+                first, last = ref[i], ref[bx - HALO + i]
+                near_ref[k * HALO + i] = jnp.where(even, last, first)
+                other_ref[k * HALO + i] = jnp.where(even, first, last)
         square_ref[...] = jnp.broadcast_to(jnp.sum(squares, axis=0, keepdims=True), (8, bz))
 
     edge = struct(2 * HALO, by, bz)
@@ -112,17 +128,20 @@
         name="reduce_pack",
         compiler_params=PARAMS,
         out_shape=(struct(bx, by, bz), edge, edge, struct(8, bz)),
-        in_specs=[VMEM, VMEM],
+        in_specs=[SMEM, VMEM, VMEM],
         out_specs=(VMEM,) * 4,
-    )(parts, velocity)
-
-
-def plane_of(main_ref, before_ref, after_ref, field, p, bx):
+    )(device, parts, velocity)
+
+
+def plane_of(main_ref, near_ref, other_ref, even, field, p):
+    bx = main_ref.shape[0]
     if p < HALO:
-        return before_ref[field * HALO + p]
+        at = field * HALO + p
+        return jnp.where(even, other_ref[at], near_ref[at])
     if p < HALO + bx:
         return main_ref[p - HALO]
-    return after_ref[field * HALO + p - HALO - bx]
+    at = field * HALO + p - HALO - bx
+    return jnp.where(even, near_ref[at], other_ref[at])
 
 
 def sublane(shape):
@@ -133,20 +152,21 @@
     return lax.broadcasted_iota(jnp.int32, shape, len(shape) - 1)
 
 
-def pack_y(gradient, velocity, before_x, after_x):
+def pack_y(device, gradient, velocity, halo_x, sizes):
     bx, by, bz = velocity.shape
     pairs = (bx + 2 * HALO) // 2
 
-    def kernel(g_ref, v_ref, before_ref, after_ref, first_ref, last_ref):
+    def kernel(dev_ref, g_ref, v_ref, nx_ref, ox_ref, near_ref, other_ref):
+        even_x, even_y = (is_even(i) for i in position(dev_ref, sizes)[:2])
         low = sublane((8, bz)) < 4
         for field, main in enumerate((g_ref, v_ref)):
             for q in range(pairs):
-                even = plane_of(main, before_ref, after_ref, field, 2 * q, bx)
-                odd = plane_of(main, before_ref, after_ref, field, 2 * q + 1, bx)
-                first_ref[field * pairs + q] = jnp.where(low, even[:8], pltpu.roll(odd[:8], 4, 0))
-                last_ref[field * pairs + q] = jnp.where(
-                    low, pltpu.roll(even[by - 8 :], 4, 0), odd[by - 8 :]
-                )
+                left = plane_of(main, nx_ref, ox_ref, even_x, field, 2 * q)
+                right = plane_of(main, nx_ref, ox_ref, even_x, field, 2 * q + 1)
+                first = jnp.where(low, left[:8], pltpu.roll(right[:8], 4, 0))
+                last = jnp.where(low, pltpu.roll(left[by - 8 :], 4, 0), right[by - 8 :])
+                near_ref[field * pairs + q] = jnp.where(even_y, last, first)
+                other_ref[field * pairs + q] = jnp.where(even_y, first, last)
 
     edge = struct(2 * pairs, 8, bz)
     return pl.pallas_call(
@@ -154,41 +174,44 @@
         name="pack_y",
         compiler_params=PARAMS,
         out_shape=(edge, edge),
-        in_specs=[VMEM] * 4,
+        in_specs=[SMEM] + [VMEM] * 4,
         out_specs=(VMEM,) * 2,
-    )(gradient, velocity, before_x, after_x)
-
-
-def rows_of(before_ref, after_ref, field, p, pairs):
-    after = after_ref[field * pairs + p // 2]
-    before = before_ref[field * pairs + p // 2]
-    low = sublane(after.shape) < 4
+    )(device, gradient, velocity, *halo_x)
+
+
+def rows_of(near_ref, other_ref, even, field, p, pairs):
+    near = near_ref[field * pairs + p // 2]
+    other = other_ref[field * pairs + p // 2]
+    low = sublane(near.shape) < 4
+    after = jnp.where(even, near, other)
+    before = jnp.where(even, other, near)
     if p % 2 == 0:
         return jnp.where(low, after, pltpu.roll(before, 4, 0))
     return jnp.where(low, pltpu.roll(after, 4, 0), before)
 
 
-def pack_z(gradient, velocity, before_x, after_x, before_y, after_y):
+def pack_z(device, gradient, velocity, halo_x, halo_y, sizes):
     bx, by, bz = velocity.shape
     planes = bx + 2 * HALO
     pairs = planes // 2
     groups = bz // 4
     tall = by + 8
 
-    def kernel(g_ref, v_ref, bx_ref, ax_ref, by_ref, ay_ref, first_ref, last_ref):
+    def kernel(dev_ref, g_ref, v_ref, nx_ref, ox_ref, ny_ref, oy_ref, near_ref, other_ref):
+        even_x, even_y, even_z = (is_even(i) for i in position(dev_ref, sizes))
         group = lane((tall, bz)) // 4
         for field, main in enumerate((g_ref, v_ref)):
             first = jnp.zeros((tall, bz), F32)
             last = jnp.zeros((tall, bz), F32)
             for p in range(planes):
-                own = plane_of(main, bx_ref, ax_ref, field, p, bx)
-                extra = rows_of(by_ref, ay_ref, field, p, pairs)
+                own = plane_of(main, nx_ref, ox_ref, even_x, field, p)
+                extra = rows_of(ny_ref, oy_ref, even_y, field, p, pairs)
                 plane = jnp.concatenate([own, extra], 0)
                 turned = pltpu.roll(plane, 4 * p, 1) if p else plane
                 first = jnp.where(group == p, turned, first)
                 last = jnp.where(group == (p - 1) % groups, turned, last)
-            first_ref[pl.ds(field * tall, tall)] = first
-            last_ref[pl.ds(field * tall, tall)] = last
+            near_ref[pl.ds(field * tall, tall)] = jnp.where(even_z, last, first)
+            other_ref[pl.ds(field * tall, tall)] = jnp.where(even_z, first, last)
 
     edge = struct(2 * tall, bz)
     return pl.pallas_call(
@@ -196,9 +219,9 @@
         name="pack_z",
         compiler_params=PARAMS,
         out_shape=(edge, edge),
-        in_specs=[VMEM] * 6,
+        in_specs=[SMEM] + [VMEM] * 6,
         out_specs=(VMEM,) * 2,
-    )(gradient, velocity, before_x, after_x, before_y, after_y)
+    )(device, gradient, velocity, *halo_x, *halo_y)
 
 
 def proximal(device, gradient, velocity, halos, squares, sizes):
@@ -214,12 +237,12 @@
         dev_ref,
         g_ref,
         v_ref,
-        bx_ref,
-        ax_ref,
-        by_ref,
-        ay_ref,
-        bz_ref,
-        az_ref,
+        nx_ref,
+        ox_ref,
+        ny_ref,
+        oy_ref,
+        nz_ref,
+        oz_ref,
         sq_ref,
         gradient_ref,
         model_ref,
@@ -234,25 +257,27 @@
     ):
         gradient_copy = pltpu.make_async_copy(g_ref, gradient_ref, sems.at[0])
         gradient_copy.start()
-        dev = dev_ref[0]
-        pos_z = dev % size_z
-        pos_y = (dev // size_z) % size_y
-        pos_x = dev // (size_z * size_y)
+        pos_x, pos_y, pos_z = position(dev_ref, sizes)
+        even_x, even_y, even_z = (is_even(i) for i in (pos_x, pos_y, pos_z))
 
         total = jnp.sum(jnp.sum(sq_ref[...], axis=0), axis=1, keepdims=True)
         scale = step_length * lax.rsqrt(total / cells + 1.0)
         scale = jnp.broadcast_to(scale, (1, bz))
 
         side_lane = lane((tall, bz)) < bz // 2
-        before_z = bz_ref[pl.ds(tall, tall)] - scale * bz_ref[pl.ds(0, tall)]
-        after_z = az_ref[pl.ds(tall, tall)] - scale * az_ref[pl.ds(0, tall)]
+        near_z = nz_ref[pl.ds(tall, tall)] - scale * nz_ref[pl.ds(0, tall)]
+        other_z = oz_ref[pl.ds(tall, tall)] - scale * oz_ref[pl.ds(0, tall)]
+        before_z = jnp.where(even_z, other_z, near_z)
+        after_z = jnp.where(even_z, near_z, other_z)
         for p in range(planes):
-            own = plane_of(v_ref, bx_ref, ax_ref, 1, p, bx) - scale * plane_of(
-                g_ref, bx_ref, ax_ref, 0, p, bx
+            own, rows = (
+                [
+                    plane_of(main, nx_ref, ox_ref, even_x, field, p),
+                    rows_of(ny_ref, oy_ref, even_y, field, p, pairs),
+                ]
+                for field, main in ((1, v_ref), (0, g_ref))
             )
-            rows = rows_of(by_ref, ay_ref, 1, p, pairs) - scale * rows_of(
-                by_ref, ay_ref, 0, p, pairs
-            )
+            own, rows = (own[0] - scale * rows[0], own[1] - scale * rows[1])
             back = (bz - 4 * p) % bz
             after = pltpu.roll(after_z, back, 1) if back else after_z
             before = pltpu.roll(before_z, back, 1) if back else before_z
@@ -338,36 +363,23 @@
 
 
 def shards(partials, code_bits, group_map, velocity):
-    _, _, bz = velocity.shape
-    size_x, size_y, size_z = (lax.axis_size(axis) for axis in (GX, GY, "gz"))
-    base = (lax.axis_index(GX) * partials.shape[0]).astype(jnp.int32).reshape(1)
+    sizes = tuple(lax.axis_size(axis) for axis in (GX, GY, "gz"))
     device = lax.axis_index(ALL).astype(jnp.int32).reshape(1)
 
-    local = presum(partials, code_bits, group_map, base, 8)
+    local = presum(device, partials, code_bits, group_map, sizes, 8)
     parts = lax.all_to_all(local, GX, split_axis=0, concat_axis=0, tiled=True)
-    gradient, first_x, last_x, squares = reduce_pack(parts, velocity, size_x)
-
-    after_x = shift(first_x, GX, -1)
-    before_x = shift(last_x, GX, 1)
-    table = jnp.broadcast_to(squares[:1][None], (size_x * size_y * size_z, 1, bz))
-    table = lax.all_to_all(table, ALL, split_axis=0, concat_axis=0, tiled=True)
-
-    first_y, last_y = pack_y(gradient, velocity, before_x, after_x)
-    after_y = shift(first_y, GY, -1)
-    before_y = shift(last_y, GY, 1)
-
-    first_z, last_z = pack_z(gradient, velocity, before_x, after_x, before_y, after_y)
-    after_z = shift(first_z, "gz", -1)
-    before_z = shift(last_z, "gz", 1)
-
-    return proximal(
-        device,
-        gradient,
-        velocity,
-        (before_x, after_x, before_y, after_y, before_z, after_z),
-        table,
-        (size_x, size_y, size_z),
-    )
+    gradient, *send_x, squares = reduce_pack(device, parts, velocity, sizes)
+    halo_x = swap(send_x, GX)
+    table = jnp.broadcast_to(squares[:1][None], (sizes[0] * sizes[2], 1, squares.shape[1]))
+    table = lax.all_to_all(table, XZ, split_axis=0, concat_axis=0, tiled=True)
+    send_y = pack_y(device, gradient, velocity, halo_x, sizes)
+    halo_y = swap(send_y, GY)
+    table = jnp.broadcast_to(jnp.sum(table, axis=0, keepdims=True), (sizes[1], 1, squares.shape[1]))
+    table = lax.all_to_all(table, GY, split_axis=0, concat_axis=0, tiled=True)
+    send_z = pack_z(device, gradient, velocity, halo_x, halo_y, sizes)
+    halo_z = swap(send_z, "gz")
+    halos = (*halo_x, *halo_y, *halo_z)
+    return proximal(device, gradient, velocity, halos, table, sizes)
 
 
 def solution(mesh):

time: 61.8 us -> 67.7 us (1.095)
  blocking collectives: 21 us -> 34.5 us
  starting transfers between devices: 23.5 us -> 16.2 us
  Pallas kernels: 5.28 us -> 7.4 us
  waiting for transfers between devices: 10.1 us -> 8.03 us
    all_to_all x0 -> x1, blocking collectives: none -> 13.5 us  [shards(): table = lax.all_to_all(table, GY, split_axis=0, concat_axis=0, tiled=True)]
    all_to_all x1, starting transfers between devices: 13.2 us -> 5.51 us  [shards(): table = lax.all_to_all(table, XZ, split_axis=0, concat_axis=0, tiled=True)]
    ppermute x6, waiting for transfers between devices: 10.1 us -> 4.28 us  [the longest x3 2.99 us: swap(): lax.ppermute(blocks[1], axis, others)]
    all_to_all x1, waiting for transfers between devices: 0.01 us -> 3.75 us  [shards(): table = lax.all_to_all(table, XZ, split_axis=0, concat_axis=0, tiled=True)]
    pallas_call x1, Pallas kernels: 2.57 us -> 4.66 us  [proximal(): pl.pallas_call(kernel, name='proximal', compiler_params=PARAMS, out_shape...]
  transfers between devices with their start and end apart: 7 -> 7, of which waited for: 4 -> 3; matrix products, arithmetic and copies ran while one was open for 0% -> 1% of each run, Pallas kernels for 0% -> 0%
where the time goes in v8:
time: 67.7 us; the launch traced here: 67.5 us
  blocking collectives  34.5 us (51%)
  starting transfers between devices  16.2 us (24%)
  waiting for transfers between devices  8.03 us (12%)
  Pallas kernels  7.4 us (11%)
  between operations  0.7 us (1%)
    all_to_all x1, blocking collectives, shards(): parts = lax.all_to_all(local, GX, split_axis=0, concat_axis=0, tiled=True)  21 us
    all_to_all x1, blocking collectives, shards(): table = lax.all_to_all(table, GY, split_axis=0, concat_axis=0, tiled=True)  13.5 us
    ppermute x3, starting transfers between devices, swap(): lax.ppermute(blocks[1], axis, others)  5.98 us
    all_to_all x1, starting transfers between devices, shards(): table = lax.all_to_all(table, XZ, split_axis=0, concat_axis=0, tiled=True)  5.51 us
    ppermute x3, starting transfers between devices, swap(): lax.ppermute(blocks[0], axis, pairs)  4.74 us
    pallas_call x1, Pallas kernels, proximal(): pl.pallas_call(kernel, name='proximal', compiler_params=PARAMS, out_shape...  4.66 us
    all_to_all x1, waiting for transfers between devices, shards(): table = lax.all_to_all(table, XZ, split_axis=0, concat_axis=0, tiled=True)  3.75 us
    ppermute x3, waiting for transfers between devices, swap(): lax.ppermute(blocks[1], axis, others)  2.99 us
  transfers between devices with their start and end apart: 7, of which 3 were waited for; matrix products, arithmetic and copies ran while one was open for 1% of the time, Pallas kernels for 0%

profile of v8, /device:TPU:1, one launch (start us, length us, event | category | flops | bytes accessed | tf_op | source)
XLA Modules:
  0.0 67.5 jit_solution(8161837428447048410)
XLA Ops:
  0.6 0.0 copy-start
  0.7 2.4 %presum.1 = f32[128,16,128]{2,1,0:T(8,128)S(1)} custom-call(s32[1]{0:T(128)} %bitcast.dev_ref, s32[32]{0:T(128)} %map_hbm.1, s32[32,128]{1,0:T(8,128)} %bits_hbm.1, f32[4,128,16,128]{3,2,1,0:T(8,128)} %part_ref.1), custom_call_target="tpu_custom_call" | custom-call | tf_op jit(solution)/shard_map/presum/pallas_call | solution.py:79
  3.1 21.0 %all_to_all.15.part_ref = f32[128,16,128]{2,1,0:T(8,128)S(1)} all-to-all(f32[128,16,128]{2,1,0:T(8,128)S(1)} %presum.1), channel_id=1, replica_groups=mesh['gx_0'=4,'gx_1'=2,'gy_0'=4,'gy_1'=2,'gz'=4] {'gx_0','gx_1'}, dimensions={0} | all-to-all | bytes 2097152 | tf_op jit(solution)/shard_map/all_to_all | solution.py:370
  24.1 0.0 copy-done
  24.1 0.1 reduce_pack.1
  24.1 0.5 collective-permute-start
  24.7 1.2 %collective-permute-start.1 = (f32[6,16,128]{2,1,0:T(8,128)S(1)}, f32[6,16,128]{2,1,0:T(8,128)S(1)}, u32[]{:S(2)}, u32[]{:S(2)}) collective-permute-start(f32[6,16,128]{2,1,0:T(8,128)S(1)} %get-tuple-element.12), channel_id=1, source_target_pairs={{0,224},{32,64},{64,32},{96,128},{128,96},{160,192},{192,160},{224... | collective-permute-start | bytes 147464 | tf_op jit(solution)/shard_map/ppermute | solution.py:33
  25.9 1.3 %collective-permute-done.nx_ref = f32[6,16,128]{2,1,0:T(8,128)S(1)} collective-permute-done((f32[6,16,128]{2,1,0:T(8,128)S(1)}, f32[6,16,128]{2,1,0:T(8,128)S(1)}, u32[]{:S(2)}, u32[]{:S(2)}) %collective-permute-start) | collective-permute-done | bytes 49184 | tf_op jit(solution)/shard_map/ppermute | solution.py:33
  27.2 3.0 %collective-permute-done.1.ox_ref = f32[6,16,128]{2,1,0:T(8,128)S(1)} collective-permute-done((f32[6,16,128]{2,1,0:T(8,128)S(1)}, f32[6,16,128]{2,1,0:T(8,128)S(1)}, u32[]{:S(2)}, u32[]{:S(2)}) %collective-permute-start.1) | collective-permute-done | bytes 49184 | tf_op jit(solution)/shard_map/ppermute | solution.py:33
  30.2 2.9 %collective-permute-start.2 = (f32[22,8,128]{2,1,0:T(8,128)S(1)}, f32[22,8,128]{2,1,0:T(8,128)S(1)}, u32[]{:S(2)}, u32[]{:S(2)}) collective-permute-start(f32[22,8,128]{2,1,0:T(8,128)S(1)} %get-tuple-element.13), channel_id=1, source_target_pairs={{0,4},{4,0},{8,12},{12,8},{16,20},{20,16},{24,28},{28,24},{1,5},{5... | collective-permute-start | bytes 270344 | tf_op jit(solution)/shard_map/ppermute | solution.py:33
  33.1 3.0 %collective-permute-start.3 = (f32[22,8,128]{2,1,0:T(8,128)S(1)}, f32[22,8,128]{2,1,0:T(8,128)S(1)}, u32[]{:S(2)}, u32[]{:S(2)}) collective-permute-start(f32[22,8,128]{2,1,0:T(8,128)S(1)} %get-tuple-element.14), channel_id=1, source_target_pairs={{0,28},{4,8},{8,4},{12,16},{16,12},{20,24},{24,20},{28,0},{1,29},{... | collective-permute-start | bytes 270344 | tf_op jit(solution)/shard_map/ppermute | solution.py:33
  36.0 0.6 broadcast_in_dim.7
  36.7 5.5 %all-to-all-start.1 = ((f32[32,1,128]{2,1,0:T(1,128)}), f32[32,1,128]{2,1,0:T(1,128)S(1)}, u32[]{:S(2)}, u32[]{:S(2)}) async-start(f32[32,1,128]{2,1,0:T(1,128)} %broadcast_in_dim.7), calls=%async_computation.1 | async-start | bytes 32768 | tf_op jit(solution)/shard_map/all_to_all | solution.py:374
  42.2 0.0 collective-permute-done.2.ny_ref
  42.2 0.0 collective-permute-done.3.oy_ref
  42.2 0.2 pack_z.1
  42.4 1.3 %collective-permute-start.4 = (f32[48,128]{1,0:T(8,128)S(1)}, f32[48,128]{1,0:T(8,128)S(1)}, u32[]{:S(2)}, u32[]{:S(2)}) collective-permute-start(f32[48,128]{1,0:T(8,128)S(1)} %get-tuple-element.15), channel_id=1, source_target_pairs={{0,1},{1,0},{2,3},{3,2},{4,5},{5,4},{6,7},{7,6},{8,9},{9,8},{10,11... | collective-permute-start | bytes 73736 | tf_op jit(solution)/shard_map/ppermute | solution.py:33
  43.7 1.8 %collective-permute-start.5 = (f32[48,128]{1,0:T(8,128)S(1)}, f32[48,128]{1,0:T(8,128)S(1)}, u32[]{:S(2)}, u32[]{:S(2)}) collective-permute-start(f32[48,128]{1,0:T(8,128)S(1)} %get-tuple-element.16), channel_id=1, source_target_pairs={{0,3},{1,2},{2,1},{3,0},{4,7},{5,6},{6,5},{7,4},{8,11},{9,10},{10,... | collective-permute-start | bytes 73736 | tf_op jit(solution)/shard_map/ppermute | solution.py:33
  45.5 3.8 %all-to-all-done.1 = f32[32,1,128]{2,1,0:T(1,128)S(1)} async-done(((f32[32,1,128]{2,1,0:T(1,128)}), f32[32,1,128]{2,1,0:T(1,128)S(1)}, u32[]{:S(2)}, u32[]{:S(2)}) %all-to-all-start.1) | async-done | bytes 16416 | tf_op jit(solution)/shard_map/all_to_all | solution.py:374
  49.3 13.5 %all_to_all.16.sq_ref = f32[8,1,128]{2,1,0:T(1,128)S(1)} all-to-all(f32[8,1,128]{2,1,0:T(1,128)S(1)} %broadcast_in_dim.16), channel_id=1, replica_groups=mesh['gx_0'=4,'gx_1'=2,'gy_0'=4,'gy_1'=2,'gz'=4] {'gy_0','gy_1'}, dimensions={0} | all-to-all | bytes 8192 | tf_op jit(solution)/shard_map/all_to_all | solution.py:378
  62.8 0.0 collective-permute-done.4.nz_ref
  62.8 0.0 collective-permute-done.5.oz_ref
  62.8 4.7 %proximal.1 = (f32[16,16,128]{2,1,0:T(8,128)}, f32[16,16,128]{2,1,0:T(8,128)}) custom-call(s32[1]{0:T(128)} %bitcast.dev_ref, f32[16,16,128]{2,1,0:T(8,128)S(1)} %get-tuple-element.10.g_ref, f32[16,16,128]{2,1,0:T(8,128)S(1)} %copy-done, f32[6,16,128]{2,1,0:T(8,128)S(1)} %collective-permute-done.nx_ref, f32[6,16,128]{2,1,0:T(8,128)S(1)} %collective-permute-done.1.ox_ref, ...), custom_call_target="tpu_custom_call" | custom-call | tf_op jit(solution)/shard_map/proximal/pallas_call | solution.py:354
  (4 shorter events, 0.1 us)
Async XLA Ops:
  0.6 23.4 %copy-start = (f32[16,16,128]{2,1,0:T(8,128)S(1)}, f32[16,16,128]{2,1,0:T(8,128)}, u32[]{:S(2)}) copy-start(f32[16,16,128]{2,1,0:T(8,128)} %v_ref.7) | copy-start | bytes 393220
  24.1 3.0 %collective-permute-start = (f32[6,16,128]{2,1,0:T(8,128)S(1)}, f32[6,16,128]{2,1,0:T(8,128)S(1)}, u32[]{:S(2)}, u32[]{:S(2)}) collective-permute-start(f32[6,16,128]{2,1,0:T(8,128)S(1)} %get-tuple-element.11), channel_id=1, source_target_pairs={{0,32},{32,0},{64,96},{96,64},{128,160},{160,128},{192,224},{224,1... | collective-permute-start | bytes 147464 | tf_op jit(solution)/shard_map/ppermute | solution.py:33
  24.7 5.5 %collective-permute-start.1 = (f32[6,16,128]{2,1,0:T(8,128)S(1)}, f32[6,16,128]{2,1,0:T(8,128)S(1)}, u32[]{:S(2)}, u32[]{:S(2)}) collective-permute-start(f32[6,16,128]{2,1,0:T(8,128)S(1)} %get-tuple-element.12), channel_id=1, source_target_pairs={{0,224},{32,64},{64,32},{96,128},{128,96},{160,192},{192,160},{224... | collective-permute-start | bytes 147464 | tf_op jit(solution)/shard_map/ppermute | solution.py:33
  30.2 12.0 %collective-permute-start.2 = (f32[22,8,128]{2,1,0:T(8,128)S(1)}, f32[22,8,128]{2,1,0:T(8,128)S(1)}, u32[]{:S(2)}, u32[]{:S(2)}) collective-permute-start(f32[22,8,128]{2,1,0:T(8,128)S(1)} %get-tuple-element.13), channel_id=1, source_target_pairs={{0,4},{4,0},{8,12},{12,8},{16,20},{20,16},{24,28},{28,24},{1,5},{5... | collective-permute-start | bytes 270344 | tf_op jit(solution)/shard_map/ppermute | solution.py:33
  33.1 9.1 %collective-permute-start.3 = (f32[22,8,128]{2,1,0:T(8,128)S(1)}, f32[22,8,128]{2,1,0:T(8,128)S(1)}, u32[]{:S(2)}, u32[]{:S(2)}) collective-permute-start(f32[22,8,128]{2,1,0:T(8,128)S(1)} %get-tuple-element.14), channel_id=1, source_target_pairs={{0,28},{4,8},{8,4},{12,16},{16,12},{20,24},{24,20},{28,0},{1,29},{... | collective-permute-start | bytes 270344 | tf_op jit(solution)/shard_map/ppermute | solution.py:33
  36.7 12.6 %all-to-all-start.1 = ((f32[32,1,128]{2,1,0:T(1,128)}), f32[32,1,128]{2,1,0:T(1,128)S(1)}, u32[]{:S(2)}, u32[]{:S(2)}) async-start(f32[32,1,128]{2,1,0:T(1,128)} %broadcast_in_dim.7), calls=%async_computation.1 | async-start | bytes 32768 | tf_op jit(solution)/shard_map/all_to_all | solution.py:374
  42.4 20.4 %collective-permute-start.4 = (f32[48,128]{1,0:T(8,128)S(1)}, f32[48,128]{1,0:T(8,128)S(1)}, u32[]{:S(2)}, u32[]{:S(2)}) collective-permute-start(f32[48,128]{1,0:T(8,128)S(1)} %get-tuple-element.15), channel_id=1, source_target_pairs={{0,1},{1,0},{2,3},{3,2},{4,5},{5,4},{6,7},{7,6},{8,9},{9,8},{10,11... | collective-permute-start | bytes 73736 | tf_op jit(solution)/shard_map/ppermute | solution.py:33
  43.7 19.1 %collective-permute-start.5 = (f32[48,128]{1,0:T(8,128)S(1)}, f32[48,128]{1,0:T(8,128)S(1)}, u32[]{:S(2)}, u32[]{:S(2)}) collective-permute-start(f32[48,128]{1,0:T(8,128)S(1)} %get-tuple-element.16), channel_id=1, source_target_pairs={{0,3},{1,2},{2,1},{3,0},{4,7},{5,6},{6,5},{7,4},{8,11},{9,10},{10,... | collective-permute-start | bytes 73736 | tf_op jit(solution)/shard_map/ppermute | solution.py:33

commit v9 on v8

--- a/solution.py
+++ b/solution.py
@@ -11,7 +11,6 @@
 GX = ("gx_0", "gx_1")
 GY = ("gy_0", "gy_1")
 ALL = GX + GY + ("gz",)
-XZ = GX + ("gz",)
 
 step_length = 0.5
 tv_weight = 0.2
@@ -28,8 +27,7 @@
 def swap(blocks, axis):
     size = lax.axis_size(axis)
     pairs = [(i, i ^ 1) for i in range(size)]
-    others = [(i, ((i + 1) ^ 1) - 1) for i in range(size)]
-    others = [(i, j % size) for i, j in others]
+    others = [(i, min(max(((i + 1) ^ 1) - 1, 0), size - 1)) for i in range(size)]
     return lax.ppermute(blocks[0], axis, pairs), lax.ppermute(blocks[1], axis, others)
 
 
@@ -370,12 +368,12 @@
     parts = lax.all_to_all(local, GX, split_axis=0, concat_axis=0, tiled=True)
     gradient, *send_x, squares = reduce_pack(device, parts, velocity, sizes)
     halo_x = swap(send_x, GX)
-    table = jnp.broadcast_to(squares[:1][None], (sizes[0] * sizes[2], 1, squares.shape[1]))
-    table = lax.all_to_all(table, XZ, split_axis=0, concat_axis=0, tiled=True)
+    table = jnp.broadcast_to(
+        squares[:1][None], (sizes[0] * sizes[1] * sizes[2], 1, squares.shape[1])
+    )
+    table = lax.all_to_all(table, ALL, split_axis=0, concat_axis=0, tiled=True)
     send_y = pack_y(device, gradient, velocity, halo_x, sizes)
     halo_y = swap(send_y, GY)
-    table = jnp.broadcast_to(jnp.sum(table, axis=0, keepdims=True), (sizes[1], 1, squares.shape[1]))
-    table = lax.all_to_all(table, GY, split_axis=0, concat_axis=0, tiled=True)
     send_z = pack_z(device, gradient, velocity, halo_x, halo_y, sizes)
     halo_z = swap(send_z, "gz")
     halos = (*halo_x, *halo_y, *halo_z)

time: 67.7 us -> 63.3 us (0.935)
  the two profiles are of different devices: /device:TPU:1 before, /device:TPU:83 now
where the time goes in v9:
time: 63.3 us; the launch traced here: 63 us
  starting transfers between devices  27.1 us (43%)
  blocking collectives  18.5 us (29%)
  waiting for transfers between devices  10.6 us (17%)
  Pallas kernels  5.32 us (8%)
  local copies, waits for them, and re-layouts  0.73 us (1%)
  between operations  0.72 us (1%)
    all_to_all x1, blocking collectives, shards(): parts = lax.all_to_all(local, GX, split_axis=0, concat_axis=0, tiled=True)  18.5 us
    all_to_all x1, starting transfers between devices, shards(): table = lax.all_to_all(table, ALL, split_axis=0, concat_axis=0, tiled=True)  14.4 us
    ppermute x3, waiting for transfers between devices, swap(): lax.ppermute(blocks[1], axis, others)  10.4 us
    ppermute x3, starting transfers between devices, swap(): lax.ppermute(blocks[1], axis, others)  8.56 us
    ppermute x3, starting transfers between devices, swap(): lax.ppermute(blocks[0], axis, pairs)  4.18 us
    pallas_call x1, Pallas kernels, proximal(): pl.pallas_call(kernel, name='proximal', compiler_params=PARAMS, out_shape...  2.58 us
    pallas_call x1, Pallas kernels, presum(): pl.pallas_call(kernel, name='presum', compiler_params=PARAMS, out_shape=s...  2.43 us
  transfers between devices with their start and end apart: 7, of which 4 were waited for; matrix products, arithmetic and copies ran while one was open for 0% of the time, Pallas kernels for 0%

profile of v9, /device:TPU:83, one launch (start us, length us, event | category | flops | bytes accessed | tf_op | source)
XLA Modules:
  0.0 63.0 jit_solution(9582750707395198435)
XLA Ops:
  0.6 0.0 copy-start
  0.7 2.4 %presum.1 = f32[128,16,128]{2,1,0:T(8,128)S(1)} custom-call(s32[1]{0:T(128)} %bitcast.dev_ref, s32[32]{0:T(128)} %map_hbm.1, s32[32,128]{1,0:T(8,128)} %bits_hbm.1, f32[4,128,16,128]{3,2,1,0:T(8,128)} %part_ref.1), custom_call_target="tpu_custom_call" | custom-call | tf_op jit(solution)/shard_map/presum/pallas_call | solution.py:77
  3.1 18.5 %all_to_all.10.part_ref = f32[128,16,128]{2,1,0:T(8,128)S(1)} all-to-all(f32[128,16,128]{2,1,0:T(8,128)S(1)} %presum.1), channel_id=1, replica_groups=mesh['gx_0'=4,'gx_1'=2,'gy_0'=4,'gy_1'=2,'gz'=4] {'gx_0','gx_1'}, dimensions={0} | all-to-all | bytes 2097152 | tf_op jit(solution)/shard_map/all_to_all | solution.py:368
  21.6 0.0 copy-done
  21.6 0.1 reduce_pack.1
  21.6 0.7 %broadcast_in_dim.9 = f32[256,1,128]{2,1,0:T(1,128)} broadcast(f32[128]{0:T(128)S(1)} %slice_bitcast_fusion), dimensions={2} | broadcast | bytes 131584 | tf_op jit(solution)/shard_map/broadcast_in_dim | solution.py:371
  22.4 14.4 %all-to-all-start.1 = ((f32[256,1,128]{2,1,0:T(1,128)}), f32[256,1,128]{2,1,0:T(1,128)S(1)}, u32[]{:S(2)}, u32[]{:S(2)}) async-start(f32[256,1,128]{2,1,0:T(1,128)} %broadcast_in_dim.9), calls=%async_computation.1 | async-start | bytes 262144 | tf_op jit(solution)/shard_map/all_to_all | solution.py:374
  36.8 1.5 %collective-permute-start = (f32[6,16,128]{2,1,0:T(8,128)S(1)}, f32[6,16,128]{2,1,0:T(8,128)S(1)}, u32[]{:S(2)}, u32[]{:S(2)}) collective-permute-start(f32[6,16,128]{2,1,0:T(8,128)S(1)} %get-tuple-element.11), channel_id=1, source_target_pairs={{0,32},{32,0},{64,96},{96,64},{128,160},{160,128},{192,224},{224,1... | collective-permute-start | bytes 147464 | tf_op jit(solution)/shard_map/ppermute | solution.py:31
  38.3 1.9 %collective-permute-start.1 = (f32[6,16,128]{2,1,0:T(8,128)S(1)}, f32[6,16,128]{2,1,0:T(8,128)S(1)}, u32[]{:S(2)}, u32[]{:S(2)}) collective-permute-start(f32[6,16,128]{2,1,0:T(8,128)S(1)} %get-tuple-element.12), channel_id=1, source_target_pairs={{0,0},{32,64},{64,32},{96,128},{128,96},{160,192},{192,160},{224,2... | collective-permute-start | bytes 147464 | tf_op jit(solution)/shard_map/ppermute | solution.py:31
  40.2 0.2 collective-permute-done.nx_ref
  40.5 3.9 %collective-permute-done.1.ox_ref = f32[6,16,128]{2,1,0:T(8,128)S(1)} collective-permute-done((f32[6,16,128]{2,1,0:T(8,128)S(1)}, f32[6,16,128]{2,1,0:T(8,128)S(1)}, u32[]{:S(2)}, u32[]{:S(2)}) %collective-permute-start.1) | collective-permute-done | bytes 49184 | tf_op jit(solution)/shard_map/ppermute | solution.py:31
  44.4 1.6 %collective-permute-start.2 = (f32[22,8,128]{2,1,0:T(8,128)S(1)}, f32[22,8,128]{2,1,0:T(8,128)S(1)}, u32[]{:S(2)}, u32[]{:S(2)}) collective-permute-start(f32[22,8,128]{2,1,0:T(8,128)S(1)} %get-tuple-element.13), channel_id=1, source_target_pairs={{0,4},{4,0},{8,12},{12,8},{16,20},{20,16},{24,28},{28,24},{1,5},{5... | collective-permute-start | bytes 270344 | tf_op jit(solution)/shard_map/ppermute | solution.py:31
  46.0 4.7 %collective-permute-start.3 = (f32[22,8,128]{2,1,0:T(8,128)S(1)}, f32[22,8,128]{2,1,0:T(8,128)S(1)}, u32[]{:S(2)}, u32[]{:S(2)}) collective-permute-start(f32[22,8,128]{2,1,0:T(8,128)S(1)} %get-tuple-element.14), channel_id=1, source_target_pairs={{0,0},{4,8},{8,4},{12,16},{16,12},{20,24},{24,20},{28,28},{1,1},{5... | collective-permute-start | bytes 270344 | tf_op jit(solution)/shard_map/ppermute | solution.py:31
  50.7 0.0 collective-permute-done.2.ny_ref
  50.7 3.9 %collective-permute-done.3.oy_ref = f32[22,8,128]{2,1,0:T(8,128)S(1)} collective-permute-done((f32[22,8,128]{2,1,0:T(8,128)S(1)}, f32[22,8,128]{2,1,0:T(8,128)S(1)}, u32[]{:S(2)}, u32[]{:S(2)}) %collective-permute-start.3) | collective-permute-done | bytes 90144 | tf_op jit(solution)/shard_map/ppermute | solution.py:31
  54.6 0.2 pack_z.1
  54.8 1.0 %collective-permute-start.4 = (f32[48,128]{1,0:T(8,128)S(1)}, f32[48,128]{1,0:T(8,128)S(1)}, u32[]{:S(2)}, u32[]{:S(2)}) collective-permute-start(f32[48,128]{1,0:T(8,128)S(1)} %get-tuple-element.15), channel_id=1, source_target_pairs={{0,1},{1,0},{2,3},{3,2},{4,5},{5,4},{6,7},{7,6},{8,9},{9,8},{10,11... | collective-permute-start | bytes 73736 | tf_op jit(solution)/shard_map/ppermute | solution.py:31
  55.9 1.9 %collective-permute-start.5 = (f32[48,128]{1,0:T(8,128)S(1)}, f32[48,128]{1,0:T(8,128)S(1)}, u32[]{:S(2)}, u32[]{:S(2)}) collective-permute-start(f32[48,128]{1,0:T(8,128)S(1)} %get-tuple-element.16), channel_id=1, source_target_pairs={{0,0},{1,2},{2,1},{3,3},{4,4},{5,6},{6,5},{7,7},{8,8},{9,10},{10,9... | collective-permute-start | bytes 73736 | tf_op jit(solution)/shard_map/ppermute | solution.py:31
  57.8 0.0 collective-permute-done.4.nz_ref
  57.8 2.6 %collective-permute-done.5.oz_ref = f32[48,128]{1,0:T(8,128)S(1)} collective-permute-done((f32[48,128]{1,0:T(8,128)S(1)}, f32[48,128]{1,0:T(8,128)S(1)}, u32[]{:S(2)}, u32[]{:S(2)}) %collective-permute-start.5) | collective-permute-done | bytes 24608 | tf_op jit(solution)/shard_map/ppermute | solution.py:31
  60.4 0.0 all-to-all-done.1.sq_ref
  60.4 2.6 %proximal.1 = (f32[16,16,128]{2,1,0:T(8,128)}, f32[16,16,128]{2,1,0:T(8,128)}) custom-call(s32[1]{0:T(128)} %bitcast.dev_ref, f32[16,16,128]{2,1,0:T(8,128)S(1)} %get-tuple-element.10.g_ref, f32[16,16,128]{2,1,0:T(8,128)S(1)} %copy-done, f32[6,16,128]{2,1,0:T(8,128)S(1)} %collective-permute-done.nx_ref, f32[6,16,128]{2,1,0:T(8,128)S(1)} %collective-permute-done.1.ox_ref, ...), custom_call_target="tpu_custom_call" | custom-call | tf_op jit(solution)/shard_map/proximal/pallas_call | solution.py:352
  (2 shorter events, 0.0 us)
Async XLA Ops:
  0.6 20.9 %copy-start = (f32[16,16,128]{2,1,0:T(8,128)S(1)}, f32[16,16,128]{2,1,0:T(8,128)}, u32[]{:S(2)}) copy-start(f32[16,16,128]{2,1,0:T(8,128)} %v_ref.7) | copy-start | bytes 393220
  22.4 38.1 %all-to-all-start.1 = ((f32[256,1,128]{2,1,0:T(1,128)}), f32[256,1,128]{2,1,0:T(1,128)S(1)}, u32[]{:S(2)}, u32[]{:S(2)}) async-start(f32[256,1,128]{2,1,0:T(1,128)} %broadcast_in_dim.9), calls=%async_computation.1 | async-start | bytes 262144 | tf_op jit(solution)/shard_map/all_to_all | solution.py:374
  36.8 3.7 %collective-permute-start = (f32[6,16,128]{2,1,0:T(8,128)S(1)}, f32[6,16,128]{2,1,0:T(8,128)S(1)}, u32[]{:S(2)}, u32[]{:S(2)}) collective-permute-start(f32[6,16,128]{2,1,0:T(8,128)S(1)} %get-tuple-element.11), channel_id=1, source_target_pairs={{0,32},{32,0},{64,96},{96,64},{128,160},{160,128},{192,224},{224,1... | collective-permute-start | bytes 147464 | tf_op jit(solution)/shard_map/ppermute | solution.py:31
  38.3 6.0 %collective-permute-start.1 = (f32[6,16,128]{2,1,0:T(8,128)S(1)}, f32[6,16,128]{2,1,0:T(8,128)S(1)}, u32[]{:S(2)}, u32[]{:S(2)}) collective-permute-start(f32[6,16,128]{2,1,0:T(8,128)S(1)} %get-tuple-element.12), channel_id=1, source_target_pairs={{0,0},{32,64},{64,32},{96,128},{128,96},{160,192},{192,160},{224,2... | collective-permute-start | bytes 147464 | tf_op jit(solution)/shard_map/ppermute | solution.py:31
  44.4 6.4 %collective-permute-start.2 = (f32[22,8,128]{2,1,0:T(8,128)S(1)}, f32[22,8,128]{2,1,0:T(8,128)S(1)}, u32[]{:S(2)}, u32[]{:S(2)}) collective-permute-start(f32[22,8,128]{2,1,0:T(8,128)S(1)} %get-tuple-element.13), channel_id=1, source_target_pairs={{0,4},{4,0},{8,12},{12,8},{16,20},{20,16},{24,28},{28,24},{1,5},{5... | collective-permute-start | bytes 270344 | tf_op jit(solution)/shard_map/ppermute | solution.py:31
  46.0 8.7 %collective-permute-start.3 = (f32[22,8,128]{2,1,0:T(8,128)S(1)}, f32[22,8,128]{2,1,0:T(8,128)S(1)}, u32[]{:S(2)}, u32[]{:S(2)}) collective-permute-start(f32[22,8,128]{2,1,0:T(8,128)S(1)} %get-tuple-element.14), channel_id=1, source_target_pairs={{0,0},{4,8},{8,4},{12,16},{16,12},{20,24},{24,20},{28,28},{1,1},{5... | collective-permute-start | bytes 270344 | tf_op jit(solution)/shard_map/ppermute | solution.py:31
  54.8 3.0 %collective-permute-start.4 = (f32[48,128]{1,0:T(8,128)S(1)}, f32[48,128]{1,0:T(8,128)S(1)}, u32[]{:S(2)}, u32[]{:S(2)}) collective-permute-start(f32[48,128]{1,0:T(8,128)S(1)} %get-tuple-element.15), channel_id=1, source_target_pairs={{0,1},{1,0},{2,3},{3,2},{4,5},{5,4},{6,7},{7,6},{8,9},{9,8},{10,11... | collective-permute-start | bytes 73736 | tf_op jit(solution)/shard_map/ppermute | solution.py:31
  55.9 4.6 %collective-permute-start.5 = (f32[48,128]{1,0:T(8,128)S(1)}, f32[48,128]{1,0:T(8,128)S(1)}, u32[]{:S(2)}, u32[]{:S(2)}) collective-permute-start(f32[48,128]{1,0:T(8,128)S(1)} %get-tuple-element.16), channel_id=1, source_target_pairs={{0,0},{1,2},{2,1},{3,3},{4,4},{5,6},{6,5},{7,7},{8,8},{9,10},{10,9... | collective-permute-start | bytes 73736 | tf_op jit(solution)/shard_map/ppermute | solution.py:31

commit v10 on v9

--- a/solution.py
+++ b/solution.py
@@ -24,11 +24,22 @@
 F32 = jnp.float32
 
 
-def swap(blocks, axis):
-    size = lax.axis_size(axis)
+def swap(blocks, axis, spare):
+    size, width = lax.axis_size(axis), lax.axis_size(spare)
     pairs = [(i, i ^ 1) for i in range(size)]
-    others = [(i, min(max(((i + 1) ^ 1) - 1, 0), size - 1)) for i in range(size)]
-    return lax.ppermute(blocks[0], axis, pairs), lax.ppermute(blocks[1], axis, others)
+    axes = axis if isinstance(axis, tuple) else (axis,)
+    ahead = ALL.index(spare) < ALL.index(axes[0])
+
+    def at(i, k):
+        return k * size + i if ahead else i * width + k
+
+    others = []
+    for i in range(size):
+        j = ((i + 1) ^ 1) - 1
+        for k in range(width):
+            others.append((at(i, k), at(j, k) if 0 <= j < size else at(i, k ^ 1)))
+    both = (spare, *axes) if ahead else (*axes, spare)
+    return lax.ppermute(blocks[0], axis, pairs), lax.ppermute(blocks[1], both, others)
 
 
 def struct(*shape):
@@ -367,15 +378,15 @@
     local = presum(device, partials, code_bits, group_map, sizes, 8)
     parts = lax.all_to_all(local, GX, split_axis=0, concat_axis=0, tiled=True)
     gradient, *send_x, squares = reduce_pack(device, parts, velocity, sizes)
-    halo_x = swap(send_x, GX)
+    halo_x = swap(send_x, GX, GY[1])
     table = jnp.broadcast_to(
         squares[:1][None], (sizes[0] * sizes[1] * sizes[2], 1, squares.shape[1])
     )
     table = lax.all_to_all(table, ALL, split_axis=0, concat_axis=0, tiled=True)
     send_y = pack_y(device, gradient, velocity, halo_x, sizes)
-    halo_y = swap(send_y, GY)
+    halo_y = swap(send_y, GY, "gz")
     send_z = pack_z(device, gradient, velocity, halo_x, halo_y, sizes)
-    halo_z = swap(send_z, "gz")
+    halo_z = swap(send_z, "gz", GY[1])
     halos = (*halo_x, *halo_y, *halo_z)
     return proximal(device, gradient, velocity, halos, table, sizes)
 

time: 63.3 us -> 57.9 us (0.915)
  starting transfers between devices: 27.1 us -> 21.1 us
  waiting for transfers between devices: 10.6 us -> 11.4 us
    ppermute x3, starting transfers between devices: 8.56 us -> 2.91 us  [swap(): lax.ppermute(blocks[1], both, others)]
    ppermute x3, waiting for transfers between devices: 0.25 us -> 3.82 us  [swap(): lax.ppermute(blocks[0], axis, pairs)]
    ppermute x3, waiting for transfers between devices: 10.4 us -> 7.56 us  [swap(): lax.ppermute(blocks[1], both, others)]
  transfers between devices with their start and end apart: 7 -> 7, of which waited for: 4 -> 5; matrix products, arithmetic and copies ran while one was open for 0% -> 0% of each run, Pallas kernels for 0% -> 0%
where the time goes in v10:
time: 57.9 us; the launch traced here: 57.7 us
  starting transfers between devices  21.1 us (36%)
  blocking collectives  18.5 us (32%)
  waiting for transfers between devices  11.4 us (20%)
  Pallas kernels  5.32 us (9%)
  local copies, waits for them, and re-layouts  0.73 us (1%)
  between operations  0.69 us (1%)
    all_to_all x1, blocking collectives, shards(): parts = lax.all_to_all(local, GX, split_axis=0, concat_axis=0, tiled=True)  18.5 us
    all_to_all x1, starting transfers between devices, shards(): table = lax.all_to_all(table, ALL, split_axis=0, concat_axis=0, tiled=True)  14.4 us
    ppermute x3, waiting for transfers between devices, swap(): lax.ppermute(blocks[1], both, others)  7.56 us
    ppermute x3, starting transfers between devices, swap(): lax.ppermute(blocks[0], axis, pairs)  3.84 us
    ppermute x3, waiting for transfers between devices, swap(): lax.ppermute(blocks[0], axis, pairs)  3.82 us
    ppermute x3, starting transfers between devices, swap(): lax.ppermute(blocks[1], both, others)  2.91 us
    pallas_call x1, Pallas kernels, proximal(): pl.pallas_call(kernel, name='proximal', compiler_params=PARAMS, out_shape...  2.58 us
    pallas_call x1, Pallas kernels, presum(): pl.pallas_call(kernel, name='presum', compiler_params=PARAMS, out_shape=s...  2.43 us
  transfers between devices with their start and end apart: 7, of which 5 were waited for; matrix products, arithmetic and copies ran while one was open for 0% of the time, Pallas kernels for 0%

profile of v10, /device:TPU:83, one launch (start us, length us, event | category | flops | bytes accessed | tf_op | source)
XLA Modules:
  0.0 57.7 jit_solution(6337689765277139955)
XLA Ops:
  0.6 0.0 copy-start
  0.7 2.4 %presum.1 = f32[128,16,128]{2,1,0:T(8,128)S(1)} custom-call(s32[1]{0:T(128)} %bitcast.dev_ref, s32[32]{0:T(128)} %map_hbm.1, s32[32,128]{1,0:T(8,128)} %bits_hbm.1, f32[4,128,16,128]{3,2,1,0:T(8,128)} %part_ref.1), custom_call_target="tpu_custom_call" | custom-call | tf_op jit(solution)/shard_map/presum/pallas_call | solution.py:88
  3.1 18.5 %all_to_all.10.part_ref = f32[128,16,128]{2,1,0:T(8,128)S(1)} all-to-all(f32[128,16,128]{2,1,0:T(8,128)S(1)} %presum.1), channel_id=1, replica_groups=mesh['gx_0'=4,'gx_1'=2,'gy_0'=4,'gy_1'=2,'gz'=4] {'gx_0','gx_1'}, dimensions={0} | all-to-all | bytes 2097152 | tf_op jit(solution)/shard_map/all_to_all | solution.py:379
  21.6 0.0 copy-done
  21.6 0.1 reduce_pack.1
  21.6 0.7 %broadcast_in_dim.9 = f32[256,1,128]{2,1,0:T(1,128)} broadcast(f32[128]{0:T(128)S(1)} %slice_bitcast_fusion), dimensions={2} | broadcast | bytes 131584 | tf_op jit(solution)/shard_map/broadcast_in_dim | solution.py:382
  22.4 14.4 %all-to-all-start.1 = ((f32[256,1,128]{2,1,0:T(1,128)}), f32[256,1,128]{2,1,0:T(1,128)S(1)}, u32[]{:S(2)}, u32[]{:S(2)}) async-start(f32[256,1,128]{2,1,0:T(1,128)} %broadcast_in_dim.9), calls=%async_computation.1 | async-start | bytes 262144 | tf_op jit(solution)/shard_map/all_to_all | solution.py:385
  36.8 1.5 %collective-permute-start = (f32[6,16,128]{2,1,0:T(8,128)S(1)}, f32[6,16,128]{2,1,0:T(8,128)S(1)}, u32[]{:S(2)}, u32[]{:S(2)}) collective-permute-start(f32[6,16,128]{2,1,0:T(8,128)S(1)} %get-tuple-element.11), channel_id=1, source_target_pairs={{0,32},{32,0},{64,96},{96,64},{128,160},{160,128},{192,224},{224,1... | collective-permute-start | bytes 147464 | tf_op jit(solution)/shard_map/ppermute | solution.py:42
  38.3 0.1 collective-permute-start.1
  38.4 2.1 %collective-permute-done.nx_ref = f32[6,16,128]{2,1,0:T(8,128)S(1)} collective-permute-done((f32[6,16,128]{2,1,0:T(8,128)S(1)}, f32[6,16,128]{2,1,0:T(8,128)S(1)}, u32[]{:S(2)}, u32[]{:S(2)}) %collective-permute-start) | collective-permute-done | bytes 49184 | tf_op jit(solution)/shard_map/ppermute | solution.py:42
  40.5 2.4 %collective-permute-done.1.ox_ref = f32[6,16,128]{2,1,0:T(8,128)S(1)} collective-permute-done((f32[6,16,128]{2,1,0:T(8,128)S(1)}, f32[6,16,128]{2,1,0:T(8,128)S(1)}, u32[]{:S(2)}, u32[]{:S(2)}) %collective-permute-start.1) | collective-permute-done | bytes 49184 | tf_op jit(solution)/shard_map/ppermute | solution.py:42
  42.9 1.3 %collective-permute-start.2 = (f32[22,8,128]{2,1,0:T(8,128)S(1)}, f32[22,8,128]{2,1,0:T(8,128)S(1)}, u32[]{:S(2)}, u32[]{:S(2)}) collective-permute-start(f32[22,8,128]{2,1,0:T(8,128)S(1)} %get-tuple-element.13), channel_id=1, source_target_pairs={{0,4},{4,0},{8,12},{12,8},{16,20},{20,16},{24,28},{28,24},{1,5},{5... | collective-permute-start | bytes 270344 | tf_op jit(solution)/shard_map/ppermute | solution.py:42
  44.2 2.8 %collective-permute-start.3 = (f32[22,8,128]{2,1,0:T(8,128)S(1)}, f32[22,8,128]{2,1,0:T(8,128)S(1)}, u32[]{:S(2)}, u32[]{:S(2)}) collective-permute-start(f32[22,8,128]{2,1,0:T(8,128)S(1)} %get-tuple-element.14), channel_id=1, source_target_pairs={{0,1},{1,0},{2,3},{3,2},{4,8},{5,9},{6,10},{7,11},{8,4},{9,5},{10,... | collective-permute-start | bytes 270344 | tf_op jit(solution)/shard_map/ppermute | solution.py:42
  47.0 0.0 collective-permute-done.2.ny_ref
  47.0 4.2 %collective-permute-done.3.oy_ref = f32[22,8,128]{2,1,0:T(8,128)S(1)} collective-permute-done((f32[22,8,128]{2,1,0:T(8,128)S(1)}, f32[22,8,128]{2,1,0:T(8,128)S(1)}, u32[]{:S(2)}, u32[]{:S(2)}) %collective-permute-start.3) | collective-permute-done | bytes 90144 | tf_op jit(solution)/shard_map/ppermute | solution.py:42
  51.2 0.2 pack_z.1
  51.4 1.0 %collective-permute-start.4 = (f32[48,128]{1,0:T(8,128)S(1)}, f32[48,128]{1,0:T(8,128)S(1)}, u32[]{:S(2)}, u32[]{:S(2)}) collective-permute-start(f32[48,128]{1,0:T(8,128)S(1)} %get-tuple-element.15), channel_id=1, source_target_pairs={{0,1},{1,0},{2,3},{3,2},{4,5},{5,4},{6,7},{7,6},{8,9},{9,8},{10,11... | collective-permute-start | bytes 73736 | tf_op jit(solution)/shard_map/ppermute | solution.py:42
  52.5 0.0 collective-permute-start.5
  52.5 1.7 %collective-permute-done.4.nz_ref = f32[48,128]{1,0:T(8,128)S(1)} collective-permute-done((f32[48,128]{1,0:T(8,128)S(1)}, f32[48,128]{1,0:T(8,128)S(1)}, u32[]{:S(2)}, u32[]{:S(2)}) %collective-permute-start.4) | collective-permute-done | bytes 24608 | tf_op jit(solution)/shard_map/ppermute | solution.py:42
  54.2 0.9 %collective-permute-done.5.oz_ref = f32[48,128]{1,0:T(8,128)S(1)} collective-permute-done((f32[48,128]{1,0:T(8,128)S(1)}, f32[48,128]{1,0:T(8,128)S(1)}, u32[]{:S(2)}, u32[]{:S(2)}) %collective-permute-start.5) | collective-permute-done | bytes 24608 | tf_op jit(solution)/shard_map/ppermute | solution.py:42
  55.1 0.0 all-to-all-done.1.sq_ref
  55.1 2.6 %proximal.1 = (f32[16,16,128]{2,1,0:T(8,128)}, f32[16,16,128]{2,1,0:T(8,128)}) custom-call(s32[1]{0:T(128)} %bitcast.dev_ref, f32[16,16,128]{2,1,0:T(8,128)S(1)} %get-tuple-element.10.g_ref, f32[16,16,128]{2,1,0:T(8,128)S(1)} %copy-done, f32[6,16,128]{2,1,0:T(8,128)S(1)} %collective-permute-done.nx_ref, f32[6,16,128]{2,1,0:T(8,128)S(1)} %collective-permute-done.1.ox_ref, ...), custom_call_target="tpu_custom_call" | custom-call | tf_op jit(solution)/shard_map/proximal/pallas_call | solution.py:363
  (2 shorter events, 0.0 us)
Async XLA Ops:
  0.6 20.9 %copy-start = (f32[16,16,128]{2,1,0:T(8,128)S(1)}, f32[16,16,128]{2,1,0:T(8,128)}, u32[]{:S(2)}) copy-start(f32[16,16,128]{2,1,0:T(8,128)} %v_ref.7) | copy-start | bytes 393220
  22.4 32.8 %all-to-all-start.1 = ((f32[256,1,128]{2,1,0:T(1,128)}), f32[256,1,128]{2,1,0:T(1,128)S(1)}, u32[]{:S(2)}, u32[]{:S(2)}) async-start(f32[256,1,128]{2,1,0:T(1,128)} %broadcast_in_dim.9), calls=%async_computation.1 | async-start | bytes 262144 | tf_op jit(solution)/shard_map/all_to_all | solution.py:385
  36.8 3.7 %collective-permute-start = (f32[6,16,128]{2,1,0:T(8,128)S(1)}, f32[6,16,128]{2,1,0:T(8,128)S(1)}, u32[]{:S(2)}, u32[]{:S(2)}) collective-permute-start(f32[6,16,128]{2,1,0:T(8,128)S(1)} %get-tuple-element.11), channel_id=1, source_target_pairs={{0,32},{32,0},{64,96},{96,64},{128,160},{160,128},{192,224},{224,1... | collective-permute-start | bytes 147464 | tf_op jit(solution)/shard_map/ppermute | solution.py:42
  38.3 4.6 %collective-permute-start.1 = (f32[6,16,128]{2,1,0:T(8,128)S(1)}, f32[6,16,128]{2,1,0:T(8,128)S(1)}, u32[]{:S(2)}, u32[]{:S(2)}) collective-permute-start(f32[6,16,128]{2,1,0:T(8,128)S(1)} %get-tuple-element.12), channel_id=1, source_target_pairs={{0,4},{4,0},{32,64},{36,68},{64,32},{68,36},{96,128},{100,132},{12... | collective-permute-start | bytes 147464 | tf_op jit(solution)/shard_map/ppermute | solution.py:42
  42.9 4.1 %collective-permute-start.2 = (f32[22,8,128]{2,1,0:T(8,128)S(1)}, f32[22,8,128]{2,1,0:T(8,128)S(1)}, u32[]{:S(2)}, u32[]{:S(2)}) collective-permute-start(f32[22,8,128]{2,1,0:T(8,128)S(1)} %get-tuple-element.13), channel_id=1, source_target_pairs={{0,4},{4,0},{8,12},{12,8},{16,20},{20,16},{24,28},{28,24},{1,5},{5... | collective-permute-start | bytes 270344 | tf_op jit(solution)/shard_map/ppermute | solution.py:42
  44.2 7.0 %collective-permute-start.3 = (f32[22,8,128]{2,1,0:T(8,128)S(1)}, f32[22,8,128]{2,1,0:T(8,128)S(1)}, u32[]{:S(2)}, u32[]{:S(2)}) collective-permute-start(f32[22,8,128]{2,1,0:T(8,128)S(1)} %get-tuple-element.14), channel_id=1, source_target_pairs={{0,1},{1,0},{2,3},{3,2},{4,8},{5,9},{6,10},{7,11},{8,4},{9,5},{10,... | collective-permute-start | bytes 270344 | tf_op jit(solution)/shard_map/ppermute | solution.py:42
  51.4 2.8 %collective-permute-start.4 = (f32[48,128]{1,0:T(8,128)S(1)}, f32[48,128]{1,0:T(8,128)S(1)}, u32[]{:S(2)}, u32[]{:S(2)}) collective-permute-start(f32[48,128]{1,0:T(8,128)S(1)} %get-tuple-element.15), channel_id=1, source_target_pairs={{0,1},{1,0},{2,3},{3,2},{4,5},{5,4},{6,7},{7,6},{8,9},{9,8},{10,11... | collective-permute-start | bytes 73736 | tf_op jit(solution)/shard_map/ppermute | solution.py:42
  52.5 2.7 %collective-permute-start.5 = (f32[48,128]{1,0:T(8,128)S(1)}, f32[48,128]{1,0:T(8,128)S(1)}, u32[]{:S(2)}, u32[]{:S(2)}) collective-permute-start(f32[48,128]{1,0:T(8,128)S(1)} %get-tuple-element.16), channel_id=1, source_target_pairs={{0,4},{4,0},{1,2},{5,6},{2,1},{6,5},{3,7},{7,3},{8,12},{12,8},{9,1... | collective-permute-start | bytes 73736 | tf_op jit(solution)/shard_map/ppermute | solution.py:42

commit v11 on v10

--- a/solution.py
+++ b/solution.py
@@ -11,6 +11,7 @@
 GX = ("gx_0", "gx_1")
 GY = ("gy_0", "gy_1")
 ALL = GX + GY + ("gz",)
+XZ = GX + ("gz",)
 
 step_length = 0.5
 tv_weight = 0.2
@@ -40,6 +41,11 @@
             others.append((at(i, k), at(j, k) if 0 <= j < size else at(i, k ^ 1)))
     both = (spare, *axes) if ahead else (*axes, spare)
     return lax.ppermute(blocks[0], axis, pairs), lax.ppermute(blocks[1], both, others)
+
+
+def add_pairs(row, axis, partner):
+    size = lax.axis_size(axis)
+    return row + lax.ppermute(row, axis, [(i, partner(i, size)) for i in range(size)])
 
 
 def struct(*shape):
@@ -269,7 +275,7 @@
         pos_x, pos_y, pos_z = position(dev_ref, sizes)
         even_x, even_y, even_z = (is_even(i) for i in (pos_x, pos_y, pos_z))
 
-        total = jnp.sum(jnp.sum(sq_ref[...], axis=0), axis=1, keepdims=True)
+        total = jnp.sum(sq_ref[0:1], axis=1, keepdims=True)
         scale = step_length * lax.rsqrt(total / cells + 1.0)
         scale = jnp.broadcast_to(scale, (1, bz))
 
@@ -310,13 +316,10 @@
             first = iteration == 0
             final = iteration == ITERS - 1
             here_ref = target if first else extra
-            ahead = here_ref[iteration]
-            before_x = None
-            for p in range(iteration, planes - 1 - iteration):
-                here = ahead
+
+            def plane(p, here, before_x, first=first, final=final, here_ref=here_ref):
                 ahead = here_ref[p + 1]
-                index = pos_x * bx + (p - HALO)
-                factor_x = factor(index, size_x * bx)
+                factor_x = factor(pos_x * bx + (p - HALO), size_x * bx)
                 dx = factor_x * (ahead - here)
                 dy = factor_y * (pltpu.roll(here, tall - 1, 0) - here)
                 dz = factor_z * (pltpu.roll(here, wide - 1, 1) - here)
@@ -333,27 +336,39 @@
                     dual_x[p] = dx
                     dual_y[p] = dy
                     dual_z[p] = dz
-                if p > iteration:
-                    if final:
+                if final:
+                    if before_x is not None:
                         spread = dx[:by, :bz] - before_x
                         spread += dy[:by, :bz] - pltpu.roll(dy[:, :bz], 1, 0)[:by]
                         spread += dz[:by, :bz] - pltpu.roll(dz[:by], 1, 1)[:, :bz]
                         goal = target[p, pl.ds(0, by), pl.ds(0, bz)]
                         old = current[p, pl.ds(0, by), pl.ds(0, bz)]
                         model[p - HALO] = shrink * old + gain * (spread + goal)
+                    return ahead, dx[:by, :bz]
+                if before_x is not None:
+                    spread = dx - before_x
+                    spread += dy - pltpu.roll(dy, 1, 0)
+                    spread += dz - pltpu.roll(dz, 1, 1)
+                    if first:
+                        new = here + gain * spread
+                        old = here
                     else:
-                        spread = dx - before_x
-                        spread += dy - pltpu.roll(dy, 1, 0)
-                        spread += dz - pltpu.roll(dz, 1, 1)
-                        if first:
-                            new = here + gain * spread
-                            old = here
-                        else:
-                            old = current[p]
-                            new = shrink * old + gain * (spread + target[p])
-                        current[p] = new
-                        extra[p] = 2.0 * new - old
-                before_x = dx[:by, :bz] if final else dx
+                        old = current[p]
+                        new = shrink * old + gain * (spread + target[p])
+                    current[p] = new
+                    extra[p] = 2.0 * new - old
+                return ahead, dx
+
+            carry = plane(iteration, here_ref[iteration], None)
+            rest = planes - 2 - 2 * iteration
+            unroll = next(u for u in (5, 6, 4, 2, 1) if rest % u == 0)
+
+            def several(j, carry, plane=plane, start=iteration + 1, unroll=unroll):
+                for k in range(unroll):
+                    carry = plane(start + j * unroll + k, *carry)
+                return carry
+
+            lax.fori_loop(0, rest // unroll, several, carry)
         model_copy = pltpu.make_async_copy(model, model_ref, sems.at[1])
         model_copy.start()
         gradient_copy.wait()
@@ -379,16 +394,20 @@
     parts = lax.all_to_all(local, GX, split_axis=0, concat_axis=0, tiled=True)
     gradient, *send_x, squares = reduce_pack(device, parts, velocity, sizes)
     halo_x = swap(send_x, GX, GY[1])
-    table = jnp.broadcast_to(
-        squares[:1][None], (sizes[0] * sizes[1] * sizes[2], 1, squares.shape[1])
-    )
-    table = lax.all_to_all(table, ALL, split_axis=0, concat_axis=0, tiled=True)
+    table = jnp.broadcast_to(squares[:1][None], (sizes[0] * sizes[2], 1, squares.shape[1]))
+    table = lax.all_to_all(table, XZ, split_axis=0, concat_axis=0, tiled=True)
     send_y = pack_y(device, gradient, velocity, halo_x, sizes)
     halo_y = swap(send_y, GY, "gz")
+    column = jnp.broadcast_to(jnp.sum(table, axis=0), squares.shape)
+    column = add_pairs(column, GY[1], lambda i, n: i ^ 1)
+    column = add_pairs(column, GY[0], lambda i, n: i ^ 1)
     send_z = pack_z(device, gradient, velocity, halo_x, halo_y, sizes)
     halo_z = swap(send_z, "gz", GY[1])
+    if lax.axis_size(GY[0]) > 2:
+        column = add_pairs(column, GY[0], lambda i, n: n - 1 - i)
+
     halos = (*halo_x, *halo_y, *halo_z)
-    return proximal(device, gradient, velocity, halos, table, sizes)
+    return proximal(device, gradient, velocity, halos, column, sizes)
 
 
 def solution(mesh):

time: 57.9 us -> 59.1 us (1.021)
  the two profiles are of different devices: /device:TPU:83 before, /device:TPU:1 now
where the time goes in v11:
time: 59.1 us; the launch traced here: 58.9 us
  blocking collectives  33.6 us (57%)
  starting transfers between devices  17.1 us (29%)
  Pallas kernels  6.09 us (10%)
  waiting for transfers between devices  1.44 us (2%)
  between operations  0.69 us (1%)
    all_to_all x1, blocking collectives, shards(): parts = lax.all_to_all(local, GX, split_axis=0, concat_axis=0, tiled=True)  21 us
    all_to_all x1, blocking collectives, shards(): table = lax.all_to_all(table, XZ, split_axis=0, concat_axis=0, tiled=True)  12.7 us
    ppermute x3, starting transfers between devices, add_pairs(): lax.ppermute(row, axis, [(i, partner(i, size)) for i in range(size)])  10.6 us
    ppermute x3, starting transfers between devices, swap(): lax.ppermute(blocks[1], both, others)  5.44 us
    pallas_call x1, Pallas kernels, proximal(): pl.pallas_call(kernel, name='proximal', compiler_params=PARAMS, out_shape...  3.36 us
    pallas_call x1, Pallas kernels, presum(): pl.pallas_call(kernel, name='presum', compiler_params=PARAMS, out_shape=s...  2.43 us
    ppermute x3, waiting for transfers between devices, add_pairs(): lax.ppermute(row, axis, [(i, partner(i, size)) for i in range(size)])  1.42 us
  transfers between devices with their start and end apart: 9, of which 2 were waited for; matrix products, arithmetic and copies ran while one was open for 0% of the time, Pallas kernels for 0%

profile of v11, /device:TPU:1, one launch (start us, length us, event | category | flops | bytes accessed | tf_op | source)
XLA Modules:
  0.0 58.9 jit_solution(14191206643749547743)
XLA Ops:
  0.6 0.0 copy-start
  0.7 2.4 %presum.1 = f32[128,16,128]{2,1,0:T(8,128)S(1)} custom-call(s32[1]{0:T(128)} %bitcast.dev_ref, s32[32]{0:T(128)} %map_hbm.1, s32[32,128]{1,0:T(8,128)} %bits_hbm.1, f32[4,128,16,128]{3,2,1,0:T(8,128)} %part_ref.1), custom_call_target="tpu_custom_call" | custom-call | tf_op jit(solution)/shard_map/presum/pallas_call | solution.py:94
  3.1 21.0 %all_to_all.10.part_ref = f32[128,16,128]{2,1,0:T(8,128)S(1)} all-to-all(f32[128,16,128]{2,1,0:T(8,128)S(1)} %presum.1), channel_id=1, replica_groups=mesh['gx_0'=4,'gx_1'=2,'gy_0'=4,'gy_1'=2,'gz'=4] {'gx_0','gx_1'}, dimensions={0} | all-to-all | bytes 2097152 | tf_op jit(solution)/shard_map/all_to_all | solution.py:394
  24.1 0.0 copy-done
  24.1 0.1 reduce_pack.1
  24.1 0.5 collective-permute-start
  24.7 2.1 %collective-permute-start.1 = (f32[6,16,128]{2,1,0:T(8,128)S(1)}, f32[6,16,128]{2,1,0:T(8,128)S(1)}, u32[]{:S(2)}, u32[]{:S(2)}) collective-permute-start(f32[6,16,128]{2,1,0:T(8,128)S(1)} %get-tuple-element.12), channel_id=1, source_target_pairs={{0,4},{4,0},{32,64},{36,68},{64,32},{68,36},{96,128},{100,132},{12... | collective-permute-start | bytes 147464 | tf_op jit(solution)/shard_map/ppermute | solution.py:43
  26.8 12.7 %all_to_all.11 = f32[32,1,128]{2,1,0:T(1,128)S(1)} all-to-all(f32[32,1,128]{2,1,0:T(1,128)S(1)} %broadcast_in_dim.14), channel_id=1, replica_groups=mesh['gx_0'=4,'gx_1'=2,'gy_0'=4,'gy_1'=2,'gz'=4] {'gx_0','gx_1','gz'}, dimensions={0} | all-to-all | bytes 32768 | tf_op jit(solution)/shard_map/all_to_all | solution.py:398
  39.4 3.5 %collective-permute-start.6 = (f32[8,128]{1,0:T(8,128)S(1)}, f32[8,128]{1,0:T(8,128)S(1)}, u32[]{:S(2)}, u32[]{:S(2)}) collective-permute-start(f32[8,128]{1,0:T(8,128)S(1)} %broadcast_in_dim.15), channel_id=1, source_target_pairs={{0,4},{4,0},{1,5},{5,1},{2,6},{6,2},{3,7},{7,3},{8,12},{12,8},{9,1... | collective-permute-start | bytes 12296 | tf_op jit(solution)/shard_map/ppermute | solution.py:48
  43.0 0.0 collective-permute-done.nx_ref
  43.0 0.0 collective-permute-done.1.ox_ref
  43.0 0.1 collective-permute-start.2
  43.1 3.4 %collective-permute-start.3 = (f32[22,8,128]{2,1,0:T(8,128)S(1)}, f32[22,8,128]{2,1,0:T(8,128)S(1)}, u32[]{:S(2)}, u32[]{:S(2)}) collective-permute-start(f32[22,8,128]{2,1,0:T(8,128)S(1)} %get-tuple-element.14), channel_id=1, source_target_pairs={{0,1},{1,0},{2,3},{3,2},{4,8},{5,9},{6,10},{7,11},{8,4},{9,5},{10,... | collective-permute-start | bytes 270344 | tf_op jit(solution)/shard_map/ppermute | solution.py:43
  46.5 0.0 collective-permute-done.6
  46.5 3.3 %collective-permute-start.7 = (f32[8,128]{1,0:T(8,128)S(1)}, f32[8,128]{1,0:T(8,128)S(1)}, u32[]{:S(2)}, u32[]{:S(2)}) collective-permute-start(f32[8,128]{1,0:T(8,128)S(1)} %broadcast_add_fusion), channel_id=1, source_target_pairs={{0,8},{8,0},{16,24},{24,16},{1,9},{9,1},{17,25},{25,17},{2,10},{10... | collective-permute-start | bytes 12296 | tf_op jit(solution)/shard_map/ppermute | solution.py:48
  49.8 0.0 collective-permute-done.2.ny_ref
  49.8 0.0 collective-permute-done.3.oy_ref
  49.8 0.2 pack_z.1
  50.0 0.4 collective-permute-start.4
  50.4 0.0 collective-permute-start.5
  50.4 0.4 collective-permute-done.7
  50.8 3.7 %collective-permute-start.8 = (f32[8,128]{1,0:T(8,128)S(1)}, f32[8,128]{1,0:T(8,128)S(1)}, u32[]{:S(2)}, u32[]{:S(2)}) collective-permute-start(f32[8,128]{1,0:T(8,128)S(1)} %fusion), channel_id=1, source_target_pairs={{0,24},{8,16},{16,8},{24,0},{1,25},{9,17},{17,9},{25,1},{2,26},{10... | collective-permute-start | bytes 12296 | tf_op jit(solution)/shard_map/ppermute | solution.py:48
  54.6 1.0 %collective-permute-done.8 = f32[8,128]{1,0:T(8,128)S(1)} collective-permute-done((f32[8,128]{1,0:T(8,128)S(1)}, f32[8,128]{1,0:T(8,128)S(1)}, u32[]{:S(2)}, u32[]{:S(2)}) %collective-permute-start.8) | collective-permute-done | bytes 4128 | tf_op jit(solution)/shard_map/ppermute | solution.py:48
  55.6 0.0 collective-permute-done.4.nz_ref
  55.6 0.0 collective-permute-done.5.oz_ref
  55.6 3.4 %proximal.1 = (f32[16,16,128]{2,1,0:T(8,128)}, f32[16,16,128]{2,1,0:T(8,128)}) custom-call(s32[1]{0:T(128)} %bitcast.dev_ref, f32[16,16,128]{2,1,0:T(8,128)S(1)} %get-tuple-element.10.g_ref, f32[16,16,128]{2,1,0:T(8,128)S(1)} %copy-done, f32[6,16,128]{2,1,0:T(8,128)S(1)} %collective-permute-done.nx_ref, f32[6,16,128]{2,1,0:T(8,128)S(1)} %collective-permute-done.1.ox_ref, ...), custom_call_target="tpu_custom_call" | custom-call | tf_op jit(solution)/shard_map/proximal/pallas_call | solution.py:378
  (8 shorter events, 0.1 us)
Async XLA Ops:
  0.6 23.4 %copy-start = (f32[16,16,128]{2,1,0:T(8,128)S(1)}, f32[16,16,128]{2,1,0:T(8,128)}, u32[]{:S(2)}) copy-start(f32[16,16,128]{2,1,0:T(8,128)} %v_ref.7) | copy-start | bytes 393220
  24.1 18.8 %collective-permute-start = (f32[6,16,128]{2,1,0:T(8,128)S(1)}, f32[6,16,128]{2,1,0:T(8,128)S(1)}, u32[]{:S(2)}, u32[]{:S(2)}) collective-permute-start(f32[6,16,128]{2,1,0:T(8,128)S(1)} %get-tuple-element.11), channel_id=1, source_target_pairs={{0,32},{32,0},{64,96},{96,64},{128,160},{160,128},{192,224},{224,1... | collective-permute-start | bytes 147464 | tf_op jit(solution)/shard_map/ppermute | solution.py:43
  24.7 18.3 %collective-permute-start.1 = (f32[6,16,128]{2,1,0:T(8,128)S(1)}, f32[6,16,128]{2,1,0:T(8,128)S(1)}, u32[]{:S(2)}, u32[]{:S(2)}) collective-permute-start(f32[6,16,128]{2,1,0:T(8,128)S(1)} %get-tuple-element.12), channel_id=1, source_target_pairs={{0,4},{4,0},{32,64},{36,68},{64,32},{68,36},{96,128},{100,132},{12... | collective-permute-start | bytes 147464 | tf_op jit(solution)/shard_map/ppermute | solution.py:43
  39.4 7.0 %collective-permute-start.6 = (f32[8,128]{1,0:T(8,128)S(1)}, f32[8,128]{1,0:T(8,128)S(1)}, u32[]{:S(2)}, u32[]{:S(2)}) collective-permute-start(f32[8,128]{1,0:T(8,128)S(1)} %broadcast_in_dim.15), channel_id=1, source_target_pairs={{0,4},{4,0},{1,5},{5,1},{2,6},{6,2},{3,7},{7,3},{8,12},{12,8},{9,1... | collective-permute-start | bytes 12296 | tf_op jit(solution)/shard_map/ppermute | solution.py:48
  43.0 6.8 %collective-permute-start.2 = (f32[22,8,128]{2,1,0:T(8,128)S(1)}, f32[22,8,128]{2,1,0:T(8,128)S(1)}, u32[]{:S(2)}, u32[]{:S(2)}) collective-permute-start(f32[22,8,128]{2,1,0:T(8,128)S(1)} %get-tuple-element.13), channel_id=1, source_target_pairs={{0,4},{4,0},{8,12},{12,8},{16,20},{20,16},{24,28},{28,24},{1,5},{5... | collective-permute-start | bytes 270344 | tf_op jit(solution)/shard_map/ppermute | solution.py:43
  43.1 6.7 %collective-permute-start.3 = (f32[22,8,128]{2,1,0:T(8,128)S(1)}, f32[22,8,128]{2,1,0:T(8,128)S(1)}, u32[]{:S(2)}, u32[]{:S(2)}) collective-permute-start(f32[22,8,128]{2,1,0:T(8,128)S(1)} %get-tuple-element.14), channel_id=1, source_target_pairs={{0,1},{1,0},{2,3},{3,2},{4,8},{5,9},{6,10},{7,11},{8,4},{9,5},{10,... | collective-permute-start | bytes 270344 | tf_op jit(solution)/shard_map/ppermute | solution.py:43
  46.5 4.3 %collective-permute-start.7 = (f32[8,128]{1,0:T(8,128)S(1)}, f32[8,128]{1,0:T(8,128)S(1)}, u32[]{:S(2)}, u32[]{:S(2)}) collective-permute-start(f32[8,128]{1,0:T(8,128)S(1)} %broadcast_add_fusion), channel_id=1, source_target_pairs={{0,8},{8,0},{16,24},{24,16},{1,9},{9,1},{17,25},{25,17},{2,10},{10... | collective-permute-start | bytes 12296 | tf_op jit(solution)/shard_map/ppermute | solution.py:48
  50.0 5.6 %collective-permute-start.4 = (f32[48,128]{1,0:T(8,128)S(1)}, f32[48,128]{1,0:T(8,128)S(1)}, u32[]{:S(2)}, u32[]{:S(2)}) collective-permute-start(f32[48,128]{1,0:T(8,128)S(1)} %get-tuple-element.15), channel_id=1, source_target_pairs={{0,1},{1,0},{2,3},{3,2},{4,5},{5,4},{6,7},{7,6},{8,9},{9,8},{10,11... | collective-permute-start | bytes 73736 | tf_op jit(solution)/shard_map/ppermute | solution.py:43
  50.4 5.2 %collective-permute-start.5 = (f32[48,128]{1,0:T(8,128)S(1)}, f32[48,128]{1,0:T(8,128)S(1)}, u32[]{:S(2)}, u32[]{:S(2)}) collective-permute-start(f32[48,128]{1,0:T(8,128)S(1)} %get-tuple-element.16), channel_id=1, source_target_pairs={{0,4},{4,0},{1,2},{5,6},{2,1},{6,5},{3,7},{7,3},{8,12},{12,8},{9,1... | collective-permute-start | bytes 73736 | tf_op jit(solution)/shard_map/ppermute | solution.py:43
  50.8 4.7 %collective-permute-start.8 = (f32[8,128]{1,0:T(8,128)S(1)}, f32[8,128]{1,0:T(8,128)S(1)}, u32[]{:S(2)}, u32[]{:S(2)}) collective-permute-start(f32[8,128]{1,0:T(8,128)S(1)} %fusion), channel_id=1, source_target_pairs={{0,24},{8,16},{16,8},{24,0},{1,25},{9,17},{17,9},{25,1},{2,26},{10... | collective-permute-start | bytes 12296 | tf_op jit(solution)/shard_map/ppermute | solution.py:48

commit v12 on v10

--- a/solution.py
+++ b/solution.py
@@ -40,6 +40,27 @@
             others.append((at(i, k), at(j, k) if 0 <= j < size else at(i, k ^ 1)))
     both = (spare, *axes) if ahead else (*axes, spare)
     return lax.ppermute(blocks[0], axis, pairs), lax.ppermute(blocks[1], both, others)
+
+
+def corner_swap(block, odd_y, odd_z):
+    axes = (GX[1], *GY, "gz")
+    sides, size_y, size_z = (lax.axis_size(axis) for axis in (GX[1], GY, "gz"))
+
+    def partner(i, size, odd):
+        j = ((i + 1) ^ 1) - 1 if odd else i ^ 1
+        return j if 0 <= j < size else None
+
+    route = []
+    for s in range(sides):
+        for y in range(size_y):
+            for z in range(size_z):
+                to_y, to_z = partner(y, size_y, odd_y), partner(z, size_z, odd_z)
+                to_s = s ^ 1 if to_y is None and to_z is None else s
+                to_y, to_z = (y if to_y is None else to_y), (z if to_z is None else to_z)
+                route.append(
+                    ((s * size_y + y) * size_z + z, (to_s * size_y + to_y) * size_z + to_z)
+                )
+    return lax.ppermute(block, axes, route)
 
 
 def struct(*shape):
@@ -199,38 +220,40 @@
     return jnp.where(low, pltpu.roll(after, 4, 0), before)
 
 
-def pack_z(device, gradient, velocity, halo_x, halo_y, sizes):
+def pack_z(device, gradient, velocity, halo_x, sizes):
     bx, by, bz = velocity.shape
     planes = bx + 2 * HALO
-    pairs = planes // 2
     groups = bz // 4
-    tall = by + 8
-
-    def kernel(dev_ref, g_ref, v_ref, nx_ref, ox_ref, ny_ref, oy_ref, near_ref, other_ref):
+
+    def kernel(dev_ref, g_ref, v_ref, nx_ref, ox_ref, near_ref, other_ref, *corner_refs):
         even_x, even_y, even_z = (is_even(i) for i in position(dev_ref, sizes))
-        group = lane((tall, bz)) // 4
+        group = lane((by, bz)) // 4
         for field, main in enumerate((g_ref, v_ref)):
-            first = jnp.zeros((tall, bz), F32)
-            last = jnp.zeros((tall, bz), F32)
+            first = jnp.zeros((by, bz), F32)
+            last = jnp.zeros((by, bz), F32)
             for p in range(planes):
-                own = plane_of(main, nx_ref, ox_ref, even_x, field, p)
-                extra = rows_of(ny_ref, oy_ref, even_y, field, p, pairs)
-                plane = jnp.concatenate([own, extra], 0)
+                plane = plane_of(main, nx_ref, ox_ref, even_x, field, p)
                 turned = pltpu.roll(plane, 4 * p, 1) if p else plane
                 first = jnp.where(group == p, turned, first)
                 last = jnp.where(group == (p - 1) % groups, turned, last)
-            near_ref[pl.ds(field * tall, tall)] = jnp.where(even_z, last, first)
-            other_ref[pl.ds(field * tall, tall)] = jnp.where(even_z, first, last)
-
-    edge = struct(2 * tall, bz)
+            near = jnp.where(even_z, last, first)
+            other = jnp.where(even_z, first, last)
+            near_ref[pl.ds(field * by, by)] = near
+            other_ref[pl.ds(field * by, by)] = other
+            for k, side in enumerate((near, other)):
+                top, bottom = side[:8], side[by - 8 :]
+                corner_refs[k][pl.ds(field * 8, 8)] = jnp.where(even_y, bottom, top)
+                corner_refs[2 + k][pl.ds(field * 8, 8)] = jnp.where(even_y, top, bottom)
+
+    edge = struct(2 * by, bz)
     return pl.pallas_call(
         kernel,
         name="pack_z",
         compiler_params=PARAMS,
-        out_shape=(edge, edge),
-        in_specs=[SMEM] + [VMEM] * 6,
-        out_specs=(VMEM,) * 2,
-    )(device, gradient, velocity, *halo_x, *halo_y)
+        out_shape=(edge,) * 2 + (struct(16, bz),) * 4,
+        in_specs=[SMEM] + [VMEM] * 4,
+        out_specs=(VMEM,) * 6,
+    )(device, gradient, velocity, *halo_x)
 
 
 def proximal(device, gradient, velocity, halos, squares, sizes):
@@ -252,6 +275,10 @@
         oy_ref,
         nz_ref,
         oz_ref,
+        c00_ref,
+        c01_ref,
+        c10_ref,
+        c11_ref,
         sq_ref,
         gradient_ref,
         model_ref,
@@ -274,8 +301,19 @@
         scale = jnp.broadcast_to(scale, (1, bz))
 
         side_lane = lane((tall, bz)) < bz // 2
-        near_z = nz_ref[pl.ds(tall, tall)] - scale * nz_ref[pl.ds(0, tall)]
-        other_z = oz_ref[pl.ds(tall, tall)] - scale * oz_ref[pl.ds(0, tall)]
+
+        def scaled(ref, rows):
+            return ref[pl.ds(rows, rows)] - scale * ref[pl.ds(0, rows)]
+
+        def tall_edge(ref, near_corner, other_corner):
+            near, other = scaled(near_corner, 8), scaled(other_corner, 8)
+            after = jnp.where(even_y, near, other)
+            before = jnp.where(even_y, other, near)
+            extra = jnp.where(sublane((8, bz)) < 4, after, before)
+            return jnp.concatenate([scaled(ref, by), extra], 0)
+
+        near_z = tall_edge(nz_ref, c00_ref, c10_ref)
+        other_z = tall_edge(oz_ref, c01_ref, c11_ref)
         before_z = jnp.where(even_z, other_z, near_z)
         after_z = jnp.where(even_z, near_z, other_z)
         for p in range(planes):
@@ -365,7 +403,7 @@
         name="proximal",
         compiler_params=PARAMS,
         out_shape=(struct(bx, by, bz),) * 2,
-        in_specs=[SMEM] + [VMEM] * 9,
+        in_specs=[SMEM] + [VMEM] * 13,
         out_specs=(HBM,) * 2,
         scratch_shapes=[field] * 6 + [pltpu.VMEM((bx, by, bz), F32), pltpu.SemaphoreType.DMA((2,))],
     )(device, gradient, velocity, *halos, squares)
@@ -385,9 +423,16 @@
     table = lax.all_to_all(table, ALL, split_axis=0, concat_axis=0, tiled=True)
     send_y = pack_y(device, gradient, velocity, halo_x, sizes)
     halo_y = swap(send_y, GY, "gz")
-    send_z = pack_z(device, gradient, velocity, halo_x, halo_y, sizes)
+    *send_z, c00, c01, c10, c11 = pack_z(device, gradient, velocity, halo_x, sizes)
     halo_z = swap(send_z, "gz", GY[1])
-    halos = (*halo_x, *halo_y, *halo_z)
+    corners = (
+        corner_swap(c00, False, False),
+        corner_swap(c01, False, True),
+        corner_swap(c10, True, False),
+        corner_swap(c11, True, True),
+    )
+
+    halos = (*halo_x, *halo_y, *halo_z, *corners)
     return proximal(device, gradient, velocity, halos, table, sizes)
 
 

time: 57.9 us -> 64.8 us (1.12)
  the two profiles are of different devices: /device:TPU:83 before, /device:TPU:75 now
where the time goes in v12:
time: 64.8 us; the launch traced here: 64.6 us
  starting transfers between devices  25.6 us (40%)
  blocking collectives  18.5 us (29%)
  waiting for transfers between devices  13.8 us (21%)
  Pallas kernels  5.29 us (8%)
  local copies, waits for them, and re-layouts  0.73 us (1%)
  between operations  0.72 us (1%)
    all_to_all x1, blocking collectives, shards(): parts = lax.all_to_all(local, GX, split_axis=0, concat_axis=0, tiled=True)  18.5 us
    all_to_all x1, starting transfers between devices, shards(): table = lax.all_to_all(table, ALL, split_axis=0, concat_axis=0, tiled=True)  14.4 us
    ppermute x4, waiting for transfers between devices, corner_swap(): return lax.ppermute(block, axes, route)  9.35 us
    ppermute x3, starting transfers between devices, swap(): lax.ppermute(blocks[0], axis, pairs)  4.25 us
    ppermute x3, starting transfers between devices, swap(): lax.ppermute(blocks[1], both, others)  3.48 us
    ppermute x4, starting transfers between devices, corner_swap(): return lax.ppermute(block, axes, route)  3.39 us
    pallas_call x1, Pallas kernels, proximal(): pl.pallas_call(kernel, name='proximal', compiler_params=PARAMS, out_shape...  2.61 us
    pallas_call x1, Pallas kernels, presum(): pl.pallas_call(kernel, name='presum', compiler_params=PARAMS, out_shape=s...  2.43 us
  transfers between devices with their start and end apart: 11, of which 5 were waited for; matrix products, arithmetic and copies ran while one was open for 0% of the time, Pallas kernels for 0%

profile of v12, /device:TPU:75, one launch (start us, length us, event | category | flops | bytes accessed | tf_op | source)
XLA Modules:
  0.0 64.6 jit_solution(15302985129903655148)
XLA Ops:
  0.6 0.0 copy-start
  0.7 2.4 %presum.1 = f32[128,16,128]{2,1,0:T(8,128)S(1)} custom-call(s32[1]{0:T(128)} %bitcast.dev_ref, s32[32]{0:T(128)} %map_hbm.1, s32[32,128]{1,0:T(8,128)} %bits_hbm.1, f32[4,128,16,128]{3,2,1,0:T(8,128)} %part_ref.1), custom_call_target="tpu_custom_call" | custom-call | tf_op jit(solution)/shard_map/presum/pallas_call | solution.py:109
  3.1 18.5 %all_to_all.10.part_ref = f32[128,16,128]{2,1,0:T(8,128)S(1)} all-to-all(f32[128,16,128]{2,1,0:T(8,128)S(1)} %presum.1), channel_id=1, replica_groups=mesh['gx_0'=4,'gx_1'=2,'gy_0'=4,'gy_1'=2,'gz'=4] {'gx_0','gx_1'}, dimensions={0} | all-to-all | bytes 2097152 | tf_op jit(solution)/shard_map/all_to_all | solution.py:417
  21.6 0.0 copy-done
  21.6 0.1 reduce_pack.1
  21.6 0.7 %broadcast_in_dim.9 = f32[256,1,128]{2,1,0:T(1,128)} broadcast(f32[128]{0:T(128)S(1)} %slice_bitcast_fusion), dimensions={2} | broadcast | bytes 131584 | tf_op jit(solution)/shard_map/broadcast_in_dim | solution.py:420
  22.4 14.4 %all-to-all-start.1 = ((f32[256,1,128]{2,1,0:T(1,128)}), f32[256,1,128]{2,1,0:T(1,128)S(1)}, u32[]{:S(2)}, u32[]{:S(2)}) async-start(f32[256,1,128]{2,1,0:T(1,128)} %broadcast_in_dim.9), calls=%async_computation.1 | async-start | bytes 262144 | tf_op jit(solution)/shard_map/all_to_all | solution.py:423
  36.8 1.5 %collective-permute-start = (f32[6,16,128]{2,1,0:T(8,128)S(1)}, f32[6,16,128]{2,1,0:T(8,128)S(1)}, u32[]{:S(2)}, u32[]{:S(2)}) collective-permute-start(f32[6,16,128]{2,1,0:T(8,128)S(1)} %get-tuple-element.15), channel_id=1, source_target_pairs={{0,32},{32,0},{64,96},{96,64},{128,160},{160,128},{192,224},{224,1... | collective-permute-start | bytes 147464 | tf_op jit(solution)/shard_map/ppermute | solution.py:42
  38.3 0.1 collective-permute-start.1
  38.4 2.1 %collective-permute-done.nx_ref = f32[6,16,128]{2,1,0:T(8,128)S(1)} collective-permute-done((f32[6,16,128]{2,1,0:T(8,128)S(1)}, f32[6,16,128]{2,1,0:T(8,128)S(1)}, u32[]{:S(2)}, u32[]{:S(2)}) %collective-permute-start) | collective-permute-done | bytes 49184 | tf_op jit(solution)/shard_map/ppermute | solution.py:42
  40.5 2.4 %collective-permute-done.1.ox_ref = f32[6,16,128]{2,1,0:T(8,128)S(1)} collective-permute-done((f32[6,16,128]{2,1,0:T(8,128)S(1)}, f32[6,16,128]{2,1,0:T(8,128)S(1)}, u32[]{:S(2)}, u32[]{:S(2)}) %collective-permute-start.1) | collective-permute-done | bytes 49184 | tf_op jit(solution)/shard_map/ppermute | solution.py:42
  42.9 1.3 %collective-permute-start.2 = (f32[22,8,128]{2,1,0:T(8,128)S(1)}, f32[22,8,128]{2,1,0:T(8,128)S(1)}, u32[]{:S(2)}, u32[]{:S(2)}) collective-permute-start(f32[22,8,128]{2,1,0:T(8,128)S(1)} %get-tuple-element.17), channel_id=1, source_target_pairs={{0,4},{4,0},{8,12},{12,8},{16,20},{20,16},{24,28},{28,24},{1,5},{5... | collective-permute-start | bytes 270344 | tf_op jit(solution)/shard_map/ppermute | solution.py:42
  44.2 2.8 %collective-permute-start.3 = (f32[22,8,128]{2,1,0:T(8,128)S(1)}, f32[22,8,128]{2,1,0:T(8,128)S(1)}, u32[]{:S(2)}, u32[]{:S(2)}) collective-permute-start(f32[22,8,128]{2,1,0:T(8,128)S(1)} %get-tuple-element.18), channel_id=1, source_target_pairs={{0,1},{1,0},{2,3},{3,2},{4,8},{5,9},{6,10},{7,11},{8,4},{9,5},{10,... | collective-permute-start | bytes 270344 | tf_op jit(solution)/shard_map/ppermute | solution.py:42
  47.0 0.2 pack_z.1
  47.2 0.1 collective-permute-start.6
  47.3 2.5 %collective-permute-start.7 = (f32[16,128]{1,0:T(8,128)S(1)}, f32[16,128]{1,0:T(8,128)S(1)}, u32[]{:S(2)}, u32[]{:S(2)}) collective-permute-start(f32[16,128]{1,0:T(8,128)S(1)} %get-tuple-element.22), channel_id=1, source_target_pairs={{0,4},{1,6},{2,5},{3,7},{4,0},{5,2},{6,1},{7,3},{8,12},{9,14},{10,... | collective-permute-start | bytes 24584 | tf_op jit(solution)/shard_map/ppermute | solution.py:63
  49.8 0.1 collective-permute-start.8
  49.9 0.7 %collective-permute-done.6.c00_ref = f32[16,128]{1,0:T(8,128)S(1)} collective-permute-done((f32[16,128]{1,0:T(8,128)S(1)}, f32[16,128]{1,0:T(8,128)S(1)}, u32[]{:S(2)}, u32[]{:S(2)}) %collective-permute-start.6) | collective-permute-done | bytes 8224 | tf_op jit(solution)/shard_map/ppermute | solution.py:63
  50.6 1.4 %collective-permute-start.4 = (f32[32,128]{1,0:T(8,128)S(1)}, f32[32,128]{1,0:T(8,128)S(1)}, u32[]{:S(2)}, u32[]{:S(2)}) collective-permute-start(f32[32,128]{1,0:T(8,128)S(1)} %get-tuple-element.19), channel_id=1, source_target_pairs={{0,1},{1,0},{2,3},{3,2},{4,5},{5,4},{6,7},{7,6},{8,9},{9,8},{10,11... | collective-permute-start | bytes 49160 | tf_op jit(solution)/shard_map/ppermute | solution.py:42
  52.0 0.0 collective-permute-done.7.c01_ref
  52.0 0.6 collective-permute-start.5
  52.6 3.3 %collective-permute-done.8.c10_ref = f32[16,128]{1,0:T(8,128)S(1)} collective-permute-done((f32[16,128]{1,0:T(8,128)S(1)}, f32[16,128]{1,0:T(8,128)S(1)}, u32[]{:S(2)}, u32[]{:S(2)}) %collective-permute-start.8) | collective-permute-done | bytes 8224 | tf_op jit(solution)/shard_map/ppermute | solution.py:63
  55.9 0.7 %collective-permute-start.9 = (f32[16,128]{1,0:T(8,128)S(1)}, f32[16,128]{1,0:T(8,128)S(1)}, u32[]{:S(2)}, u32[]{:S(2)}) collective-permute-start(f32[16,128]{1,0:T(8,128)S(1)} %get-tuple-element.24), channel_id=1, source_target_pairs={{0,32},{1,2},{2,1},{3,35},{4,8},{5,10},{6,9},{7,11},{8,4},{9,6},{1... | collective-permute-start | bytes 24584 | tf_op jit(solution)/shard_map/ppermute | solution.py:63
  56.6 5.4 %collective-permute-done.9.c11_ref = f32[16,128]{1,0:T(8,128)S(1)} collective-permute-done((f32[16,128]{1,0:T(8,128)S(1)}, f32[16,128]{1,0:T(8,128)S(1)}, u32[]{:S(2)}, u32[]{:S(2)}) %collective-permute-start.9) | collective-permute-done | bytes 8224 | tf_op jit(solution)/shard_map/ppermute | solution.py:63
  61.9 0.0 collective-permute-done.4.nz_ref
  61.9 0.0 collective-permute-done.5.oz_ref
  62.0 0.0 collective-permute-done.2.ny_ref
  62.0 0.0 collective-permute-done.3.oy_ref
  62.0 0.0 all-to-all-done.1.sq_ref
  62.0 2.6 %proximal.1 = (f32[16,16,128]{2,1,0:T(8,128)}, f32[16,16,128]{2,1,0:T(8,128)}) custom-call(s32[1]{0:T(128)} %bitcast.dev_ref, f32[16,16,128]{2,1,0:T(8,128)S(1)} %get-tuple-element.14.g_ref, f32[16,16,128]{2,1,0:T(8,128)S(1)} %copy-done, f32[6,16,128]{2,1,0:T(8,128)S(1)} %collective-permute-done.nx_ref, f32[6,16,128]{2,1,0:T(8,128)S(1)} %collective-permute-done.1.ox_ref, ...), custom_call_target="tpu_custom_call" | custom-call | tf_op jit(solution)/shard_map/proximal/pallas_call | solution.py:401
  (2 shorter events, 0.0 us)
Async XLA Ops:
  0.6 20.9 %copy-start = (f32[16,16,128]{2,1,0:T(8,128)S(1)}, f32[16,16,128]{2,1,0:T(8,128)}, u32[]{:S(2)}) copy-start(f32[16,16,128]{2,1,0:T(8,128)} %v_ref.7) | copy-start | bytes 393220
  22.4 39.6 %all-to-all-start.1 = ((f32[256,1,128]{2,1,0:T(1,128)}), f32[256,1,128]{2,1,0:T(1,128)S(1)}, u32[]{:S(2)}, u32[]{:S(2)}) async-start(f32[256,1,128]{2,1,0:T(1,128)} %broadcast_in_dim.9), calls=%async_computation.1 | async-start | bytes 262144 | tf_op jit(solution)/shard_map/all_to_all | solution.py:423
  36.8 3.7 %collective-permute-start = (f32[6,16,128]{2,1,0:T(8,128)S(1)}, f32[6,16,128]{2,1,0:T(8,128)S(1)}, u32[]{:S(2)}, u32[]{:S(2)}) collective-permute-start(f32[6,16,128]{2,1,0:T(8,128)S(1)} %get-tuple-element.15), channel_id=1, source_target_pairs={{0,32},{32,0},{64,96},{96,64},{128,160},{160,128},{192,224},{224,1... | collective-permute-start | bytes 147464 | tf_op jit(solution)/shard_map/ppermute | solution.py:42
  38.3 4.5 %collective-permute-start.1 = (f32[6,16,128]{2,1,0:T(8,128)S(1)}, f32[6,16,128]{2,1,0:T(8,128)S(1)}, u32[]{:S(2)}, u32[]{:S(2)}) collective-permute-start(f32[6,16,128]{2,1,0:T(8,128)S(1)} %get-tuple-element.16), channel_id=1, source_target_pairs={{0,4},{4,0},{32,64},{36,68},{64,32},{68,36},{96,128},{100,132},{12... | collective-permute-start | bytes 147464 | tf_op jit(solution)/shard_map/ppermute | solution.py:42
  42.9 19.0 %collective-permute-start.2 = (f32[22,8,128]{2,1,0:T(8,128)S(1)}, f32[22,8,128]{2,1,0:T(8,128)S(1)}, u32[]{:S(2)}, u32[]{:S(2)}) collective-permute-start(f32[22,8,128]{2,1,0:T(8,128)S(1)} %get-tuple-element.17), channel_id=1, source_target_pairs={{0,4},{4,0},{8,12},{12,8},{16,20},{20,16},{24,28},{28,24},{1,5},{5... | collective-permute-start | bytes 270344 | tf_op jit(solution)/shard_map/ppermute | solution.py:42
  44.2 17.7 %collective-permute-start.3 = (f32[22,8,128]{2,1,0:T(8,128)S(1)}, f32[22,8,128]{2,1,0:T(8,128)S(1)}, u32[]{:S(2)}, u32[]{:S(2)}) collective-permute-start(f32[22,8,128]{2,1,0:T(8,128)S(1)} %get-tuple-element.18), channel_id=1, source_target_pairs={{0,1},{1,0},{2,3},{3,2},{4,8},{5,9},{6,10},{7,11},{8,4},{9,5},{10,... | collective-permute-start | bytes 270344 | tf_op jit(solution)/shard_map/ppermute | solution.py:42
  47.2 3.4 %collective-permute-start.6 = (f32[16,128]{1,0:T(8,128)S(1)}, f32[16,128]{1,0:T(8,128)S(1)}, u32[]{:S(2)}, u32[]{:S(2)}) collective-permute-start(f32[16,128]{1,0:T(8,128)S(1)} %get-tuple-element.21), channel_id=1, source_target_pairs={{0,5},{1,4},{2,7},{3,6},{4,1},{5,0},{6,3},{7,2},{8,13},{9,12},{10,... | collective-permute-start | bytes 24584 | tf_op jit(solution)/shard_map/ppermute | solution.py:63
  47.3 4.7 %collective-permute-start.7 = (f32[16,128]{1,0:T(8,128)S(1)}, f32[16,128]{1,0:T(8,128)S(1)}, u32[]{:S(2)}, u32[]{:S(2)}) collective-permute-start(f32[16,128]{1,0:T(8,128)S(1)} %get-tuple-element.22), channel_id=1, source_target_pairs={{0,4},{1,6},{2,5},{3,7},{4,0},{5,2},{6,1},{7,3},{8,12},{9,14},{10,... | collective-permute-start | bytes 24584 | tf_op jit(solution)/shard_map/ppermute | solution.py:63
  49.8 6.1 %collective-permute-start.8 = (f32[16,128]{1,0:T(8,128)S(1)}, f32[16,128]{1,0:T(8,128)S(1)}, u32[]{:S(2)}, u32[]{:S(2)}) collective-permute-start(f32[16,128]{1,0:T(8,128)S(1)} %get-tuple-element.23), channel_id=1, source_target_pairs={{0,1},{1,0},{2,3},{3,2},{4,9},{5,8},{6,11},{7,10},{8,5},{9,4},{10,... | collective-permute-start | bytes 24584 | tf_op jit(solution)/shard_map/ppermute | solution.py:63
  50.6 11.4 %collective-permute-start.4 = (f32[32,128]{1,0:T(8,128)S(1)}, f32[32,128]{1,0:T(8,128)S(1)}, u32[]{:S(2)}, u32[]{:S(2)}) collective-permute-start(f32[32,128]{1,0:T(8,128)S(1)} %get-tuple-element.19), channel_id=1, source_target_pairs={{0,1},{1,0},{2,3},{3,2},{4,5},{5,4},{6,7},{7,6},{8,9},{9,8},{10,11... | collective-permute-start | bytes 49160 | tf_op jit(solution)/shard_map/ppermute | solution.py:42
  52.0 10.0 %collective-permute-start.5 = (f32[32,128]{1,0:T(8,128)S(1)}, f32[32,128]{1,0:T(8,128)S(1)}, u32[]{:S(2)}, u32[]{:S(2)}) collective-permute-start(f32[32,128]{1,0:T(8,128)S(1)} %get-tuple-element.20), channel_id=1, source_target_pairs={{0,4},{4,0},{1,2},{5,6},{2,1},{6,5},{3,7},{7,3},{8,12},{12,8},{9,1... | collective-permute-start | bytes 49160 | tf_op jit(solution)/shard_map/ppermute | solution.py:42
  55.9 6.1 %collective-permute-start.9 = (f32[16,128]{1,0:T(8,128)S(1)}, f32[16,128]{1,0:T(8,128)S(1)}, u32[]{:S(2)}, u32[]{:S(2)}) collective-permute-start(f32[16,128]{1,0:T(8,128)S(1)} %get-tuple-element.24), channel_id=1, source_target_pairs={{0,32},{1,2},{2,1},{3,35},{4,8},{5,10},{6,9},{7,11},{8,4},{9,6},{1... | collective-permute-start | bytes 24584 | tf_op jit(solution)/shard_map/ppermute | solution.py:63

commit v13 on v11

--- a/solution.py
+++ b/solution.py
@@ -11,7 +11,6 @@
 GX = ("gx_0", "gx_1")
 GY = ("gy_0", "gy_1")
 ALL = GX + GY + ("gz",)
-XZ = GX + ("gz",)
 
 step_length = 0.5
 tv_weight = 0.2
@@ -41,11 +40,6 @@
             others.append((at(i, k), at(j, k) if 0 <= j < size else at(i, k ^ 1)))
     both = (spare, *axes) if ahead else (*axes, spare)
     return lax.ppermute(blocks[0], axis, pairs), lax.ppermute(blocks[1], both, others)
-
-
-def add_pairs(row, axis, partner):
-    size = lax.axis_size(axis)
-    return row + lax.ppermute(row, axis, [(i, partner(i, size)) for i in range(size)])
 
 
 def struct(*shape):
@@ -205,28 +199,59 @@
     return jnp.where(low, pltpu.roll(after, 4, 0), before)
 
 
-def pack_z(device, gradient, velocity, halo_x, halo_y, sizes):
+def pack_lanes(device, gradient, velocity, halo_x, sizes):
     bx, by, bz = velocity.shape
     planes = bx + 2 * HALO
-    pairs = planes // 2
     groups = bz // 4
-    tall = by + 8
-
-    def kernel(dev_ref, g_ref, v_ref, nx_ref, ox_ref, ny_ref, oy_ref, near_ref, other_ref):
-        even_x, even_y, even_z = (is_even(i) for i in position(dev_ref, sizes))
-        group = lane((tall, bz)) // 4
+
+    def kernel(dev_ref, g_ref, v_ref, nx_ref, ox_ref, first_ref, last_ref, near_ref, other_ref):
+        even_x, even_y = (is_even(i) for i in position(dev_ref, sizes)[:2])
+        group = lane((by, bz)) // 4
         for field, main in enumerate((g_ref, v_ref)):
-            first = jnp.zeros((tall, bz), F32)
-            last = jnp.zeros((tall, bz), F32)
+            first = jnp.zeros((by, bz), F32)
+            last = jnp.zeros((by, bz), F32)
             for p in range(planes):
-                own = plane_of(main, nx_ref, ox_ref, even_x, field, p)
-                extra = rows_of(ny_ref, oy_ref, even_y, field, p, pairs)
-                plane = jnp.concatenate([own, extra], 0)
+                plane = plane_of(main, nx_ref, ox_ref, even_x, field, p)
                 turned = pltpu.roll(plane, 4 * p, 1) if p else plane
                 first = jnp.where(group == p, turned, first)
                 last = jnp.where(group == (p - 1) % groups, turned, last)
-            near_ref[pl.ds(field * tall, tall)] = jnp.where(even_z, last, first)
-            other_ref[pl.ds(field * tall, tall)] = jnp.where(even_z, first, last)
+            first_ref[pl.ds(field * by, by)] = first
+            last_ref[pl.ds(field * by, by)] = last
+            for k, packed in enumerate((first, last)):
+                top, bottom = packed[:8], packed[by - 8 :]
+                near_ref[2 * field + k] = jnp.where(even_y, bottom, top)
+                other_ref[2 * field + k] = jnp.where(even_y, top, bottom)
+
+    own = struct(2 * by, bz)
+    edge = struct(4, 8, bz)
+    return pl.pallas_call(
+        kernel,
+        name="pack_lanes",
+        compiler_params=PARAMS,
+        out_shape=(own, own, edge, edge),
+        in_specs=[SMEM] + [VMEM] * 4,
+        out_specs=(VMEM,) * 4,
+    )(device, gradient, velocity, *halo_x)
+
+
+def pack_z(device, first, last, corners, sizes):
+    rows, bz = first.shape
+    by = rows // 2
+    tall = by + 8
+
+    def kernel(dev_ref, first_ref, last_ref, nc_ref, oc_ref, near_ref, other_ref):
+        even_y, even_z = (is_even(i) for i in position(dev_ref, sizes)[1:])
+        low = sublane((8, bz)) < 4
+        for field in range(2):
+            both = []
+            for k, ref in enumerate((first_ref, last_ref)):
+                near, other = nc_ref[2 * field + k], oc_ref[2 * field + k]
+                after = jnp.where(even_y, near, other)
+                before = jnp.where(even_y, other, near)
+                extra = jnp.where(low, after, before)
+                both.append(jnp.concatenate([ref[pl.ds(field * by, by)], extra], 0))
+            near_ref[pl.ds(field * tall, tall)] = jnp.where(even_z, both[1], both[0])
+            other_ref[pl.ds(field * tall, tall)] = jnp.where(even_z, both[0], both[1])
 
     edge = struct(2 * tall, bz)
     return pl.pallas_call(
@@ -234,9 +259,9 @@
         name="pack_z",
         compiler_params=PARAMS,
         out_shape=(edge, edge),
-        in_specs=[SMEM] + [VMEM] * 6,
+        in_specs=[SMEM] + [VMEM] * 4,
         out_specs=(VMEM,) * 2,
-    )(device, gradient, velocity, *halo_x, *halo_y)
+    )(device, first, last, *corners)
 
 
 def proximal(device, gradient, velocity, halos, squares, sizes):
@@ -275,7 +300,7 @@
         pos_x, pos_y, pos_z = position(dev_ref, sizes)
         even_x, even_y, even_z = (is_even(i) for i in (pos_x, pos_y, pos_z))
 
-        total = jnp.sum(sq_ref[0:1], axis=1, keepdims=True)
+        total = jnp.sum(jnp.sum(sq_ref[...], axis=0), axis=1, keepdims=True)
         scale = step_length * lax.rsqrt(total / cells + 1.0)
         scale = jnp.broadcast_to(scale, (1, bz))
 
@@ -390,24 +415,24 @@
     sizes = tuple(lax.axis_size(axis) for axis in (GX, GY, "gz"))
     device = lax.axis_index(ALL).astype(jnp.int32).reshape(1)
 
-    local = presum(device, partials, code_bits, group_map, sizes, 8)
+    local = presum(device, partials, code_bits, group_map, sizes, 16)
     parts = lax.all_to_all(local, GX, split_axis=0, concat_axis=0, tiled=True)
     gradient, *send_x, squares = reduce_pack(device, parts, velocity, sizes)
     halo_x = swap(send_x, GX, GY[1])
-    table = jnp.broadcast_to(squares[:1][None], (sizes[0] * sizes[2], 1, squares.shape[1]))
-    table = lax.all_to_all(table, XZ, split_axis=0, concat_axis=0, tiled=True)
+    table = jnp.broadcast_to(
+        squares[:1][None], (sizes[0] * sizes[1] * sizes[2], 1, squares.shape[1])
+    )
+    table = lax.all_to_all(table, ALL, split_axis=0, concat_axis=0, tiled=True)
+    first, last, *send_corners = pack_lanes(device, gradient, velocity, halo_x, sizes)
+    corners = swap(send_corners, GY, "gz")
     send_y = pack_y(device, gradient, velocity, halo_x, sizes)
     halo_y = swap(send_y, GY, "gz")
-    column = jnp.broadcast_to(jnp.sum(table, axis=0), squares.shape)
-    column = add_pairs(column, GY[1], lambda i, n: i ^ 1)
-    column = add_pairs(column, GY[0], lambda i, n: i ^ 1)
-    send_z = pack_z(device, gradient, velocity, halo_x, halo_y, sizes)
+
+    send_z = pack_z(device, first, last, corners, sizes)
     halo_z = swap(send_z, "gz", GY[1])
-    if lax.axis_size(GY[0]) > 2:
-        column = add_pairs(column, GY[0], lambda i, n: n - 1 - i)
 
     halos = (*halo_x, *halo_y, *halo_z)
-    return proximal(device, gradient, velocity, halos, column, sizes)
+    return proximal(device, gradient, velocity, halos, table, sizes)
 
 
 def solution(mesh):

time: 59.1 us -> 60.7 us (1.027)
  the two profiles are of different devices: /device:TPU:1 before, /device:TPU:83 now
where the time goes in v13:
time: 60.7 us; the launch traced here: 60.5 us
  starting transfers between devices  22.4 us (37%)
  blocking collectives  18.5 us (30%)
  waiting for transfers between devices  11.8 us (19%)
  Pallas kernels  6.4 us (11%)
  local copies, waits for them, and re-layouts  0.73 us (1%)
  between operations  0.71 us (1%)
    all_to_all x1, blocking collectives, shards(): parts = lax.all_to_all(local, GX, split_axis=0, concat_axis=0, tiled=True)  18.5 us
    all_to_all x1, starting transfers between devices, shards(): table = lax.all_to_all(table, ALL, split_axis=0, concat_axis=0, tiled=True)  14.4 us
    ppermute x4, waiting for transfers between devices, swap(): lax.ppermute(blocks[1], both, others)  7.96 us
    ppermute x4, starting transfers between devices, swap(): lax.ppermute(blocks[1], both, others)  4.11 us
    ppermute x4, starting transfers between devices, swap(): lax.ppermute(blocks[0], axis, pairs)  3.94 us
    ppermute x4, waiting for transfers between devices, swap(): lax.ppermute(blocks[0], axis, pairs)  3.8 us
    pallas_call x1, Pallas kernels, proximal(): pl.pallas_call(kernel, name='proximal', compiler_params=PARAMS, out_shape...  3.62 us
    pallas_call x1, Pallas kernels, presum(): pl.pallas_call(kernel, name='presum', compiler_params=PARAMS, out_shape=s...  2.51 us
  transfers between devices with their start and end apart: 9, of which 5 were waited for; matrix products, arithmetic and copies ran while one was open for 0% of the time, Pallas kernels for 0%

profile of v13, /device:TPU:83, one launch (start us, length us, event | category | flops | bytes accessed | tf_op | source)
XLA Modules:
  0.0 60.5 jit_solution(6922552366652049015)
XLA Ops:
  0.6 0.0 copy-start
  0.7 2.5 %presum.1 = f32[128,16,128]{2,1,0:T(8,128)S(1)} custom-call(s32[1]{0:T(128)} %bitcast.dev_ref, s32[32]{0:T(128)} %map_hbm.1, s32[32,128]{1,0:T(8,128)} %bits_hbm.1, f32[4,128,16,128]{3,2,1,0:T(8,128)} %part_ref.1), custom_call_target="tpu_custom_call" | custom-call | tf_op jit(solution)/shard_map/presum/pallas_call | solution.py:88
  3.2 18.5 %all_to_all.10.part_ref = f32[128,16,128]{2,1,0:T(8,128)S(1)} all-to-all(f32[128,16,128]{2,1,0:T(8,128)S(1)} %presum.1), channel_id=1, replica_groups=mesh['gx_0'=4,'gx_1'=2,'gy_0'=4,'gy_1'=2,'gz'=4] {'gx_0','gx_1'}, dimensions={0} | all-to-all | bytes 2097152 | tf_op jit(solution)/shard_map/all_to_all | solution.py:419
  21.6 0.0 copy-done
  21.6 0.1 reduce_pack.1
  21.7 0.7 %broadcast_in_dim.9 = f32[256,1,128]{2,1,0:T(1,128)} broadcast(f32[128]{0:T(128)S(1)} %slice_bitcast_fusion), dimensions={2} | broadcast | bytes 131584 | tf_op jit(solution)/shard_map/broadcast_in_dim | solution.py:422
  22.4 14.4 %all-to-all-start.1 = ((f32[256,1,128]{2,1,0:T(1,128)}), f32[256,1,128]{2,1,0:T(1,128)S(1)}, u32[]{:S(2)}, u32[]{:S(2)}) async-start(f32[256,1,128]{2,1,0:T(1,128)} %broadcast_in_dim.9), calls=%async_computation.1 | async-start | bytes 262144 | tf_op jit(solution)/shard_map/all_to_all | solution.py:425
  36.8 1.5 %collective-permute-start = (f32[6,16,128]{2,1,0:T(8,128)S(1)}, f32[6,16,128]{2,1,0:T(8,128)S(1)}, u32[]{:S(2)}, u32[]{:S(2)}) collective-permute-start(f32[6,16,128]{2,1,0:T(8,128)S(1)} %get-tuple-element.15), channel_id=1, source_target_pairs={{0,32},{32,0},{64,96},{96,64},{128,160},{160,128},{192,224},{224,1... | collective-permute-start | bytes 147464 | tf_op jit(solution)/shard_map/ppermute | solution.py:42
  38.4 0.1 collective-permute-start.1
  38.5 2.1 %collective-permute-done.nx_ref = f32[6,16,128]{2,1,0:T(8,128)S(1)} collective-permute-done((f32[6,16,128]{2,1,0:T(8,128)S(1)}, f32[6,16,128]{2,1,0:T(8,128)S(1)}, u32[]{:S(2)}, u32[]{:S(2)}) %collective-permute-start) | collective-permute-done | bytes 49184 | tf_op jit(solution)/shard_map/ppermute | solution.py:42
  40.5 2.4 %collective-permute-done.1.ox_ref = f32[6,16,128]{2,1,0:T(8,128)S(1)} collective-permute-done((f32[6,16,128]{2,1,0:T(8,128)S(1)}, f32[6,16,128]{2,1,0:T(8,128)S(1)}, u32[]{:S(2)}, u32[]{:S(2)}) %collective-permute-start.1) | collective-permute-done | bytes 49184 | tf_op jit(solution)/shard_map/ppermute | solution.py:42
  43.0 1.3 %collective-permute-start.2 = (f32[22,8,128]{2,1,0:T(8,128)S(1)}, f32[22,8,128]{2,1,0:T(8,128)S(1)}, u32[]{:S(2)}, u32[]{:S(2)}) collective-permute-start(f32[22,8,128]{2,1,0:T(8,128)S(1)} %get-tuple-element.17), channel_id=1, source_target_pairs={{0,4},{4,0},{8,12},{12,8},{16,20},{20,16},{24,28},{28,24},{1,5},{5... | collective-permute-start | bytes 270344 | tf_op jit(solution)/shard_map/ppermute | solution.py:42
  44.3 2.8 %collective-permute-start.3 = (f32[22,8,128]{2,1,0:T(8,128)S(1)}, f32[22,8,128]{2,1,0:T(8,128)S(1)}, u32[]{:S(2)}, u32[]{:S(2)}) collective-permute-start(f32[22,8,128]{2,1,0:T(8,128)S(1)} %get-tuple-element.18), channel_id=1, source_target_pairs={{0,1},{1,0},{2,3},{3,2},{4,8},{5,9},{6,10},{7,11},{8,4},{9,5},{10,... | collective-permute-start | bytes 270344 | tf_op jit(solution)/shard_map/ppermute | solution.py:42
  47.1 0.2 pack_lanes.1
  47.2 0.1 collective-permute-start.4
  47.3 1.2 %collective-permute-start.5 = (f32[4,8,128]{2,1,0:T(8,128)S(1)}, f32[4,8,128]{2,1,0:T(8,128)S(1)}, u32[]{:S(2)}, u32[]{:S(2)}) collective-permute-start(f32[4,8,128]{2,1,0:T(8,128)S(1)} %get-tuple-element.22), channel_id=1, source_target_pairs={{0,1},{1,0},{2,3},{3,2},{4,8},{5,9},{6,10},{7,11},{8,4},{9,5},{10,... | collective-permute-start | bytes 49160 | tf_op jit(solution)/shard_map/ppermute | solution.py:42
  48.5 0.0 collective-permute-done.4.nc_ref
  48.5 4.2 %collective-permute-done.5.oc_ref = f32[4,8,128]{2,1,0:T(8,128)S(1)} collective-permute-done((f32[4,8,128]{2,1,0:T(8,128)S(1)}, f32[4,8,128]{2,1,0:T(8,128)S(1)}, u32[]{:S(2)}, u32[]{:S(2)}) %collective-permute-start.5) | collective-permute-done | bytes 16416 | tf_op jit(solution)/shard_map/ppermute | solution.py:42
  52.7 1.0 %collective-permute-start.6 = (f32[48,128]{1,0:T(8,128)S(1)}, f32[48,128]{1,0:T(8,128)S(1)}, u32[]{:S(2)}, u32[]{:S(2)}) collective-permute-start(f32[48,128]{1,0:T(8,128)S(1)} %get-tuple-element.23), channel_id=1, source_target_pairs={{0,1},{1,0},{2,3},{3,2},{4,5},{5,4},{6,7},{7,6},{8,9},{9,8},{10,11... | collective-permute-start | bytes 73736 | tf_op jit(solution)/shard_map/ppermute | solution.py:42
  53.8 0.0 collective-permute-start.7
  53.8 1.7 %collective-permute-done.6.nz_ref = f32[48,128]{1,0:T(8,128)S(1)} collective-permute-done((f32[48,128]{1,0:T(8,128)S(1)}, f32[48,128]{1,0:T(8,128)S(1)}, u32[]{:S(2)}, u32[]{:S(2)}) %collective-permute-start.6) | collective-permute-done | bytes 24608 | tf_op jit(solution)/shard_map/ppermute | solution.py:42
  55.5 1.4 %collective-permute-done.7.oz_ref = f32[48,128]{1,0:T(8,128)S(1)} collective-permute-done((f32[48,128]{1,0:T(8,128)S(1)}, f32[48,128]{1,0:T(8,128)S(1)}, u32[]{:S(2)}, u32[]{:S(2)}) %collective-permute-start.7) | collective-permute-done | bytes 24608 | tf_op jit(solution)/shard_map/ppermute | solution.py:42
  56.9 0.0 collective-permute-done.2.ny_ref
  56.9 0.0 collective-permute-done.3.oy_ref
  56.9 0.0 all-to-all-done.1.sq_ref
  56.9 3.6 %proximal.1 = (f32[16,16,128]{2,1,0:T(8,128)}, f32[16,16,128]{2,1,0:T(8,128)}) custom-call(s32[1]{0:T(128)} %bitcast.dev_ref, f32[16,16,128]{2,1,0:T(8,128)S(1)} %get-tuple-element.14.g_ref, f32[16,16,128]{2,1,0:T(8,128)S(1)} %copy-done, f32[6,16,128]{2,1,0:T(8,128)S(1)} %collective-permute-done.nx_ref, f32[6,16,128]{2,1,0:T(8,128)S(1)} %collective-permute-done.1.ox_ref, ...), custom_call_target="tpu_custom_call" | custom-call | tf_op jit(solution)/shard_map/proximal/pallas_call | solution.py:403
  (3 shorter events, 0.1 us)
Async XLA Ops:
  0.6 21.0 %copy-start = (f32[16,16,128]{2,1,0:T(8,128)S(1)}, f32[16,16,128]{2,1,0:T(8,128)}, u32[]{:S(2)}) copy-start(f32[16,16,128]{2,1,0:T(8,128)} %v_ref.7) | copy-start | bytes 393220
  22.4 34.4 %all-to-all-start.1 = ((f32[256,1,128]{2,1,0:T(1,128)}), f32[256,1,128]{2,1,0:T(1,128)S(1)}, u32[]{:S(2)}, u32[]{:S(2)}) async-start(f32[256,1,128]{2,1,0:T(1,128)} %broadcast_in_dim.9), calls=%async_computation.1 | async-start | bytes 262144 | tf_op jit(solution)/shard_map/all_to_all | solution.py:425
  36.8 3.7 %collective-permute-start = (f32[6,16,128]{2,1,0:T(8,128)S(1)}, f32[6,16,128]{2,1,0:T(8,128)S(1)}, u32[]{:S(2)}, u32[]{:S(2)}) collective-permute-start(f32[6,16,128]{2,1,0:T(8,128)S(1)} %get-tuple-element.15), channel_id=1, source_target_pairs={{0,32},{32,0},{64,96},{96,64},{128,160},{160,128},{192,224},{224,1... | collective-permute-start | bytes 147464 | tf_op jit(solution)/shard_map/ppermute | solution.py:42
  38.4 4.6 %collective-permute-start.1 = (f32[6,16,128]{2,1,0:T(8,128)S(1)}, f32[6,16,128]{2,1,0:T(8,128)S(1)}, u32[]{:S(2)}, u32[]{:S(2)}) collective-permute-start(f32[6,16,128]{2,1,0:T(8,128)S(1)} %get-tuple-element.16), channel_id=1, source_target_pairs={{0,4},{4,0},{32,64},{36,68},{64,32},{68,36},{96,128},{100,132},{12... | collective-permute-start | bytes 147464 | tf_op jit(solution)/shard_map/ppermute | solution.py:42
  43.0 13.9 %collective-permute-start.2 = (f32[22,8,128]{2,1,0:T(8,128)S(1)}, f32[22,8,128]{2,1,0:T(8,128)S(1)}, u32[]{:S(2)}, u32[]{:S(2)}) collective-permute-start(f32[22,8,128]{2,1,0:T(8,128)S(1)} %get-tuple-element.17), channel_id=1, source_target_pairs={{0,4},{4,0},{8,12},{12,8},{16,20},{20,16},{24,28},{28,24},{1,5},{5... | collective-permute-start | bytes 270344 | tf_op jit(solution)/shard_map/ppermute | solution.py:42
  44.3 12.6 %collective-permute-start.3 = (f32[22,8,128]{2,1,0:T(8,128)S(1)}, f32[22,8,128]{2,1,0:T(8,128)S(1)}, u32[]{:S(2)}, u32[]{:S(2)}) collective-permute-start(f32[22,8,128]{2,1,0:T(8,128)S(1)} %get-tuple-element.18), channel_id=1, source_target_pairs={{0,1},{1,0},{2,3},{3,2},{4,8},{5,9},{6,10},{7,11},{8,4},{9,5},{10,... | collective-permute-start | bytes 270344 | tf_op jit(solution)/shard_map/ppermute | solution.py:42
  47.2 1.3 %collective-permute-start.4 = (f32[4,8,128]{2,1,0:T(8,128)S(1)}, f32[4,8,128]{2,1,0:T(8,128)S(1)}, u32[]{:S(2)}, u32[]{:S(2)}) collective-permute-start(f32[4,8,128]{2,1,0:T(8,128)S(1)} %get-tuple-element.21), channel_id=1, source_target_pairs={{0,4},{4,0},{8,12},{12,8},{16,20},{20,16},{24,28},{28,24},{1,5},{5... | collective-permute-start | bytes 49160 | tf_op jit(solution)/shard_map/ppermute | solution.py:42
  47.3 5.4 %collective-permute-start.5 = (f32[4,8,128]{2,1,0:T(8,128)S(1)}, f32[4,8,128]{2,1,0:T(8,128)S(1)}, u32[]{:S(2)}, u32[]{:S(2)}) collective-permute-start(f32[4,8,128]{2,1,0:T(8,128)S(1)} %get-tuple-element.22), channel_id=1, source_target_pairs={{0,1},{1,0},{2,3},{3,2},{4,8},{5,9},{6,10},{7,11},{8,4},{9,5},{10,... | collective-permute-start | bytes 49160 | tf_op jit(solution)/shard_map/ppermute | solution.py:42
  52.7 2.8 %collective-permute-start.6 = (f32[48,128]{1,0:T(8,128)S(1)}, f32[48,128]{1,0:T(8,128)S(1)}, u32[]{:S(2)}, u32[]{:S(2)}) collective-permute-start(f32[48,128]{1,0:T(8,128)S(1)} %get-tuple-element.23), channel_id=1, source_target_pairs={{0,1},{1,0},{2,3},{3,2},{4,5},{5,4},{6,7},{7,6},{8,9},{9,8},{10,11... | collective-permute-start | bytes 73736 | tf_op jit(solution)/shard_map/ppermute | solution.py:42
  53.8 3.1 %collective-permute-start.7 = (f32[48,128]{1,0:T(8,128)S(1)}, f32[48,128]{1,0:T(8,128)S(1)}, u32[]{:S(2)}, u32[]{:S(2)}) collective-permute-start(f32[48,128]{1,0:T(8,128)S(1)} %get-tuple-element.24), channel_id=1, source_target_pairs={{0,4},{4,0},{1,2},{5,6},{2,1},{6,5},{3,7},{7,3},{8,12},{12,8},{9,1... | collective-permute-start | bytes 73736 | tf_op jit(solution)/shard_map/ppermute | solution.py:42
